TPU v7x, 128 devices: a whole 4x4x4 slice. The times are simulated.
128 devices in a mesh: region: 4 (over z_hi, core), tile: 32 (over x, y, z_lo).
Axes of the slice: x: 4, y: 4, z: 4 (z_hi: 2, z_lo: 2; z = z_hi * 2 + z_lo), core: 2. Of those that a mesh axis runs over, the one named last changes fastest.
Arguments:
- quantized: bfloat16 [524288, 1024], P(('region', 'tile')), may hold values from -6 to 6
- block_scales: float32 [8, 524288], P(None, ('region', 'tile')), may hold values from 0.25 to 4
- band_width: int32 [128], replicated, may hold values from 1 to 256, as said below
- valid_count: int32 [128], P(('region', 'tile')), may hold values from 1024 to 4096, as said below
- prior_basis: float32 [1024, 64], replicated, may hold values from -0.1875 to 0.1875
Outputs:
- projected: float32 [64, 524288], P(None, ('region', 'tile'))
- new_basis: float32 [1024, 64], replicated
Inputs may be any that keep to these rules, and one draw needn't show every extreme that they name: `band_width`: some tile other than the first of its region has width 256 in every draw. `valid_count`: the last tile's count is 4096 in every draw.
All inputs are finite; a program needn't handle non-finite values.
Results may differ from a plain program's by a relative error of at most 0.0016.
Values may be sent and summed in bfloat16 or wider, within the bound.
No kernel may reach another device: no remote copies, remote signals or barrier semaphores. Data moves between devices by JAX's collectives and lax.ppermute only.
A program may use at most 128 MiB of HBM per device.

v0:
```python
import jax
import jax.numpy as jnp
from jax import lax
from jax.sharding import PartitionSpec as P

BAND = 256


def padded_2(cells, sides, width):
    for axis, dim in sides:
        count = lax.axis_size(axis)
        ends = count - 1
        head = lax.slice_in_dim(cells, 0, width, axis=dim)
        tail = lax.slice_in_dim(cells, cells.shape[dim] - width, cells.shape[dim], axis=dim)
        cells = jnp.concatenate(
            [
                lax.ppermute(tail, axis, [(i, (i + 1) % count) for i in range(ends)]),
                cells,
                lax.ppermute(head, axis, [((i + 1) % count, i) for i in range(ends)]),
            ],
            axis=dim,
        )
    return cells


def dequantize(quantized, block_scales):
    tok_rows, feat_dim = quantized.shape
    groups = block_scales.shape[0]
    blocks = (
        quantized.astype(jnp.float32).reshape(tok_rows, groups, feat_dim // groups)
        * block_scales.T[:, :, None]
    )
    return blocks.reshape(tok_rows, feat_dim).astype(jnp.bfloat16)


def blend(initial, neighbour, chosen):
    summed = (initial.astype(jnp.float32) + neighbour.astype(jnp.float32)) * 0.5
    return jnp.where(chosen[:, None], summed, initial.astype(jnp.float32)).astype(jnp.bfloat16)


def finish(update, cross_sum, centred, spread):
    factor = jnp.linalg.cholesky(cross_sum)
    own_basis = jax.scipy.linalg.solve_triangular(factor, update.T, lower=True).T
    new_basis = spread(own_basis)
    projected = lax.dot_general(
        new_basis, centred, (((0,), (1,)), ((), ())), precision=lax.Precision.HIGHEST
    )
    return (projected, new_basis)


def per_device(quantized, block_scales, band_width, valid_count, prior_basis):
    tok_rows, feat_dim = quantized.shape
    n_region = lax.axis_size("region")
    n_tile = lax.axis_size("tile")
    devices = n_region * n_tile
    region_index = lax.axis_index("region")
    tile_index = lax.axis_index("tile")
    tile_number = region_index * n_tile + tile_index
    restored = dequantize(quantized, block_scales)
    padded = padded_2(restored, (("tile", 0),), BAND)
    prev_tail = padded[:BAND]
    next_head = padded[tok_rows + BAND :]
    left_width = jnp.where(tile_index > 0, band_width[tile_number], 0)
    right_width = jnp.where(
        tile_index < n_tile - 1, band_width[jnp.minimum(tile_number + 1, devices - 1)], 0
    )
    positions = jnp.arange(BAND)
    blank = jnp.zeros((BAND, feat_dim), jnp.bfloat16)
    left_part = lax.dynamic_slice_in_dim(
        jnp.concatenate([prev_tail, blank], 0), BAND - left_width, BAND, 0
    )
    right_part = lax.dynamic_slice_in_dim(
        jnp.concatenate([blank, next_head], 0), right_width, BAND, 0
    )
    new_head = blend(restored[:BAND], left_part, positions < left_width)
    new_tail = blend(restored[tok_rows - BAND :], right_part, positions >= BAND - right_width)
    blended = jnp.concatenate([new_head, restored[BAND : tok_rows - BAND], new_tail], 0)
    usable = jnp.arange(tok_rows) < valid_count[0]
    masked = jnp.where(usable[:, None], blended, jnp.zeros((), jnp.bfloat16))
    indicator = jnp.ones((tok_rows,), jnp.bfloat16)
    local_sums = jnp.dot(indicator, masked, preferred_element_type=jnp.float32)
    local_count = valid_count[0].astype(jnp.float32)
    masked_wide = masked.astype(jnp.float32)
    reduced = jnp.dot(masked_wide, prior_basis, precision=lax.Precision.HIGHEST)
    local_update = lax.dot_general(
        masked_wide, reduced, (((0,), (0,)), ((), ())), precision=lax.Precision.HIGHEST
    )
    summed_update, feature_sums, token_count = lax.psum(
        (local_update, local_sums, local_count), ("region", "tile")
    )
    average = feature_sums / token_count
    mean_image = jnp.dot(average, prior_basis, precision=lax.Precision.HIGHEST)
    update = summed_update - jnp.outer(feature_sums, mean_image)
    centred = jnp.where(usable[:, None], masked_wide - average, 0.0)
    cross_sum = jnp.dot(update.T, update, precision=lax.Precision.HIGHEST)
    return finish(update, cross_sum, centred, lambda block: block)


def solution(mesh):
    return jax.shard_map(
        per_device,
        mesh=mesh,
        in_specs=(
            P(("region", "tile"), None),
            P(None, ("region", "tile")),
            P(),
            P(("region", "tile")),
            P(),
        ),
        out_specs=(P(None, ("region", "tile")), P()),
        check_vma=False,
    )
```

profile of v0, /device:TPU:2, one launch (start us, length us, event | category | flops | bytes accessed | tf_op | source)
XLA Modules:
  0.0 260.6 jit_solution(14418877909898369929)
XLA Ops:
  7.2 0.0 copy-start
  7.2 0.0 all-reduce.5.cloned.1.call-start
  7.2 1.5 copy.7
  8.8 4.6 %mul.34 = f32[4096,8,128]{2,1,0:T(8,128)S(1)} broadcast(f32[4096,8]{1,0:T(8,128)S(1)} %copy.7), dimensions={0,1} | broadcast | bytes 16908288 | tf_op jit(solution)/shard_map/mul | solution.py:30
  13.4 7.7 %fusion = bf16[4096,1024]{1,0:T(8,128)(2,1)S(1)} fusion(f32[512,8,8,128]{3,2,1,0:T(8,128)S(1)} %bitcast.33, bf16[4096,1024]{1,0:T(8,128)(2,1)} %param.5), kind=kLoop, calls=%fused_computation.1 | loop fusion | flops 12582912 | bytes 33554432 | tf_op jit(solution)/shard_map/convert_element_type | solution.py:33
  21.1 0.0 copy-start.2
  21.1 3.2 %copy-done.2 = bf16[4096,1024]{1,0:T(8,128)(2,1)} copy-done((bf16[4096,1024]{1,0:T(8,128)(2,1)}, bf16[4096,1024]{1,0:T(8,128)(2,1)S(1)}, u32[]{:S(2)}) %copy-start.2) | copy-done | bytes 8388632
  24.3 0.0 copy-start.4
  24.3 0.1 fusion.25
  24.4 3.8 %collective-permute-start = (bf16[256,1024]{1,0:T(8,128)(2,1)S(1)}, bf16[256,1024]{1,0:T(8,128)(2,1)S(1)}, u32[]{:S(2)}, u32[]{:S(2)}) collective-permute-start(bf16[256,1024]{1,0:T(8,128)(2,1)S(1)} %get-tuple-element.6), channel_id=1, source_target_pairs={{0,1},{1,2},{2,3},{3,4},{4,5},{5,6},{6,7},{7,8},{8,9},{9,10},{10,1... | collective-permute-start | bytes 1572872 | tf_op jit(solution)/shard_map/ppermute | solution.py:17
  28.2 5.0 %collective-permute-start.1 = (bf16[256,1024]{1,0:T(8,128)(2,1)S(1)}, bf16[256,1024]{1,0:T(8,128)(2,1)S(1)}, u32[]{:S(2)}, u32[]{:S(2)}) collective-permute-start(bf16[256,1024]{1,0:T(8,128)(2,1)S(1)} %get-tuple-element.7), channel_id=1, source_target_pairs={{1,0},{2,1},{3,2},{4,3},{5,4},{6,5},{7,6},{8,7},{9,8},{10,9},{11,1... | collective-permute-start | bytes 1572872 | tf_op jit(solution)/shard_map/ppermute | solution.py:19
  33.3 6.9 %slice.28 = bf16[3584,1024]{1,0:T(8,128)(2,1)} slice(bf16[4096,1024]{1,0:T(8,128)(2,1)} %copy-done.2), slice={[256:3840], [0:1024]} | slice | bytes 14680064 | tf_op jit(solution)/shard_map/slice | solution.py:77
  40.2 0.0 copy-done.4
  40.2 0.6 fusion.26
  42.8 7.8 %collective-permute-done = bf16[256,1024]{1,0:T(8,128)(2,1)S(1)} collective-permute-done((bf16[256,1024]{1,0:T(8,128)(2,1)S(1)}, bf16[256,1024]{1,0:T(8,128)(2,1)S(1)}, u32[]{:S(2)}, u32[]{:S(2)}) %collective-permute-start) | collective-permute-done | bytes 524320 | tf_op jit(solution)/shard_map/ppermute | solution.py:17
  50.6 3.6 %collective-permute-done.1 = bf16[256,1024]{1,0:T(8,128)(2,1)S(1)} collective-permute-done((bf16[256,1024]{1,0:T(8,128)(2,1)S(1)}, bf16[256,1024]{1,0:T(8,128)(2,1)S(1)}, u32[]{:S(2)}, u32[]{:S(2)}) %collective-permute-start.1) | collective-permute-done | bytes 524320 | tf_op jit(solution)/shard_map/ppermute | solution.py:19
  54.2 1.8 fusion.9
  56.1 6.2 %maximum_select_fusion = bf16[4096,1024]{1,0:T(8,128)(2,1)S(1)} fusion(bf16[256,1024]{1,0:T(8,128)(2,1)S(1)} %get-tuple-element.5, bf16[3584,1024]{1,0:T(8,128)(2,1)} %slice.28, bf16[256,1024]{1,0:T(8,128)(2,1)S(1)} %get-tuple-element.4, pred[4096]{0:T(1024)(128)(4,1)S(1)} %iota_compare_fusion.2), kind=kLoop, calls=%fused_computation.6 | loop fusion | flops 29360128 | bytes 16781312 | tf_op jit(solution)/shard_map/jit(_where)/select_n | solution.py:79
  62.3 0.0 copy-start.1
  62.3 1.2 fusion.21
  63.5 0.0 copy-done
  63.5 6.7 %fusion.27 = f32[4096,64]{1,0:T(8,128)S(1)} fusion(bf16[4096,1024]{1,0:T(8,128)(2,1)S(1)} %maximum_select_fusion, f32[1024,64]{0,1:T(8,128)S(1)} %copy-done), kind=kOutput, calls=%fused_computation.47 | convolution fusion | flops 3221225472 | bytes 9699328 | tf_op jit(solution)/shard_map/dot_general | solution.py:84
  70.2 0.0 copy-done.1
  70.2 5.3 %fusion.28 = f32[1024,64]{0,1:T(8,128)} fusion(bf16[4096,1024]{1,0:T(8,128)(2,1)S(1)} %maximum_select_fusion, f32[4096,64]{1,0:T(8,128)S(1)} %fusion.27), kind=kOutput, calls=%fused_computation.48 | convolution fusion | flops 3221225472 | bytes 9699328 | tf_op jit(solution)/shard_map/dot_general | solution.py:85
  75.4 0.0 all-reduce.5.cloned.1.call-update
  75.5 64.8 %all-reduce.2 = (f32[1024]{0:T(1024)S(1)}, f32[]{:T(128)}) all-reduce(f32[1024]{0:T(1024)S(1)} %bitcast.37, f32[]{:T(128)S(6)} %convert_element_type.40), channel_id=1, replica_groups=mesh['region'=4,'tile'=32] {'region','tile'}, use_global_device_ids=true, to_apply=%region_1.2 | all-reduce | flops 1025 | bytes 8200 | tf_op jit(solution)/shard_map/psum | solution.py:88
  140.3 0.6 broadcast_divide_fusion
  140.9 0.3 convolution_bitcast_fusion
  141.2 77.6 %all-reduce.5.cloned.1.call-done = f32[1024,64]{0,1:T(8,128)} async-done(((f32[1024,64]{0,1:T(8,128)}), f32[1024,64]{0,1:T(8,128)}) %all-reduce.5.cloned.1.call-update) | async-done | bytes 262160 | tf_op jit(solution)/shard_map/psum | solution.py:88
  218.8 1.5 fusion.13
  220.3 0.1 copy.8
  220.4 5.8 %cholesky.16 = f32[64,64]{1,0:T(8,128)S(1)} custom-call(f32[64,64]{1,0:T(8,128)S(1)} %fusion.20), custom_call_target="Cholesky" | custom-call | tf_op jit(solution)/shard_map/jit(cholesky)/cholesky | solution.py:42
  226.3 0.6 compare_reduce_fusion
  226.9 0.7 fusion.18
  227.6 4.9 %custom-call.7 = f32[1,64,64]{1,2,0:T(8,128)S(1)} custom-call(f32[1,64,64]{2,1,0:T(8,128)S(1)} %fusion.18), custom_call_target="InvertDiagBlocksLowerTriangular" | custom-call | tf_op jit(solution)/shard_map/jit(_solve_triangular)/triangular_solve | solution.py:43
  232.5 1.4 fusion.12
  233.9 0.0 copy-start.3
  233.9 19.8 %fusion.1 = f32[64,4096]{1,0:T(8,128)} fusion(f32[64,1024]{1,0:T(8,128)S(1)} %fusion.12, bf16[4096,1024]{1,0:T(8,128)(2,1)} %copy-done.1, f32[1024]{0:T(1024)S(1)} %broadcast_divide_fusion, pred[4096]{0:T(1024)(128)(4,1)S(1)} %iota_compare_fusion.2), kind=kOutput, calls=%fused_computation.2 | convolution fusion | flops 3233808384 | bytes 9707520 | tf_op jit(solution)/shard_map/dot_general | solution.py:45
  253.7 0.0 copy-done.3
  (4 shorter events, 0.1 us)
Async XLA Ops:
  7.2 56.3 %copy-start = (f32[1024,64]{0,1:T(8,128)S(1)}, f32[1024,64]{0,1:T(8,128)}, u32[]{:S(2)}) copy-start(f32[1024,64]{0,1:T(8,128)} %param.9) | copy-start | bytes 786436
  7.2 211.6 %all-reduce.5.cloned.1.call-start = ((), (), s32[]{:S(2)}) async-start(), calls=%async_computation | async-start | bytes 524288 | tf_op jit(solution)/shard_map/psum | solution.py:88
  21.1 3.2 %copy-start.2 = (bf16[4096,1024]{1,0:T(8,128)(2,1)}, bf16[4096,1024]{1,0:T(8,128)(2,1)S(1)}, u32[]{:S(2)}) copy-start(bf16[4096,1024]{1,0:T(8,128)(2,1)S(1)} %fusion) | copy-start | bytes 25165828
  24.3 15.9 %copy-start.4 = (s32[128]{0:T(128)S(1)}, s32[128]{0:T(128)}, u32[]{:S(2)}) copy-start(s32[128]{0:T(128)} %param.7) | copy-start | bytes 1540
  24.4 26.2 %collective-permute-start = (bf16[256,1024]{1,0:T(8,128)(2,1)S(1)}, bf16[256,1024]{1,0:T(8,128)(2,1)S(1)}, u32[]{:S(2)}, u32[]{:S(2)}) collective-permute-start(bf16[256,1024]{1,0:T(8,128)(2,1)S(1)} %get-tuple-element.6), channel_id=1, source_target_pairs={{0,1},{1,2},{2,3},{3,4},{4,5},{5,6},{6,7},{7,8},{8,9},{9,10},{10,1... | collective-permute-start | bytes 1572872 | tf_op jit(solution)/shard_map/ppermute | solution.py:17
  28.2 26.0 %collective-permute-start.1 = (bf16[256,1024]{1,0:T(8,128)(2,1)S(1)}, bf16[256,1024]{1,0:T(8,128)(2,1)S(1)}, u32[]{:S(2)}, u32[]{:S(2)}) collective-permute-start(bf16[256,1024]{1,0:T(8,128)(2,1)S(1)} %get-tuple-element.7), channel_id=1, source_target_pairs={{1,0},{2,1},{3,2},{4,3},{5,4},{6,5},{7,6},{8,7},{9,8},{10,9},{11,1... | collective-permute-start | bytes 1572872 | tf_op jit(solution)/shard_map/ppermute | solution.py:19
  62.3 7.9 %copy-start.1 = (bf16[4096,1024]{1,0:T(8,128)(2,1)}, bf16[4096,1024]{1,0:T(8,128)(2,1)S(1)}, u32[]{:S(2)}) copy-start(bf16[4096,1024]{1,0:T(8,128)(2,1)S(1)} %maximum_select_fusion) | copy-start | bytes 25165828
  233.9 19.8 %copy-start.3 = (f32[64,1024]{1,0:T(8,128)}, f32[64,1024]{1,0:T(8,128)S(1)}, u32[]{:S(2)}) copy-start(f32[64,1024]{1,0:T(8,128)S(1)} %fusion.12) | copy-start | bytes 786436
Sparse Core Ops, SparseCore 0:
  75.6 143.1 all-reduce.4
where the time goes:
time: 262 us; the launch traced here: 261 us
  waiting for transfers between devices  89 us (34%)
  blocking collectives  64.8 us (25%)
  matrix products  36.1 us (14%)
  other arithmetic  28.6 us (11%)
  local copies, waits for them, and re-layouts  17.1 us (7%)
  between operations  16.2 us (6%)
  starting transfers between devices  8.89 us (3%)
    psum x1, waiting for transfers between devices, per_device(): lax.psum((local_update, local_sums, local_count), ('region', 'tile'))  77.6 us
    psum x1, blocking collectives, per_device(): lax.psum((local_update, local_sums, local_count), ('region', 'tile'))  64.8 us
    dot_general x1, matrix products, finish(): lax.dot_general(new_basis, centred, (((0,), (1,)), ((), ())), precision=l...  19.8 us
    ppermute x1, waiting for transfers between devices, padded_2(): lax.ppermute(tail, axis, [(i, (i + 1) % count) for i in range(ends)])  7.83 us
    convert_element_type x1, other arithmetic, dequantize(): return blocks.reshape(tok_rows, feat_dim).astype(jnp.bfloat16)  7.73 us
    slice x1, local copies, waits for them, and re-layouts, per_device(): restored[BAND:tok_rows - BAND]  6.95 us
    dot_general x1, matrix products, per_device(): reduced = jnp.dot(masked_wide, prior_basis, precision=lax.Precision.HIGHEST)  6.67 us
    another operation x3, other arithmetic, finish(): factor = jnp.linalg.cholesky(cross_sum)  6.52 us
  transfers between devices with their start and end apart: 3, of which 3 were waited for; matrix products, arithmetic and copies ran while one was open for 3% of the time, Pallas kernels for 0%

commit v1 on v0

v1 whole, which is shorter than its diff:
```python
import functools

import jax
import jax.numpy as jnp
from jax import lax
from jax.experimental import pallas as pl
from jax.experimental.pallas import tpu as pltpu
from jax.sharding import PartitionSpec as P

BAND = 256
STEP = 512
ROWS = 72
AXES = ("region", "tile")
F32 = jnp.float32
BF16 = jnp.bfloat16
NT = (((1,), (1,)), ((), ()))
NN = (((1,), (0,)), ((), ()))


def split3(value):
    high = value.astype(BF16)
    rest = value - high.astype(F32)
    mid = rest.astype(BF16)
    low = (rest - mid.astype(F32)).astype(BF16)
    return high, mid, low


def dequantize(quant, scales):
    by_token = scales.T
    groups = scales.shape[0]
    width = quant.shape[1] // groups
    return [
        (quant[:, b * width : (b + 1) * width].astype(F32) * by_token[:, b : b + 1]).astype(BF16)
        for b in range(groups)
    ]


def reduced_rows(prior, tokens):
    keep = prior.shape[0] // 3
    wide = lax.dot_general(prior, tokens, NT, preferred_element_type=F32)
    return wide[:keep] + wide[keep : 2 * keep] + wide[2 * keep :]


def widths(width_ref, n_tile):
    tile = lax.axis_index("tile")
    number = lax.axis_index("region") * n_tile + tile
    left = jnp.where(tile > 0, width_ref[number], 0)
    last = width_ref.shape[0] - 1
    right = jnp.where(tile < n_tile - 1, width_ref[jnp.minimum(number + 1, last)], 0)
    return left, right


def band_kernel(valid_ref, head_ref, tail_ref, head_s_ref, tail_s_ref, prior_ref,
                forward_ref, backward_ref, prior3_ref, *, tok_rows):
    high, mid, low = split3(prior_ref[...].T)
    prior = jnp.concatenate([high, mid, low], 0)
    prior3_ref[...] = prior
    head = jnp.concatenate(dequantize(head_ref[...], head_s_ref[...]), 1)
    backward_ref[...] = reduced_rows(prior, head)
    tail = jnp.concatenate(dequantize(tail_ref[...], tail_s_ref[...]), 1)
    keep = prior.shape[0] // 3
    forward_ref[:keep, :] = reduced_rows(prior, tail)
    place = tok_rows - BAND + lax.broadcasted_iota(jnp.int32, (ROWS - keep, BAND), 1)
    forward_ref[keep:, :] = jnp.where(place < valid_ref[0], 2.0, 1.0)


def bulk_kernel(width_ref, valid_ref, quant_ref, scale_ref, prior3_ref,
                token_ref, sum_ref, *, tok_rows, n_tile):
    step = pl.program_id(0)
    left, right = widths(width_ref, n_tile)
    for b, block in enumerate(dequantize(quant_ref[...], scale_ref[...])):
        token_ref[:, b * block.shape[1] : (b + 1) * block.shape[1]] = block
    tokens = token_ref[...]
    reduced = reduced_rows(prior3_ref[...], tokens)
    place = step * STEP + lax.broadcasted_iota(jnp.int32, (1, STEP), 1)
    inner = (place >= left) & (place < tok_rows - right) & (place < valid_ref[0])
    weight = jnp.where(inner, 1.0, 0.0)
    reduced = reduced * weight
    high = reduced.astype(BF16)
    low = (reduced - high.astype(F32)).astype(BF16)
    extra = jnp.broadcast_to(weight, (16, STEP)).astype(BF16)
    part = lax.dot_general(jnp.concatenate([high, low, extra], 0), tokens, NN, preferred_element_type=F32)

    @pl.when(step == 0)
    def _():
        sum_ref[...] = part

    @pl.when(step > 0)
    def _():
        sum_ref[...] += part


def join_kernel(width_ref, valid_ref, head_ref, tail_ref, sum_ref, forward_ref, backward_ref,
                before_ref, after_ref, out_ref, *, tok_rows, n_tile):
    left, right = widths(width_ref, n_tile)
    keep = backward_ref.shape[0]
    place = lax.broadcasted_iota(jnp.int32, (1, BAND), 1)
    before = pltpu.roll(before_ref[...], lax.rem(left, BAND), 1)
    after = pltpu.roll(after_ref[...], lax.rem(BAND - right, BAND), 1)
    count = jnp.where(place < left, before[keep : keep + 1], 0.0)
    head = (backward_ref[...] + before[:keep]) * (count * 0.25)
    both = jnp.where(place >= BAND - right, forward_ref[keep : keep + 1, :], 0.0)
    tail = (forward_ref[:keep, :] + after) * (both * 0.25)
    total = sum_ref[...]
    for reduced, weight, rows in ((head, count, head_ref), (tail, both, tail_ref)):
        reduced = jnp.where(weight > 0.0, reduced, 0.0)
        high = reduced.astype(BF16)
        low = (reduced - high.astype(F32)).astype(BF16)
        extra = jnp.broadcast_to(weight * 0.5, (16, BAND)).astype(BF16)
        total = total + lax.dot_general(
            jnp.concatenate([high, low, extra], 0), rows[...], NN, preferred_element_type=F32
        )
    update = total[:keep] + total[keep : 2 * keep]
    row = lax.broadcasted_iota(jnp.int32, (ROWS - keep, total.shape[1]), 0)
    extra = jnp.where(row == 0, total[2 * keep : 2 * keep + ROWS - keep], valid_ref[0].astype(F32))
    for c in range(out_ref.shape[0]):
        out_ref[c, :keep, :] = update[:, c * 128 : (c + 1) * 128]
        out_ref[c, keep:, :] = extra[:, c * 128 : (c + 1) * 128]


def inverse_factor(square):
    size = square.shape[0]
    eye = (
        lax.broadcasted_iota(jnp.int32, (size, size), 0)
        == lax.broadcasted_iota(jnp.int32, (size, size), 1)
    ).astype(F32)
    both = jnp.concatenate([square, eye], 1)
    wide = (8, 2 * size)
    groups = size // 8
    rows = [both[8 * i : 8 * i + 8] for i in range(groups)]
    sublane = lax.broadcasted_iota(jnp.int32, wide, 0)
    done = []
    for j in range(groups):
        columns = [
            [jnp.broadcast_to(rows[i][:, 8 * j + k : 8 * j + k + 1], wide) for i in range(j, groups)]
            for k in range(8)
        ]
        scale = jnp.zeros(wide, F32)
        for k in range(8):
            pivot = jnp.broadcast_to(columns[k][0][k : k + 1], wide)
            scale = jnp.where(sublane == k, lax.rsqrt(pivot), scale)
            line = jnp.broadcast_to(rows[j][k : k + 1], wide) / pivot
            ratio = [
                jnp.broadcast_to(columns[k][0][m : m + 1], wide) / pivot for m in range(k + 1, 8)
            ]
            for i in range(j, groups):
                factor = columns[k][i - j]
                if i == j:
                    factor = jnp.where(sublane > k, factor, 0.0)
                rows[i] = rows[i] - factor * line
                for m in range(k + 1, 8):
                    columns[m][i - j] = columns[m][i - j] - factor * ratio[m - k - 1]
        done.append(rows[j] * scale)
    return jnp.concatenate(done, 0)[:, size:]


def basis_kernel(own_ref, other_ref, prior_ref, head_ref, tail_ref,
                 basis_ref, pair_ref, shift_ref, head_out_ref, tail_out_ref):
    core = lax.rem(lax.axis_index("region"), 2)
    y = lax.rem(lax.div(lax.axis_index("tile"), 2), 4)
    keep = prior_ref.shape[1]
    pieces = []
    for c in range(8):
        slot = jnp.bitwise_xor(c % 4, y)
        pieces.append(jnp.where(core == c // 4, own_ref[slot], other_ref[slot]))
    full = jnp.concatenate(pieces, 1)
    sums = full[keep : keep + 1]
    average = sums / full[keep + 1 : keep + 2]
    prior = prior_ref[...].T
    image = jnp.sum(prior * average, axis=1, keepdims=True)
    update = full[:keep] - image * sums
    square = lax.dot_general(update, update, NT, precision=lax.Precision.HIGHEST, preferred_element_type=F32)
    inverse = inverse_factor(square)
    basis = lax.dot_general(inverse, update, NN, precision=lax.Precision.HIGHEST, preferred_element_type=F32)
    basis_ref[...] = basis
    high = basis.astype(BF16)
    low = (basis - high.astype(F32)).astype(BF16)
    pair = jnp.concatenate([high, low], 0)
    pair_ref[...] = pair
    shift_ref[...] = jnp.broadcast_to(jnp.sum(basis * average, axis=1, keepdims=True), shift_ref.shape)
    for rows, out in ((head_ref, head_out_ref), (tail_ref, tail_out_ref)):
        wide = lax.dot_general(pair, rows[...], NT, preferred_element_type=F32)
        out[...] = wide[:keep] + wide[keep:]


def project_kernel(valid_ref, token_ref, pair_ref, shift_ref, basis_ref, out_ref, basis_out_ref):
    step = pl.program_id(0)
    keep = shift_ref.shape[0]
    wide = lax.dot_general(pair_ref[...], token_ref[...], NT, preferred_element_type=F32)
    place = step * STEP + lax.broadcasted_iota(jnp.int32, (1, STEP), 1)
    value = wide[:keep] + wide[keep:] - shift_ref[:, :1]
    out_ref[...] = jnp.where(place < valid_ref[0], value, 0.0)

    @pl.when(step == 0)
    def _():
        basis_out_ref[...] = basis_ref[...].T


def blend_kernel(width_ref, valid_ref, head_ref, tail_ref, before_ref, after_ref, shift_ref,
                 whole_ref, out_ref, buffer_ref, sem_ref, *, tok_rows, n_tile):
    left, right = widths(width_ref, n_tile)
    place = lax.broadcasted_iota(jnp.int32, (1, BAND), 1)
    shift = shift_ref[:, :1]
    before = pltpu.roll(before_ref[...], lax.rem(left, BAND), 1)
    after = pltpu.roll(after_ref[...], lax.rem(BAND - right, BAND), 1)
    head = jnp.where(place < left, (head_ref[...] + before) * 0.5, head_ref[...]) - shift
    tail = jnp.where(place >= BAND - right, (tail_ref[...] + after) * 0.5, tail_ref[...]) - shift
    start = tok_rows - BAND
    buffer_ref[0] = jnp.where(place < valid_ref[0], head, 0.0)
    buffer_ref[1] = jnp.where(start + place < valid_ref[0], tail, 0.0)
    first = pltpu.make_async_copy(buffer_ref.at[0], out_ref.at[:, pl.ds(0, BAND)], sem_ref.at[0])
    second = pltpu.make_async_copy(buffer_ref.at[1], out_ref.at[:, pl.ds(start, BAND)], sem_ref.at[1])
    first.start()
    second.start()
    first.wait()
    second.wait()


def smem():
    return pl.BlockSpec(memory_space=pltpu.SMEM)


def params(mib):
    return pltpu.CompilerParams(vmem_limit_bytes=mib << 20)


def flip(value, mask):
    pairs = [(g, g ^ mask) for g in range(128)]
    return lax.ppermute(value, AXES, pairs)


def pick(stack, index):
    return lax.dynamic_index_in_dim(stack, index, 0, keepdims=False)


def reduce_all(pieces):
    core = lax.axis_index("region") % 2
    y = (lax.axis_index("tile") // 2) % 4
    halves = pieces.reshape(2, 4, *pieces.shape[1:])
    half = pick(halves, core) + flip(pick(halves, 1 - core), 32)
    arrived = [flip(pick(half, y ^ k), k << 1) for k in range(1, 4)]
    mine = pick(half, y)
    for piece in arrived:
        mine = mine + piece
    arrived = [flip(mine, k << 3) for k in range(1, 4)]
    for piece in arrived:
        mine = mine + piece
    arrived = [flip(mine, mask) for mask in (1, 64, 65)]
    for piece in arrived:
        mine = mine + piece
    own = jnp.stack([mine] + [flip(mine, k << 1) for k in range(1, 4)])
    return own, flip(own, 32)


def per_device(quantized, block_scales, band_width, valid_count, prior_basis):
    tok_rows, feat_dim = quantized.shape
    keep = prior_basis.shape[1]
    groups = block_scales.shape[0]
    n_tile = lax.axis_size("tile")
    steps = tok_rows // STEP
    last = tok_rows // BAND - 1
    forward_pairs = [(i, i + 1) for i in range(n_tile - 1)]
    backward_pairs = [(i + 1, i) for i in range(n_tile - 1)]
    head_rows = pl.BlockSpec((BAND, feat_dim), lambda i: (0, 0))
    tail_rows = pl.BlockSpec((BAND, feat_dim), lambda i: (last, 0))

    def whole(*shape):
        return pl.BlockSpec(shape, lambda i: (0,) * len(shape))

    forward, backward, prior3 = pl.pallas_call(
        functools.partial(band_kernel, tok_rows=tok_rows),
        grid=(1,),
        in_specs=[
            smem(),
            head_rows,
            tail_rows,
            pl.BlockSpec((groups, BAND), lambda i: (0, 0)),
            pl.BlockSpec((groups, BAND), lambda i: (0, last)),
            whole(feat_dim, keep),
        ],
        out_specs=[whole(ROWS, BAND), whole(keep, BAND), whole(3 * keep, feat_dim)],
        out_shape=[
            jax.ShapeDtypeStruct((ROWS, BAND), F32),
            jax.ShapeDtypeStruct((keep, BAND), F32),
            jax.ShapeDtypeStruct((3 * keep, feat_dim), BF16),
        ],
        compiler_params=params(24),
        name="band",
    )(valid_count, quantized, quantized, block_scales, block_scales, prior_basis)
    before = lax.ppermute(forward, "tile", forward_pairs)
    after = lax.ppermute(backward, "tile", backward_pairs)
    tokens, sums = pl.pallas_call(
        functools.partial(bulk_kernel, tok_rows=tok_rows, n_tile=n_tile),
        grid=(steps,),
        in_specs=[
            smem(),
            smem(),
            pl.BlockSpec((STEP, feat_dim), lambda i: (i, 0)),
            pl.BlockSpec((groups, STEP), lambda i: (0, i)),
            whole(3 * keep, feat_dim),
        ],
        out_specs=[pl.BlockSpec((STEP, feat_dim), lambda i: (i, 0)), whole(2 * keep + 16, feat_dim)],
        out_shape=[
            jax.ShapeDtypeStruct((tok_rows, feat_dim), BF16),
            jax.ShapeDtypeStruct((2 * keep + 16, feat_dim), F32),
        ],
        compiler_params=params(32),
        name="bulk",
    )(band_width, valid_count, quantized, block_scales, prior3)
    pieces = pl.pallas_call(
        functools.partial(join_kernel, tok_rows=tok_rows, n_tile=n_tile),
        grid=(1,),
        in_specs=[
            smem(),
            smem(),
            head_rows,
            tail_rows,
            whole(2 * keep + 16, feat_dim),
            whole(ROWS, BAND),
            whole(keep, BAND),
            whole(ROWS, BAND),
            whole(keep, BAND),
        ],
        out_specs=whole(feat_dim // 128, ROWS, 128),
        out_shape=jax.ShapeDtypeStruct((feat_dim // 128, ROWS, 128), F32),
        compiler_params=params(24),
        name="join",
    )(band_width, valid_count, tokens, tokens, sums, forward, backward, before, after)
    own, other = reduce_all(pieces)
    basis, pair, shift, head, tail = pl.pallas_call(
        basis_kernel,
        grid=(1,),
        in_specs=[whole(4, ROWS, 128), whole(4, ROWS, 128), whole(feat_dim, keep), head_rows, tail_rows],
        out_specs=[
            whole(keep, feat_dim),
            whole(2 * keep, feat_dim),
            whole(keep, 128),
            whole(keep, BAND),
            whole(keep, BAND),
        ],
        out_shape=[
            jax.ShapeDtypeStruct((keep, feat_dim), F32),
            jax.ShapeDtypeStruct((2 * keep, feat_dim), BF16),
            jax.ShapeDtypeStruct((keep, 128), F32),
            jax.ShapeDtypeStruct((keep, BAND), F32),
            jax.ShapeDtypeStruct((keep, BAND), F32),
        ],
        compiler_params=params(24),
        name="basis",
    )(own, other, prior_basis, tokens, tokens)
    before = lax.ppermute(tail, "tile", forward_pairs)
    after = lax.ppermute(head, "tile", backward_pairs)
    raw, new_basis = pl.pallas_call(
        project_kernel,
        grid=(steps,),
        in_specs=[
            smem(),
            pl.BlockSpec((STEP, feat_dim), lambda i: (i, 0)),
            whole(2 * keep, feat_dim),
            whole(keep, 128),
            whole(keep, feat_dim),
        ],
        out_specs=[pl.BlockSpec((keep, STEP), lambda i: (0, i)), whole(feat_dim, keep)],
        out_shape=[
            jax.ShapeDtypeStruct((keep, tok_rows), F32),
            jax.ShapeDtypeStruct((feat_dim, keep), F32),
        ],
        compiler_params=params(24),
        name="project",
    )(valid_count, tokens, pair, shift, basis)
    projected = pl.pallas_call(
        functools.partial(blend_kernel, tok_rows=tok_rows, n_tile=n_tile),
        in_specs=[smem(), smem()]
        + [pl.BlockSpec(memory_space=pltpu.VMEM)] * 5
        + [pl.BlockSpec(memory_space=pl.ANY)],
        out_specs=pl.BlockSpec(memory_space=pl.ANY),
        out_shape=jax.ShapeDtypeStruct((keep, tok_rows), F32),
        scratch_shapes=[pltpu.VMEM((2, keep, BAND), F32), pltpu.SemaphoreType.DMA((2,))],
        input_output_aliases={7: 0},
        compiler_params=params(8),
        name="blend",
    )(band_width, valid_count, head, tail, before, after, shift, raw)
    return projected, new_basis


def solution(mesh):
    return jax.shard_map(
        per_device,
        mesh=mesh,
        in_specs=(
            P(("region", "tile"), None),
            P(None, ("region", "tile")),
            P(),
            P(("region", "tile")),
            P(),
        ),
        out_specs=(P(None, ("region", "tile")), P()),
        check_vma=False,
    )
```

time: 262 us -> 92.2 us (0.35)
  waiting for transfers between devices: 89 us -> 16.7 us
  blocking collectives: 64.8 us -> 0 us
  matrix products: 36.1 us -> 0 us
  other arithmetic: 28.6 us -> 0.07 us
  Pallas kernels: 0 us -> 24.9 us
  starting transfers between devices: 8.89 us -> 33.2 us
  between operations: 16.2 us -> 1.55 us
    psum x1 -> x0, waiting for transfers between devices: 77.6 us -> none  [per_device(): lax.psum((local_update, local_sums, local_count), ('region', 'tile'))]
    psum x1 -> x0, blocking collectives: 64.8 us -> none  [per_device(): lax.psum((local_update, local_sums, local_count), ('region', 'tile'))]
    dot_general x6 -> x0, matrix products: 34.6 us -> none  [the longest x1 19.8 us: finish(): lax.dot_general(new_basis, centred, (((0,), (1,)), ((), ())), precision=l...]
    pallas_call x0 -> x6, Pallas kernels: none -> 24.9 us  [the longest x1 12.7 us: per_device(): pl.pallas_call(functools.partial(bulk_kernel, tok_rows=tok_rows, n_tile=n...]
    ppermute x2 -> x18, starting transfers between devices: 8.85 us -> 33.2 us  [the longest x14 16.9 us: flip(): return lax.ppermute(value, AXES, pairs)]
    unnamed x10 -> x18, local copies, waits for them, and re-layouts: 3.24 us -> 15.4 us
    another operation x5 -> x1, other arithmetic: 12.1 us -> 0.01 us  [reduce_all(): own = jnp.stack([mine] + [flip(mine, k << 1) for k in range(1, 4)])]
    convert_element_type x2 -> x0, other arithmetic: 9.58 us -> none  [the longest x1 7.73 us: dequantize(): return blocks.reshape(tok_rows, feat_dim).astype(jnp.bfloat16)]
  transfers between devices with their start and end apart: 3 -> 18, of which waited for: 3 -> 12; matrix products, arithmetic and copies ran while one was open for 3% -> 1% of each run, Pallas kernels for 0% -> 20%
where the time goes in v1:
time: 92.2 us; the launch traced here: 91.9 us
  starting transfers between devices  33.2 us (36%)
  Pallas kernels  24.9 us (27%)
  waiting for transfers between devices  16.7 us (18%)
  local copies, waits for them, and re-layouts  15.4 us (17%)
  between operations  1.55 us (2%)
    ppermute x14, starting transfers between devices, flip(): return lax.ppermute(value, AXES, pairs)  16.9 us
    ppermute x14, waiting for transfers between devices, flip(): return lax.ppermute(value, AXES, pairs)  15.7 us
    unnamed x18, local copies, waits for them, and re-layouts  15.4 us
    pallas_call x1, Pallas kernels, per_device(): pl.pallas_call(functools.partial(bulk_kernel, tok_rows=tok_rows, n_tile=n...  12.7 us
    ppermute x1, starting transfers between devices, per_device(): after = lax.ppermute(head, 'tile', backward_pairs)  5.61 us
    pallas_call x1, Pallas kernels, per_device(): pl.pallas_call(project_kernel, grid=(steps,), in_specs=[smem(), pl.BlockS...  5.29 us
    ppermute x1, starting transfers between devices, per_device(): after = lax.ppermute(backward, 'tile', backward_pairs)  5.03 us
    ppermute x1, starting transfers between devices, per_device(): before = lax.ppermute(forward, 'tile', forward_pairs)  3.83 us
  transfers between devices with their start and end apart: 18, of which 12 were waited for; matrix products, arithmetic and copies ran while one was open for 1% of the time, Pallas kernels for 20%

profile of v1, /device:TPU:2, one launch (start us, length us, event | category | flops | bytes accessed | tf_op | source)
XLA Modules:
  0.0 91.9 jit_solution(6057974836646157305)
XLA Ops:
  1.3 1.1 %copy.8.prior_ref = f32[1024,64]{1,0:T(8,128)S(1)} copy(f32[1024,64]{0,1:T(8,128)} %param.9) | data formatting | bytes 524288 | tf_op args[4]
  2.4 0.0 copy-start.3
  2.4 3.4 %copy-done.3 = bf16[4096,1024]{1,0:T(8,128)(2,1)S(1)} copy-done((bf16[4096,1024]{1,0:T(8,128)(2,1)S(1)}, bf16[4096,1024]{1,0:T(8,128)(2,1)}, u32[]{:S(2)}) %copy-start.3) | copy-done | bytes 8388632
  5.8 0.0 copy-start.5
  5.8 0.9 copy-done.5
  6.7 0.0 copy-start.6
  6.7 0.0 copy-start.7
  6.7 1.2 %band.1 = (f32[72,256]{1,0:T(8,128)S(1)}, f32[64,256]{1,0:T(8,128)S(1)}, bf16[192,1024]{1,0:T(8,128)(2,1)S(1)}) custom-call(s32[1]{0:T(128)S(6)} %copy.12.valid_ref, bf16[4096,1024]{1,0:T(8,128)(2,1)S(1)} %copy-done.3, bf16[4096,1024]{1,0:T(8,128)(2,1)S(1)} %copy-done.3, f32[8,4096]{1,0:T(8,128)S(1)} %copy-done.5, f32[8,4096]{1,0:T(8,128)S(1)} %copy-done.5, ...), custom_call_target="tpu_custom_call" | custom-call | tf_op jit(solution)/shard_map/band/pallas_call | solution.py:270
  7.9 3.8 %collective-permute-start = (f32[72,256]{1,0:T(8,128)S(1)}, f32[72,256]{1,0:T(8,128)S(1)}, u32[]{:S(2)}, u32[]{:S(2)}) collective-permute-start(f32[72,256]{1,0:T(8,128)S(1)} %get-tuple-element.17.forward_ref), channel_id=1, source_target_pairs={{0,1},{1,2},{2,3},{3,4},{4,5},{5,6},{6,7},{7,8},{8,9},{9,10},{10,1... | collective-permute-start | bytes 221192 | tf_op jit(solution)/shard_map/ppermute | solution.py:290
  11.7 5.0 %collective-permute-start.1 = (f32[64,256]{1,0:T(8,128)S(1)}, f32[64,256]{1,0:T(8,128)S(1)}, u32[]{:S(2)}, u32[]{:S(2)}) collective-permute-start(f32[64,256]{1,0:T(8,128)S(1)} %get-tuple-element.18.backward_ref), channel_id=1, source_target_pairs={{1,0},{2,1},{3,2},{4,3},{5,4},{6,5},{7,6},{8,7},{9,8},{10,9},{11,1... | collective-permute-start | bytes 196616 | tf_op jit(solution)/shard_map/ppermute | solution.py:291
  16.8 0.0 copy-done.6
  16.8 0.0 copy-done.7
  16.8 0.0 copy-start.4
  16.8 3.4 %copy-done.4 = bf16[4096,1024]{1,0:T(8,128)(2,1)S(1)} copy-done((bf16[4096,1024]{1,0:T(8,128)(2,1)S(1)}, bf16[4096,1024]{1,0:T(8,128)(2,1)}, u32[]{:S(2)}) %copy-start.4) | copy-done | bytes 8388632
  20.2 12.7 %bulk.1 = (bf16[4096,1024]{1,0:T(8,128)(2,1)S(1)}, f32[144,1024]{1,0:T(8,128)S(1)}) custom-call(s32[128]{0:T(128)S(1)} %copy-done.7, s32[1]{0:T(128)S(6)} %copy.12.valid_ref, bf16[4096,1024]{1,0:T(8,128)(2,1)S(1)} %copy-done.4, f32[8,4096]{1,0:T(8,128)S(1)} %copy-done.6, bf16[192,1024]{1,0:T(8,128)(2,1)S(1)} %get-tuple-element.14.prior3_ref), custom_call_target="tpu_custom_call" | custom-call | tf_op jit(solution)/shard_map/bulk/pallas_call | solution.py:292
  32.9 0.0 copy-start
  32.9 0.0 collective-permute-done.1.after_ref
  32.9 0.0 collective-permute-done.before_ref
  32.9 0.9 %join.1 = f32[8,72,128]{2,1,0:T(8,128)S(1)} custom-call(s32[128]{0:T(128)S(1)} %copy-done.7, s32[1]{0:T(128)S(6)} %copy.12.valid_ref, bf16[4096,1024]{1,0:T(8,128)(2,1)S(1)} %get-tuple-element.15.head_ref.tail_ref.token_ref, bf16[4096,1024]{1,0:T(8,128)(2,1)S(1)} %get-tuple-element.15.head_ref.tail_ref.token_ref, f32[144,1024]{1,0:T(8,128)S(1)} %get-tuple-element.16.sum_ref, ...), custom_call_target="tpu_custom_call" | custom-call | tf_op jit(solution)/shard_map/join/pallas_call | solution.py:310
  33.9 2.3 %copy-done = bf16[4096,1024]{1,0:T(8,128)(2,1)} copy-done((bf16[4096,1024]{1,0:T(8,128)(2,1)}, bf16[4096,1024]{1,0:T(8,128)(2,1)S(1)}, u32[]{:S(2)}) %copy-start) | copy-done | bytes 8388632
  36.2 0.1 collective-permute-start.2
  36.3 1.3 %collective-permute-done.2 = f32[4,72,128]{2,1,0:T(8,128)S(1)} collective-permute-done((f32[4,72,128]{2,1,0:T(8,128)S(1)}, f32[4,72,128]{2,1,0:T(8,128)S(1)}, u32[]{:S(2)}, u32[]{:S(2)}) %collective-permute-start.2) | collective-permute-done | bytes 147488 | tf_op jit(solution)/shard_map/ppermute | solution.py:229
  37.7 0.1 collective-permute-start.3
  37.8 1.6 %collective-permute-start.5 = (f32[72,128]{1,0:T(8,128)S(1)}, f32[72,128]{1,0:T(8,128)S(1)}, u32[]{:S(2)}, u32[]{:S(2)}) collective-permute-start(f32[72,128]{1,0:T(8,128)S(1)} %get-tuple-element.29), channel_id=1, source_target_pairs={{0,6},{1,7},{2,4},{3,5},{4,2},{5,3},{6,0},{7,1},{8,14},{9,15},{10,... | collective-permute-start | bytes 110600 | tf_op jit(solution)/shard_map/ppermute | solution.py:229
  39.4 2.4 %collective-permute-start.4 = (f32[72,128]{1,0:T(8,128)S(1)}, f32[72,128]{1,0:T(8,128)S(1)}, u32[]{:S(2)}, u32[]{:S(2)}) collective-permute-start(f32[72,128]{1,0:T(8,128)S(1)} %get-tuple-element.30), channel_id=1, source_target_pairs={{0,4},{1,5},{2,6},{3,7},{4,0},{5,1},{6,2},{7,3},{8,12},{9,13},{10,... | collective-permute-start | bytes 110600 | tf_op jit(solution)/shard_map/ppermute | solution.py:229
  41.8 0.0 collective-permute-done.3
  41.8 1.2 %collective-permute-done.5 = f32[72,128]{1,0:T(8,128)S(1)} collective-permute-done((f32[72,128]{1,0:T(8,128)S(1)}, f32[72,128]{1,0:T(8,128)S(1)}, u32[]{:S(2)}, u32[]{:S(2)}) %collective-permute-start.5) | collective-permute-done | bytes 36896 | tf_op jit(solution)/shard_map/ppermute | solution.py:229
  43.0 1.8 %collective-permute-done.4 = f32[72,128]{1,0:T(8,128)S(1)} collective-permute-done((f32[72,128]{1,0:T(8,128)S(1)}, f32[72,128]{1,0:T(8,128)S(1)}, u32[]{:S(2)}, u32[]{:S(2)}) %collective-permute-start.4) | collective-permute-done | bytes 36896 | tf_op jit(solution)/shard_map/ppermute | solution.py:229
  44.9 1.6 %collective-permute-start.8 = (f32[72,128]{1,0:T(8,128)S(1)}, f32[72,128]{1,0:T(8,128)S(1)}, u32[]{:S(2)}, u32[]{:S(2)}) collective-permute-start(f32[72,128]{1,0:T(8,128)S(1)} %fusion.1), channel_id=1, source_target_pairs={{0,24},{1,25},{2,26},{3,27},{4,28},{5,29},{6,30},{7,31},{8,16},{9,... | collective-permute-start | bytes 110600 | tf_op jit(solution)/shard_map/ppermute | solution.py:229
  46.5 1.1 %collective-permute-start.7 = (f32[72,128]{1,0:T(8,128)S(1)}, f32[72,128]{1,0:T(8,128)S(1)}, u32[]{:S(2)}, u32[]{:S(2)}) collective-permute-start(f32[72,128]{1,0:T(8,128)S(1)} %fusion.1), channel_id=1, source_target_pairs={{0,16},{1,17},{2,18},{3,19},{4,20},{5,21},{6,22},{7,23},{8,24},{9,... | collective-permute-start | bytes 110600 | tf_op jit(solution)/shard_map/ppermute | solution.py:229
  47.6 1.5 %collective-permute-start.6 = (f32[72,128]{1,0:T(8,128)S(1)}, f32[72,128]{1,0:T(8,128)S(1)}, u32[]{:S(2)}, u32[]{:S(2)}) collective-permute-start(f32[72,128]{1,0:T(8,128)S(1)} %fusion.1), channel_id=1, source_target_pairs={{0,8},{1,9},{2,10},{3,11},{4,12},{5,13},{6,14},{7,15},{8,0},{9,1},... | collective-permute-start | bytes 110600 | tf_op jit(solution)/shard_map/ppermute | solution.py:229
  49.1 0.3 collective-permute-done.8
  49.3 2.6 %collective-permute-done.7 = f32[72,128]{1,0:T(8,128)S(1)} collective-permute-done((f32[72,128]{1,0:T(8,128)S(1)}, f32[72,128]{1,0:T(8,128)S(1)}, u32[]{:S(2)}, u32[]{:S(2)}) %collective-permute-start.7) | collective-permute-done | bytes 36896 | tf_op jit(solution)/shard_map/ppermute | solution.py:229
  51.9 0.0 collective-permute-done.6
  51.9 3.2 %collective-permute-start.11 = (f32[72,128]{1,0:T(8,128)S(1)}, f32[72,128]{1,0:T(8,128)S(1)}, u32[]{:S(2)}, u32[]{:S(2)}) collective-permute-start(f32[72,128]{1,0:T(8,128)S(1)} %add_add_fusion.1), channel_id=1, source_target_pairs={{0,65},{1,64},{2,67},{3,66},{4,69},{5,68},{6,71},{7,70},{8,73},{9,... | collective-permute-start | bytes 110600 | tf_op jit(solution)/shard_map/ppermute | solution.py:229
  55.1 0.8 collective-permute-start.10
  56.0 0.1 collective-permute-start.9
  56.1 1.1 %collective-permute-done.11 = f32[72,128]{1,0:T(8,128)S(1)} collective-permute-done((f32[72,128]{1,0:T(8,128)S(1)}, f32[72,128]{1,0:T(8,128)S(1)}, u32[]{:S(2)}, u32[]{:S(2)}) %collective-permute-start.11) | collective-permute-done | bytes 36896 | tf_op jit(solution)/shard_map/ppermute | solution.py:229
  57.2 3.4 %collective-permute-done.10 = f32[72,128]{1,0:T(8,128)S(1)} collective-permute-done((f32[72,128]{1,0:T(8,128)S(1)}, f32[72,128]{1,0:T(8,128)S(1)}, u32[]{:S(2)}, u32[]{:S(2)}) %collective-permute-start.10) | collective-permute-done | bytes 36896 | tf_op jit(solution)/shard_map/ppermute | solution.py:229
  60.6 0.0 collective-permute-done.9
  60.6 1.1 %collective-permute-start.14 = (f32[72,128]{1,0:T(8,128)S(1)}, f32[72,128]{1,0:T(8,128)S(1)}, u32[]{:S(2)}, u32[]{:S(2)}) collective-permute-start(f32[72,128]{1,0:T(8,128)S(1)} %add_add_fusion), channel_id=1, source_target_pairs={{0,6},{1,7},{2,4},{3,5},{4,2},{5,3},{6,0},{7,1},{8,14},{9,15},{10,... | collective-permute-start | bytes 110600 | tf_op jit(solution)/shard_map/ppermute | solution.py:229
  61.8 1.7 %collective-permute-start.13 = (f32[72,128]{1,0:T(8,128)S(1)}, f32[72,128]{1,0:T(8,128)S(1)}, u32[]{:S(2)}, u32[]{:S(2)}) collective-permute-start(f32[72,128]{1,0:T(8,128)S(1)} %add_add_fusion), channel_id=1, source_target_pairs={{0,4},{1,5},{2,6},{3,7},{4,0},{5,1},{6,2},{7,3},{8,12},{9,13},{10,... | collective-permute-start | bytes 110600 | tf_op jit(solution)/shard_map/ppermute | solution.py:229
  63.5 1.3 %collective-permute-start.12 = (f32[72,128]{1,0:T(8,128)S(1)}, f32[72,128]{1,0:T(8,128)S(1)}, u32[]{:S(2)}, u32[]{:S(2)}) collective-permute-start(f32[72,128]{1,0:T(8,128)S(1)} %add_add_fusion), channel_id=1, source_target_pairs={{0,2},{1,3},{2,0},{3,1},{4,6},{5,7},{6,4},{7,5},{8,10},{9,11},{10,... | collective-permute-start | bytes 110600 | tf_op jit(solution)/shard_map/ppermute | solution.py:229
  64.8 1.1 %collective-permute-done.14 = f32[72,128]{1,0:T(8,128)S(1)} collective-permute-done((f32[72,128]{1,0:T(8,128)S(1)}, f32[72,128]{1,0:T(8,128)S(1)}, u32[]{:S(2)}, u32[]{:S(2)}) %collective-permute-start.14) | collective-permute-done | bytes 36896 | tf_op jit(solution)/shard_map/ppermute | solution.py:229
  65.9 1.3 %collective-permute-done.13 = f32[72,128]{1,0:T(8,128)S(1)} collective-permute-done((f32[72,128]{1,0:T(8,128)S(1)}, f32[72,128]{1,0:T(8,128)S(1)}, u32[]{:S(2)}, u32[]{:S(2)}) %collective-permute-start.13) | collective-permute-done | bytes 36896 | tf_op jit(solution)/shard_map/ppermute | solution.py:229
  67.2 0.2 collective-permute-done.12
  67.4 0.1 collective-permute-start.15
  67.5 1.4 %collective-permute-done.15.other_ref = f32[4,72,128]{2,1,0:T(8,128)S(1)} collective-permute-done((f32[4,72,128]{2,1,0:T(8,128)S(1)}, f32[4,72,128]{2,1,0:T(8,128)S(1)}, u32[]{:S(2)}, u32[]{:S(2)}) %collective-permute-start.15) | collective-permute-done | bytes 147488 | tf_op jit(solution)/shard_map/ppermute | solution.py:229
  68.9 0.0 copy-start.1
  68.9 3.4 %copy-done.1 = bf16[4096,1024]{1,0:T(8,128)(2,1)S(1)} copy-done((bf16[4096,1024]{1,0:T(8,128)(2,1)S(1)}, bf16[4096,1024]{1,0:T(8,128)(2,1)}, u32[]{:S(2)}) %copy-start.1) | copy-done | bytes 8388632
  72.3 0.0 copy-start.2
  72.3 3.5 %basis.1 = (f32[64,1024]{1,0:T(8,128)S(1)}, bf16[128,1024]{1,0:T(8,128)(2,1)S(1)}, f32[64,128]{1,0:T(8,128)S(1)}, f32[64,256]{1,0:T(8,128)S(1)}, f32[64,256]{1,0:T(8,128)S(1)}) custom-call(f32[4,72,128]{2,1,0:T(8,128)S(1)} %pad_maximum_fusion.own_ref, f32[4,72,128]{2,1,0:T(8,128)S(1)} %collective-permute-done.15.other_ref, f32[1024,64]{1,0:T(8,128)S(1)} %copy.8.prior_ref, ...), custom_call_target="tpu_custom_call" | custom-call | tf_op jit(solution)/shard_map/basis/pallas_call | solution.py:330
  75.8 5.6 %collective-permute-start.17 = (f32[64,256]{1,0:T(8,128)S(1)}, f32[64,256]{1,0:T(8,128)S(1)}, u32[]{:S(2)}, u32[]{:S(2)}) collective-permute-start(f32[64,256]{1,0:T(8,128)S(1)} %get-tuple-element.19.head_ref), channel_id=1, source_target_pairs={{1,0},{2,1},{3,2},{4,3},{5,4},{6,5},{7,6},{8,7},{9,8},{10,9},{11,1... | collective-permute-start | bytes 196616 | tf_op jit(solution)/shard_map/ppermute | solution.py:352
  81.4 1.9 %collective-permute-start.16 = (f32[64,256]{1,0:T(8,128)S(1)}, f32[64,256]{1,0:T(8,128)S(1)}, u32[]{:S(2)}, u32[]{:S(2)}) collective-permute-start(f32[64,256]{1,0:T(8,128)S(1)} %get-tuple-element.20.tail_ref), channel_id=1, source_target_pairs={{0,1},{1,2},{2,3},{3,4},{4,5},{5,6},{6,7},{7,8},{8,9},{9,10},{10,1... | collective-permute-start | bytes 196616 | tf_op jit(solution)/shard_map/ppermute | solution.py:351
  83.3 0.0 copy-done.2
  83.3 5.3 %project.1 = (f32[64,4096]{1,0:T(8,128)}, f32[1024,64]{1,0:T(8,128)S(1)}) custom-call(s32[1]{0:T(128)S(6)} %copy.12.valid_ref, bf16[4096,1024]{1,0:T(8,128)(2,1)S(1)} %copy-done.2, bf16[128,1024]{1,0:T(8,128)(2,1)S(1)} %get-tuple-element.22.pair_ref, f32[64,128]{1,0:T(8,128)S(1)} %get-tuple-element.21.shift_ref, f32[64,1024]{1,0:T(8,128)S(1)} %get-tuple-element.23.basis_ref), custom_call_target="tpu_custom_call" | custom-call | tf_op jit(solution)/shard_map/project/pallas_call | solution.py:353
  88.6 0.9 copy.10
  89.5 0.0 collective-permute-done.17.after_ref
  89.5 1.0 %collective-permute-done.16.before_ref = f32[64,256]{1,0:T(8,128)S(1)} collective-permute-done((f32[64,256]{1,0:T(8,128)S(1)}, f32[64,256]{1,0:T(8,128)S(1)}, u32[]{:S(2)}, u32[]{:S(2)}) %collective-permute-start.16) | collective-permute-done | bytes 65568 | tf_op jit(solution)/shard_map/ppermute | solution.py:351
  90.6 1.3 %blend.1 = f32[64,4096]{1,0:T(8,128)} custom-call(s32[128]{0:T(128)S(1)} %copy-done.7, s32[1]{0:T(128)S(6)} %copy.12.valid_ref, f32[64,256]{1,0:T(8,128)S(1)} %get-tuple-element.19.head_ref, f32[64,256]{1,0:T(8,128)S(1)} %get-tuple-element.20.tail_ref, f32[64,256]{1,0:T(8,128)S(1)} %collective-permute-done.16.before_ref, ...), custom_call_target="tpu_custom_call", output_to_operand_aliasing={{}: (7, {})} | custom-call | tf_op jit(solution)/shard_map/blend/pallas_call | solution.py:371
  (7 shorter events, 0.1 us)
Async XLA Ops:
  2.4 3.4 %copy-start.3 = (bf16[4096,1024]{1,0:T(8,128)(2,1)S(1)}, bf16[4096,1024]{1,0:T(8,128)(2,1)}, u32[]{:S(2)}) copy-start(bf16[4096,1024]{1,0:T(8,128)(2,1)} %quant_ref.1) | copy-start | bytes 25165828
  5.8 0.9 copy-start.5
  6.7 10.1 %copy-start.6 = (f32[8,4096]{1,0:T(8,128)S(1)}, f32[8,4096]{1,0:T(8,128)}, u32[]{:S(2)}) copy-start(f32[8,4096]{1,0:T(8,128)} %scale_ref.1) | copy-start | bytes 393220
  6.7 10.1 %copy-start.7 = (s32[128]{0:T(128)S(1)}, s32[128]{0:T(128)}, u32[]{:S(2)}) copy-start(s32[128]{0:T(128)} %width_ref.5) | copy-start | bytes 1540
  7.9 25.0 %collective-permute-start = (f32[72,256]{1,0:T(8,128)S(1)}, f32[72,256]{1,0:T(8,128)S(1)}, u32[]{:S(2)}, u32[]{:S(2)}) collective-permute-start(f32[72,256]{1,0:T(8,128)S(1)} %get-tuple-element.17.forward_ref), channel_id=1, source_target_pairs={{0,1},{1,2},{2,3},{3,4},{4,5},{5,6},{6,7},{7,8},{8,9},{9,10},{10,1... | collective-permute-start | bytes 221192 | tf_op jit(solution)/shard_map/ppermute | solution.py:290
  11.7 21.2 %collective-permute-start.1 = (f32[64,256]{1,0:T(8,128)S(1)}, f32[64,256]{1,0:T(8,128)S(1)}, u32[]{:S(2)}, u32[]{:S(2)}) collective-permute-start(f32[64,256]{1,0:T(8,128)S(1)} %get-tuple-element.18.backward_ref), channel_id=1, source_target_pairs={{1,0},{2,1},{3,2},{4,3},{5,4},{6,5},{7,6},{8,7},{9,8},{10,9},{11,1... | collective-permute-start | bytes 196616 | tf_op jit(solution)/shard_map/ppermute | solution.py:291
  16.8 3.4 %copy-start.4 = (bf16[4096,1024]{1,0:T(8,128)(2,1)S(1)}, bf16[4096,1024]{1,0:T(8,128)(2,1)}, u32[]{:S(2)}) copy-start(bf16[4096,1024]{1,0:T(8,128)(2,1)} %quant_ref.1) | copy-start | bytes 25165828
  32.9 3.3 %copy-start = (bf16[4096,1024]{1,0:T(8,128)(2,1)}, bf16[4096,1024]{1,0:T(8,128)(2,1)S(1)}, u32[]{:S(2)}) copy-start(bf16[4096,1024]{1,0:T(8,128)(2,1)S(1)} %get-tuple-element.15.head_ref.tail_ref.token_ref) | copy-start | bytes 25165828
  36.2 1.5 %collective-permute-start.2 = (f32[4,72,128]{2,1,0:T(8,128)S(1)}, f32[4,72,128]{2,1,0:T(8,128)S(1)}, u32[]{:S(2)}, u32[]{:S(2)}) collective-permute-start(f32[4,72,128]{2,1,0:T(8,128)S(1)} %dynamic-slice_bitcast_fusion), channel_id=1, source_target_pairs={{0,32},{1,33},{2,34},{3,35},{4,36},{5,37},{6,38},{7,39},{8,40},{9,... | collective-permute-start | bytes 442376 | tf_op jit(solution)/shard_map/ppermute | solution.py:229
  37.7 4.2 %collective-permute-start.3 = (f32[72,128]{1,0:T(8,128)S(1)}, f32[72,128]{1,0:T(8,128)S(1)}, u32[]{:S(2)}, u32[]{:S(2)}) collective-permute-start(f32[72,128]{1,0:T(8,128)S(1)} %get-tuple-element.28), channel_id=1, source_target_pairs={{0,2},{1,3},{2,0},{3,1},{4,6},{5,7},{6,4},{7,5},{8,10},{9,11},{10,... | collective-permute-start | bytes 110600 | tf_op jit(solution)/shard_map/ppermute | solution.py:229
  37.8 5.2 %collective-permute-start.5 = (f32[72,128]{1,0:T(8,128)S(1)}, f32[72,128]{1,0:T(8,128)S(1)}, u32[]{:S(2)}, u32[]{:S(2)}) collective-permute-start(f32[72,128]{1,0:T(8,128)S(1)} %get-tuple-element.29), channel_id=1, source_target_pairs={{0,6},{1,7},{2,4},{3,5},{4,2},{5,3},{6,0},{7,1},{8,14},{9,15},{10,... | collective-permute-start | bytes 110600 | tf_op jit(solution)/shard_map/ppermute | solution.py:229
  39.4 5.5 %collective-permute-start.4 = (f32[72,128]{1,0:T(8,128)S(1)}, f32[72,128]{1,0:T(8,128)S(1)}, u32[]{:S(2)}, u32[]{:S(2)}) collective-permute-start(f32[72,128]{1,0:T(8,128)S(1)} %get-tuple-element.30), channel_id=1, source_target_pairs={{0,4},{1,5},{2,6},{3,7},{4,0},{5,1},{6,2},{7,3},{8,12},{9,13},{10,... | collective-permute-start | bytes 110600 | tf_op jit(solution)/shard_map/ppermute | solution.py:229
  44.9 4.4 %collective-permute-start.8 = (f32[72,128]{1,0:T(8,128)S(1)}, f32[72,128]{1,0:T(8,128)S(1)}, u32[]{:S(2)}, u32[]{:S(2)}) collective-permute-start(f32[72,128]{1,0:T(8,128)S(1)} %fusion.1), channel_id=1, source_target_pairs={{0,24},{1,25},{2,26},{3,27},{4,28},{5,29},{6,30},{7,31},{8,16},{9,... | collective-permute-start | bytes 110600 | tf_op jit(solution)/shard_map/ppermute | solution.py:229
  46.5 5.5 %collective-permute-start.7 = (f32[72,128]{1,0:T(8,128)S(1)}, f32[72,128]{1,0:T(8,128)S(1)}, u32[]{:S(2)}, u32[]{:S(2)}) collective-permute-start(f32[72,128]{1,0:T(8,128)S(1)} %fusion.1), channel_id=1, source_target_pairs={{0,16},{1,17},{2,18},{3,19},{4,20},{5,21},{6,22},{7,23},{8,24},{9,... | collective-permute-start | bytes 110600 | tf_op jit(solution)/shard_map/ppermute | solution.py:229
  47.6 4.4 %collective-permute-start.6 = (f32[72,128]{1,0:T(8,128)S(1)}, f32[72,128]{1,0:T(8,128)S(1)}, u32[]{:S(2)}, u32[]{:S(2)}) collective-permute-start(f32[72,128]{1,0:T(8,128)S(1)} %fusion.1), channel_id=1, source_target_pairs={{0,8},{1,9},{2,10},{3,11},{4,12},{5,13},{6,14},{7,15},{8,0},{9,1},... | collective-permute-start | bytes 110600 | tf_op jit(solution)/shard_map/ppermute | solution.py:229
  51.9 5.2 %collective-permute-start.11 = (f32[72,128]{1,0:T(8,128)S(1)}, f32[72,128]{1,0:T(8,128)S(1)}, u32[]{:S(2)}, u32[]{:S(2)}) collective-permute-start(f32[72,128]{1,0:T(8,128)S(1)} %add_add_fusion.1), channel_id=1, source_target_pairs={{0,65},{1,64},{2,67},{3,66},{4,69},{5,68},{6,71},{7,70},{8,73},{9,... | collective-permute-start | bytes 110600 | tf_op jit(solution)/shard_map/ppermute | solution.py:229
  55.1 5.5 %collective-permute-start.10 = (f32[72,128]{1,0:T(8,128)S(1)}, f32[72,128]{1,0:T(8,128)S(1)}, u32[]{:S(2)}, u32[]{:S(2)}) collective-permute-start(f32[72,128]{1,0:T(8,128)S(1)} %add_add_fusion.1), channel_id=1, source_target_pairs={{0,64},{1,65},{2,66},{3,67},{4,68},{5,69},{6,70},{7,71},{8,72},{9,... | collective-permute-start | bytes 110600 | tf_op jit(solution)/shard_map/ppermute | solution.py:229
  56.0 4.6 %collective-permute-start.9 = (f32[72,128]{1,0:T(8,128)S(1)}, f32[72,128]{1,0:T(8,128)S(1)}, u32[]{:S(2)}, u32[]{:S(2)}) collective-permute-start(f32[72,128]{1,0:T(8,128)S(1)} %add_add_fusion.1), channel_id=1, source_target_pairs={{0,1},{1,0},{2,3},{3,2},{4,5},{5,4},{6,7},{7,6},{8,9},{9,8},{10,11... | collective-permute-start | bytes 110600 | tf_op jit(solution)/shard_map/ppermute | solution.py:229
  60.6 5.2 %collective-permute-start.14 = (f32[72,128]{1,0:T(8,128)S(1)}, f32[72,128]{1,0:T(8,128)S(1)}, u32[]{:S(2)}, u32[]{:S(2)}) collective-permute-start(f32[72,128]{1,0:T(8,128)S(1)} %add_add_fusion), channel_id=1, source_target_pairs={{0,6},{1,7},{2,4},{3,5},{4,2},{5,3},{6,0},{7,1},{8,14},{9,15},{10,... | collective-permute-start | bytes 110600 | tf_op jit(solution)/shard_map/ppermute | solution.py:229
  61.8 5.5 %collective-permute-start.13 = (f32[72,128]{1,0:T(8,128)S(1)}, f32[72,128]{1,0:T(8,128)S(1)}, u32[]{:S(2)}, u32[]{:S(2)}) collective-permute-start(f32[72,128]{1,0:T(8,128)S(1)} %add_add_fusion), channel_id=1, source_target_pairs={{0,4},{1,5},{2,6},{3,7},{4,0},{5,1},{6,2},{7,3},{8,12},{9,13},{10,... | collective-permute-start | bytes 110600 | tf_op jit(solution)/shard_map/ppermute | solution.py:229
  63.5 4.0 %collective-permute-start.12 = (f32[72,128]{1,0:T(8,128)S(1)}, f32[72,128]{1,0:T(8,128)S(1)}, u32[]{:S(2)}, u32[]{:S(2)}) collective-permute-start(f32[72,128]{1,0:T(8,128)S(1)} %add_add_fusion), channel_id=1, source_target_pairs={{0,2},{1,3},{2,0},{3,1},{4,6},{5,7},{6,4},{7,5},{8,10},{9,11},{10,... | collective-permute-start | bytes 110600 | tf_op jit(solution)/shard_map/ppermute | solution.py:229
  67.4 1.5 %collective-permute-start.15 = (f32[4,72,128]{2,1,0:T(8,128)S(1)}, f32[4,72,128]{2,1,0:T(8,128)S(1)}, u32[]{:S(2)}, u32[]{:S(2)}) collective-permute-start(f32[4,72,128]{2,1,0:T(8,128)S(1)} %pad_maximum_fusion.own_ref), channel_id=1, source_target_pairs={{0,32},{1,33},{2,34},{3,35},{4,36},{5,37},{6,38},{7,39},{8,40},{9,... | collective-permute-start | bytes 442376 | tf_op jit(solution)/shard_map/ppermute | solution.py:229
  68.9 3.4 %copy-start.1 = (bf16[4096,1024]{1,0:T(8,128)(2,1)S(1)}, bf16[4096,1024]{1,0:T(8,128)(2,1)}, u32[]{:S(2)}) copy-start(bf16[4096,1024]{1,0:T(8,128)(2,1)} %copy-done) | copy-start | bytes 25165828
  72.3 11.1 %copy-start.2 = (bf16[4096,1024]{1,0:T(8,128)(2,1)S(1)}, bf16[4096,1024]{1,0:T(8,128)(2,1)}, u32[]{:S(2)}) copy-start(bf16[4096,1024]{1,0:T(8,128)(2,1)} %copy-done) | copy-start | bytes 25165828
  75.8 13.7 %collective-permute-start.17 = (f32[64,256]{1,0:T(8,128)S(1)}, f32[64,256]{1,0:T(8,128)S(1)}, u32[]{:S(2)}, u32[]{:S(2)}) collective-permute-start(f32[64,256]{1,0:T(8,128)S(1)} %get-tuple-element.19.head_ref), channel_id=1, source_target_pairs={{1,0},{2,1},{3,2},{4,3},{5,4},{6,5},{7,6},{8,7},{9,8},{10,9},{11,1... | collective-permute-start | bytes 196616 | tf_op jit(solution)/shard_map/ppermute | solution.py:352
  81.4 9.2 %collective-permute-start.16 = (f32[64,256]{1,0:T(8,128)S(1)}, f32[64,256]{1,0:T(8,128)S(1)}, u32[]{:S(2)}, u32[]{:S(2)}) collective-permute-start(f32[64,256]{1,0:T(8,128)S(1)} %get-tuple-element.20.tail_ref), channel_id=1, source_target_pairs={{0,1},{1,2},{2,3},{3,4},{4,5},{5,6},{6,7},{7,8},{8,9},{9,10},{10,1... | collective-permute-start | bytes 196616 | tf_op jit(solution)/shard_map/ppermute | solution.py:351

commit v2 on v1

--- a/solution.py
+++ b/solution.py
@@ -36,9 +36,9 @@
 
 
 def reduced_rows(prior, tokens):
-    keep = prior.shape[0] // 3
-    wide = lax.dot_general(prior, tokens, NT, preferred_element_type=F32)
-    return wide[:keep] + wide[keep : 2 * keep] + wide[2 * keep :]
+    wide = lax.dot_general(tokens, prior, NN, preferred_element_type=F32)
+    half = (wide[:, :128] + wide[:, 128:]).T
+    return half[:64] + half[64:]
 
 
 def widths(width_ref, n_tile):
@@ -51,14 +51,16 @@
 
 
 def band_kernel(valid_ref, head_ref, tail_ref, head_s_ref, tail_s_ref, prior_ref,
-                forward_ref, backward_ref, prior3_ref, *, tok_rows):
-    high, mid, low = split3(prior_ref[...].T)
-    prior = jnp.concatenate([high, mid, low], 0)
+                forward_ref, backward_ref, prior3_ref, head_out_ref, tail_out_ref, *, tok_rows):
+    high, mid, low = split3(prior_ref[...])
+    prior = jnp.concatenate([high, mid, low, jnp.zeros_like(low)], 0).T
     prior3_ref[...] = prior
     head = jnp.concatenate(dequantize(head_ref[...], head_s_ref[...]), 1)
+    head_out_ref[...] = head
     backward_ref[...] = reduced_rows(prior, head)
     tail = jnp.concatenate(dequantize(tail_ref[...], tail_s_ref[...]), 1)
-    keep = prior.shape[0] // 3
+    tail_out_ref[...] = tail
+    keep = high.shape[0]
     forward_ref[:keep, :] = reduced_rows(prior, tail)
     place = tok_rows - BAND + lax.broadcasted_iota(jnp.int32, (ROWS - keep, BAND), 1)
     forward_ref[keep:, :] = jnp.where(place < valid_ref[0], 2.0, 1.0)
@@ -158,7 +160,7 @@
                  basis_ref, pair_ref, shift_ref, head_out_ref, tail_out_ref):
     core = lax.rem(lax.axis_index("region"), 2)
     y = lax.rem(lax.div(lax.axis_index("tile"), 2), 4)
-    keep = prior_ref.shape[1]
+    keep = prior_ref.shape[0]
     pieces = []
     for c in range(8):
         slot = jnp.bitwise_xor(c % 4, y)
@@ -166,8 +168,7 @@
     full = jnp.concatenate(pieces, 1)
     sums = full[keep : keep + 1]
     average = sums / full[keep + 1 : keep + 2]
-    prior = prior_ref[...].T
-    image = jnp.sum(prior * average, axis=1, keepdims=True)
+    image = jnp.sum(prior_ref[...] * average, axis=1, keepdims=True)
     update = full[:keep] - image * sums
     square = lax.dot_general(update, update, NT, precision=lax.Precision.HIGHEST, preferred_element_type=F32)
     inverse = inverse_factor(square)
@@ -175,25 +176,21 @@
     basis_ref[...] = basis
     high = basis.astype(BF16)
     low = (basis - high.astype(F32)).astype(BF16)
-    pair = jnp.concatenate([high, low], 0)
+    pair = jnp.concatenate([high, low], 0).T
     pair_ref[...] = pair
     shift_ref[...] = jnp.broadcast_to(jnp.sum(basis * average, axis=1, keepdims=True), shift_ref.shape)
     for rows, out in ((head_ref, head_out_ref), (tail_ref, tail_out_ref)):
-        wide = lax.dot_general(pair, rows[...], NT, preferred_element_type=F32)
+        wide = lax.dot_general(rows[...], pair, NN, preferred_element_type=F32).T
         out[...] = wide[:keep] + wide[keep:]
 
 
-def project_kernel(valid_ref, token_ref, pair_ref, shift_ref, basis_ref, out_ref, basis_out_ref):
+def project_kernel(valid_ref, token_ref, pair_ref, shift_ref, out_ref):
     step = pl.program_id(0)
     keep = shift_ref.shape[0]
-    wide = lax.dot_general(pair_ref[...], token_ref[...], NT, preferred_element_type=F32)
+    wide = lax.dot_general(token_ref[...], pair_ref[...], NN, preferred_element_type=F32).T
     place = step * STEP + lax.broadcasted_iota(jnp.int32, (1, STEP), 1)
     value = wide[:keep] + wide[keep:] - shift_ref[:, :1]
     out_ref[...] = jnp.where(place < valid_ref[0], value, 0.0)
-
-    @pl.when(step == 0)
-    def _():
-        basis_out_ref[...] = basis_ref[...].T
 
 
 def blend_kernel(width_ref, valid_ref, head_ref, tail_ref, before_ref, after_ref, shift_ref,
@@ -267,7 +264,9 @@
     def whole(*shape):
         return pl.BlockSpec(shape, lambda i: (0,) * len(shape))
 
-    forward, backward, prior3 = pl.pallas_call(
+    quantized = pltpu.with_memory_space_constraint(quantized, pltpu.HBM)
+    prior = prior_basis.T
+    forward, backward, prior3, head_tokens, tail_tokens = pl.pallas_call(
         functools.partial(band_kernel, tok_rows=tok_rows),
         grid=(1,),
         in_specs=[
@@ -276,17 +275,25 @@
             tail_rows,
             pl.BlockSpec((groups, BAND), lambda i: (0, 0)),
             pl.BlockSpec((groups, BAND), lambda i: (0, last)),
-            whole(feat_dim, keep),
-        ],
-        out_specs=[whole(ROWS, BAND), whole(keep, BAND), whole(3 * keep, feat_dim)],
+            whole(keep, feat_dim),
+        ],
+        out_specs=[
+            whole(ROWS, BAND),
+            whole(keep, BAND),
+            whole(feat_dim, 4 * keep),
+            whole(BAND, feat_dim),
+            whole(BAND, feat_dim),
+        ],
         out_shape=[
             jax.ShapeDtypeStruct((ROWS, BAND), F32),
             jax.ShapeDtypeStruct((keep, BAND), F32),
-            jax.ShapeDtypeStruct((3 * keep, feat_dim), BF16),
+            jax.ShapeDtypeStruct((feat_dim, 4 * keep), BF16),
+            jax.ShapeDtypeStruct((BAND, feat_dim), BF16),
+            jax.ShapeDtypeStruct((BAND, feat_dim), BF16),
         ],
         compiler_params=params(24),
         name="band",
-    )(valid_count, quantized, quantized, block_scales, block_scales, prior_basis)
+    )(valid_count, quantized, quantized, block_scales, block_scales, prior)
     before = lax.ppermute(forward, "tile", forward_pairs)
     after = lax.ppermute(backward, "tile", backward_pairs)
     tokens, sums = pl.pallas_call(
@@ -297,11 +304,11 @@
             smem(),
             pl.BlockSpec((STEP, feat_dim), lambda i: (i, 0)),
             pl.BlockSpec((groups, STEP), lambda i: (0, i)),
-            whole(3 * keep, feat_dim),
+            whole(feat_dim, 4 * keep),
         ],
         out_specs=[pl.BlockSpec((STEP, feat_dim), lambda i: (i, 0)), whole(2 * keep + 16, feat_dim)],
         out_shape=[
-            jax.ShapeDtypeStruct((tok_rows, feat_dim), BF16),
+            pltpu.HBM((tok_rows, feat_dim), BF16),
             jax.ShapeDtypeStruct((2 * keep + 16, feat_dim), F32),
         ],
         compiler_params=params(32),
@@ -313,8 +320,8 @@
         in_specs=[
             smem(),
             smem(),
-            head_rows,
-            tail_rows,
+            whole(BAND, feat_dim),
+            whole(BAND, feat_dim),
             whole(2 * keep + 16, feat_dim),
             whole(ROWS, BAND),
             whole(keep, BAND),
@@ -325,49 +332,51 @@
         out_shape=jax.ShapeDtypeStruct((feat_dim // 128, ROWS, 128), F32),
         compiler_params=params(24),
         name="join",
-    )(band_width, valid_count, tokens, tokens, sums, forward, backward, before, after)
+    )(band_width, valid_count, head_tokens, tail_tokens, sums, forward, backward, before, after)
     own, other = reduce_all(pieces)
     basis, pair, shift, head, tail = pl.pallas_call(
         basis_kernel,
         grid=(1,),
-        in_specs=[whole(4, ROWS, 128), whole(4, ROWS, 128), whole(feat_dim, keep), head_rows, tail_rows],
+        in_specs=[
+            whole(4, ROWS, 128),
+            whole(4, ROWS, 128),
+            whole(keep, feat_dim),
+            whole(BAND, feat_dim),
+            whole(BAND, feat_dim),
+        ],
         out_specs=[
             whole(keep, feat_dim),
-            whole(2 * keep, feat_dim),
+            whole(feat_dim, 2 * keep),
             whole(keep, 128),
             whole(keep, BAND),
             whole(keep, BAND),
         ],
         out_shape=[
             jax.ShapeDtypeStruct((keep, feat_dim), F32),
-            jax.ShapeDtypeStruct((2 * keep, feat_dim), BF16),
+            jax.ShapeDtypeStruct((feat_dim, 2 * keep), BF16),
             jax.ShapeDtypeStruct((keep, 128), F32),
             jax.ShapeDtypeStruct((keep, BAND), F32),
             jax.ShapeDtypeStruct((keep, BAND), F32),
         ],
         compiler_params=params(24),
         name="basis",
-    )(own, other, prior_basis, tokens, tokens)
+    )(own, other, prior, head_tokens, tail_tokens)
     before = lax.ppermute(tail, "tile", forward_pairs)
     after = lax.ppermute(head, "tile", backward_pairs)
-    raw, new_basis = pl.pallas_call(
+    raw = pl.pallas_call(
         project_kernel,
         grid=(steps,),
         in_specs=[
             smem(),
             pl.BlockSpec((STEP, feat_dim), lambda i: (i, 0)),
-            whole(2 * keep, feat_dim),
+            whole(feat_dim, 2 * keep),
             whole(keep, 128),
-            whole(keep, feat_dim),
-        ],
-        out_specs=[pl.BlockSpec((keep, STEP), lambda i: (0, i)), whole(feat_dim, keep)],
-        out_shape=[
-            jax.ShapeDtypeStruct((keep, tok_rows), F32),
-            jax.ShapeDtypeStruct((feat_dim, keep), F32),
-        ],
+        ],
+        out_specs=pl.BlockSpec((keep, STEP), lambda i: (0, i)),
+        out_shape=jax.ShapeDtypeStruct((keep, tok_rows), F32),
         compiler_params=params(24),
         name="project",
-    )(valid_count, tokens, pair, shift, basis)
+    )(valid_count, pltpu.with_memory_space_constraint(tokens, pltpu.HBM), pair, shift)
     projected = pl.pallas_call(
         functools.partial(blend_kernel, tok_rows=tok_rows, n_tile=n_tile),
         in_specs=[smem(), smem()]
@@ -380,7 +389,7 @@
         compiler_params=params(8),
         name="blend",
     )(band_width, valid_count, head, tail, before, after, shift, raw)
-    return projected, new_basis
+    return projected, basis.T
 
 
 def solution(mesh):

time: 92.2 us -> 88.2 us (0.957)
  local copies, waits for them, and re-layouts: 15.4 us -> 1.9 us
  Pallas kernels: 24.9 us -> 34 us
  starting transfers between devices: 33.2 us -> 34.7 us
  waiting for transfers between devices: 16.7 us -> 15.3 us
    unnamed x18 -> x10, local copies, waits for them, and re-layouts: 15.4 us -> 1.86 us
    pallas_call x1, Pallas kernels: 12.7 us -> 16.2 us  [per_device(): pl.pallas_call(functools.partial(bulk_kernel, tok_rows=tok_rows, n_tile=n...]
    pallas_call x1, Pallas kernels: 5.29 us -> 8.65 us  [per_device(): pl.pallas_call(project_kernel, grid=(steps,), in_specs=[smem(), pl.BlockS...]
    pallas_call x1, Pallas kernels: 1.16 us -> 2.71 us  [per_device(): pl.pallas_call(functools.partial(band_kernel, tok_rows=tok_rows), grid=(1...]
    ppermute x1, starting transfers between devices: 1.92 us -> 3.27 us  [per_device(): before = lax.ppermute(tail, 'tile', forward_pairs)]
    ppermute x1, waiting for transfers between devices: 1.05 us -> 0.01 us  [per_device(): before = lax.ppermute(tail, 'tile', forward_pairs)]
  transfers between devices with their start and end apart: 18 -> 18, of which waited for: 12 -> 10; matrix products, arithmetic and copies ran while one was open for 1% -> 0% of each run, Pallas kernels for 20% -> 28%
where the time goes in v2:
time: 88.2 us; the launch traced here: 87.4 us
  starting transfers between devices  34.7 us (39%)
  Pallas kernels  34 us (39%)
  waiting for transfers between devices  15.3 us (17%)
  local copies, waits for them, and re-layouts  1.9 us (2%)
  between operations  1.49 us (2%)
    ppermute x14, starting transfers between devices, flip(): return lax.ppermute(value, AXES, pairs)  16.9 us
    pallas_call x1, Pallas kernels, per_device(): pl.pallas_call(functools.partial(bulk_kernel, tok_rows=tok_rows, n_tile=n...  16.2 us
    ppermute x14, waiting for transfers between devices, flip(): return lax.ppermute(value, AXES, pairs)  15.3 us
    pallas_call x1, Pallas kernels, per_device(): pl.pallas_call(project_kernel, grid=(steps,), in_specs=[smem(), pl.BlockS...  8.65 us
    ppermute x1, starting transfers between devices, per_device(): after = lax.ppermute(head, 'tile', backward_pairs)  5.57 us
    ppermute x1, starting transfers between devices, per_device(): after = lax.ppermute(backward, 'tile', backward_pairs)  5.03 us
    pallas_call x1, Pallas kernels, per_device(): pl.pallas_call(basis_kernel, grid=(1,), in_specs=[whole(4, ROWS, 128), wh...  4.13 us
    ppermute x1, starting transfers between devices, per_device(): before = lax.ppermute(forward, 'tile', forward_pairs)  3.96 us
  transfers between devices with their start and end apart: 18, of which 10 were waited for; matrix products, arithmetic and copies ran while one was open for 0% of the time, Pallas kernels for 28%

profile of v2, /device:TPU:2, one launch (start us, length us, event | category | flops | bytes accessed | tf_op | source)
XLA Modules:
  0.0 87.4 jit_solution(5341769901378829723)
XLA Ops:
  1.3 0.0 copy-start
  1.3 0.9 %copy-done = f32[8,4096]{1,0:T(8,128)S(1)} copy-done((f32[8,4096]{1,0:T(8,128)S(1)}, f32[8,4096]{1,0:T(8,128)}, u32[]{:S(2)}) %copy-start) | copy-done | bytes 131096
  2.2 0.0 copy-start.2
  2.2 0.9 %copy-done.2 = f32[1024,64]{0,1:T(8,128)S(1)} copy-done((f32[1024,64]{0,1:T(8,128)S(1)}, f32[1024,64]{0,1:T(8,128)}, u32[]{:S(2)}) %copy-start.2) | copy-done | bytes 262168
  3.1 0.0 copy-start.1
  3.1 0.0 copy-start.4
  3.1 2.7 %band.1 = (f32[72,256]{1,0:T(8,128)S(1)}, f32[64,256]{1,0:T(8,128)S(1)}, bf16[1024,256]{1,0:T(8,128)(2,1)S(1)}, bf16[256,1024]{1,0:T(8,128)(2,1)S(1)}, bf16[256,1024]{1,0:T(8,128)(2,1)S(1)}) custom-call(s32[1]{0:T(128)S(6)} %copy.9.valid_ref, bf16[4096,1024]{1,0:T(8,128)(2,1)} %quant_ref.1, bf16[4096,1024]{1,0:T(8,128)(2,1)} %quant_ref.1, ...), custom_call_target="tpu_custom_call" | custom-call | tf_op jit(solution)/shard_map/band/pallas_call | solution.py:269
  5.9 0.0 copy-start.3
  5.9 4.0 %collective-permute-start = (f32[72,256]{1,0:T(8,128)S(1)}, f32[72,256]{1,0:T(8,128)S(1)}, u32[]{:S(2)}, u32[]{:S(2)}) collective-permute-start(f32[72,256]{1,0:T(8,128)S(1)} %get-tuple-element.18.forward_ref), channel_id=1, source_target_pairs={{0,1},{1,2},{2,3},{3,4},{4,5},{5,6},{6,7},{7,8},{8,9},{9,10},{10,1... | collective-permute-start | bytes 221192 | tf_op jit(solution)/shard_map/ppermute | solution.py:297
  9.8 5.0 %collective-permute-start.1 = (f32[64,256]{1,0:T(8,128)S(1)}, f32[64,256]{1,0:T(8,128)S(1)}, u32[]{:S(2)}, u32[]{:S(2)}) collective-permute-start(f32[64,256]{1,0:T(8,128)S(1)} %get-tuple-element.19.backward_ref), channel_id=1, source_target_pairs={{1,0},{2,1},{3,2},{4,3},{5,4},{6,5},{7,6},{8,7},{9,8},{10,9},{11,1... | collective-permute-start | bytes 196616 | tf_op jit(solution)/shard_map/ppermute | solution.py:298
  14.9 0.0 copy-done.1
  14.9 0.0 copy-done.4
  14.9 16.2 %bulk.1 = (bf16[4096,1024]{1,0:T(8,128)(2,1)}, f32[144,1024]{1,0:T(8,128)S(1)}) custom-call(s32[128]{0:T(128)S(1)} %copy-done.4, s32[1]{0:T(128)S(6)} %copy.9.valid_ref, bf16[4096,1024]{1,0:T(8,128)(2,1)} %quant_ref.1, f32[8,4096]{1,0:T(8,128)S(1)} %copy-done.1, bf16[1024,256]{1,0:T(8,128)(2,1)S(1)} %get-tuple-element.16.prior3_ref), custom_call_target="tpu_custom_call" | custom-call | tf_op jit(solution)/shard_map/bulk/pallas_call | solution.py:299
  31.1 0.0 collective-permute-done.1.after_ref
  31.1 0.0 collective-permute-done.before_ref
  31.1 0.9 %join.1 = f32[8,72,128]{2,1,0:T(8,128)S(1)} custom-call(s32[128]{0:T(128)S(1)} %copy-done.4, s32[1]{0:T(128)S(6)} %copy.9.valid_ref, bf16[256,1024]{1,0:T(8,128)(2,1)S(1)} %get-tuple-element.14.head_ref, bf16[256,1024]{1,0:T(8,128)(2,1)S(1)} %get-tuple-element.15.tail_ref, f32[144,1024]{1,0:T(8,128)S(1)} %get-tuple-element.17.sum_ref, ...), custom_call_target="tpu_custom_call" | custom-call | tf_op jit(solution)/shard_map/join/pallas_call | solution.py:317
  32.1 0.1 collective-permute-start.2
  32.2 1.3 %collective-permute-done.2 = f32[4,72,128]{2,1,0:T(8,128)S(1)} collective-permute-done((f32[4,72,128]{2,1,0:T(8,128)S(1)}, f32[4,72,128]{2,1,0:T(8,128)S(1)}, u32[]{:S(2)}, u32[]{:S(2)}) %collective-permute-start.2) | collective-permute-done | bytes 147488 | tf_op jit(solution)/shard_map/ppermute | solution.py:226
  33.6 1.0 %collective-permute-start.5 = (f32[72,128]{1,0:T(8,128)S(1)}, f32[72,128]{1,0:T(8,128)S(1)}, u32[]{:S(2)}, u32[]{:S(2)}) collective-permute-start(f32[72,128]{1,0:T(8,128)S(1)} %get-tuple-element.27), channel_id=1, source_target_pairs={{0,6},{1,7},{2,4},{3,5},{4,2},{5,3},{6,0},{7,1},{8,14},{9,15},{10,... | collective-permute-start | bytes 110600 | tf_op jit(solution)/shard_map/ppermute | solution.py:226
  34.6 0.6 collective-permute-start.4
  35.2 2.6 %collective-permute-start.3 = (f32[72,128]{1,0:T(8,128)S(1)}, f32[72,128]{1,0:T(8,128)S(1)}, u32[]{:S(2)}, u32[]{:S(2)}) collective-permute-start(f32[72,128]{1,0:T(8,128)S(1)} %get-tuple-element.26), channel_id=1, source_target_pairs={{0,2},{1,3},{2,0},{3,1},{4,6},{5,7},{6,4},{7,5},{8,10},{9,11},{10,... | collective-permute-start | bytes 110600 | tf_op jit(solution)/shard_map/ppermute | solution.py:226
  37.8 1.5 %collective-permute-done.5 = f32[72,128]{1,0:T(8,128)S(1)} collective-permute-done((f32[72,128]{1,0:T(8,128)S(1)}, f32[72,128]{1,0:T(8,128)S(1)}, u32[]{:S(2)}, u32[]{:S(2)}) %collective-permute-start.5) | collective-permute-done | bytes 36896 | tf_op jit(solution)/shard_map/ppermute | solution.py:226
  39.2 0.8 collective-permute-done.4
  40.0 0.1 collective-permute-done.3
  40.1 1.6 %collective-permute-start.8 = (f32[72,128]{1,0:T(8,128)S(1)}, f32[72,128]{1,0:T(8,128)S(1)}, u32[]{:S(2)}, u32[]{:S(2)}) collective-permute-start(f32[72,128]{1,0:T(8,128)S(1)} %fusion.1), channel_id=1, source_target_pairs={{0,24},{1,25},{2,26},{3,27},{4,28},{5,29},{6,30},{7,31},{8,16},{9,... | collective-permute-start | bytes 110600 | tf_op jit(solution)/shard_map/ppermute | solution.py:226
  41.7 1.1 %collective-permute-start.7 = (f32[72,128]{1,0:T(8,128)S(1)}, f32[72,128]{1,0:T(8,128)S(1)}, u32[]{:S(2)}, u32[]{:S(2)}) collective-permute-start(f32[72,128]{1,0:T(8,128)S(1)} %fusion.1), channel_id=1, source_target_pairs={{0,16},{1,17},{2,18},{3,19},{4,20},{5,21},{6,22},{7,23},{8,24},{9,... | collective-permute-start | bytes 110600 | tf_op jit(solution)/shard_map/ppermute | solution.py:226
  42.7 1.5 %collective-permute-start.6 = (f32[72,128]{1,0:T(8,128)S(1)}, f32[72,128]{1,0:T(8,128)S(1)}, u32[]{:S(2)}, u32[]{:S(2)}) collective-permute-start(f32[72,128]{1,0:T(8,128)S(1)} %fusion.1), channel_id=1, source_target_pairs={{0,8},{1,9},{2,10},{3,11},{4,12},{5,13},{6,14},{7,15},{8,0},{9,1},... | collective-permute-start | bytes 110600 | tf_op jit(solution)/shard_map/ppermute | solution.py:226
  44.3 0.0 collective-permute-done.8
  44.3 2.9 %collective-permute-done.7 = f32[72,128]{1,0:T(8,128)S(1)} collective-permute-done((f32[72,128]{1,0:T(8,128)S(1)}, f32[72,128]{1,0:T(8,128)S(1)}, u32[]{:S(2)}, u32[]{:S(2)}) %collective-permute-start.7) | collective-permute-done | bytes 36896 | tf_op jit(solution)/shard_map/ppermute | solution.py:226
  47.1 0.0 collective-permute-done.6
  47.1 3.2 %collective-permute-start.11 = (f32[72,128]{1,0:T(8,128)S(1)}, f32[72,128]{1,0:T(8,128)S(1)}, u32[]{:S(2)}, u32[]{:S(2)}) collective-permute-start(f32[72,128]{1,0:T(8,128)S(1)} %add_add_fusion.1), channel_id=1, source_target_pairs={{0,65},{1,64},{2,67},{3,66},{4,69},{5,68},{6,71},{7,70},{8,73},{9,... | collective-permute-start | bytes 110600 | tf_op jit(solution)/shard_map/ppermute | solution.py:226
  50.3 0.9 %collective-permute-start.10 = (f32[72,128]{1,0:T(8,128)S(1)}, f32[72,128]{1,0:T(8,128)S(1)}, u32[]{:S(2)}, u32[]{:S(2)}) collective-permute-start(f32[72,128]{1,0:T(8,128)S(1)} %add_add_fusion.1), channel_id=1, source_target_pairs={{0,64},{1,65},{2,66},{3,67},{4,68},{5,69},{6,70},{7,71},{8,72},{9,... | collective-permute-start | bytes 110600 | tf_op jit(solution)/shard_map/ppermute | solution.py:226
  51.2 0.1 collective-permute-start.9
  51.3 1.1 %collective-permute-done.11 = f32[72,128]{1,0:T(8,128)S(1)} collective-permute-done((f32[72,128]{1,0:T(8,128)S(1)}, f32[72,128]{1,0:T(8,128)S(1)}, u32[]{:S(2)}, u32[]{:S(2)}) %collective-permute-start.11) | collective-permute-done | bytes 36896 | tf_op jit(solution)/shard_map/ppermute | solution.py:226
  52.4 3.4 %collective-permute-done.10 = f32[72,128]{1,0:T(8,128)S(1)} collective-permute-done((f32[72,128]{1,0:T(8,128)S(1)}, f32[72,128]{1,0:T(8,128)S(1)}, u32[]{:S(2)}, u32[]{:S(2)}) %collective-permute-start.10) | collective-permute-done | bytes 36896 | tf_op jit(solution)/shard_map/ppermute | solution.py:226
  55.8 0.0 collective-permute-done.9
  55.8 1.7 %collective-permute-start.14 = (f32[72,128]{1,0:T(8,128)S(1)}, f32[72,128]{1,0:T(8,128)S(1)}, u32[]{:S(2)}, u32[]{:S(2)}) collective-permute-start(f32[72,128]{1,0:T(8,128)S(1)} %add_add_fusion), channel_id=1, source_target_pairs={{0,6},{1,7},{2,4},{3,5},{4,2},{5,3},{6,0},{7,1},{8,14},{9,15},{10,... | collective-permute-start | bytes 110600 | tf_op jit(solution)/shard_map/ppermute | solution.py:226
  57.5 1.4 %collective-permute-start.13 = (f32[72,128]{1,0:T(8,128)S(1)}, f32[72,128]{1,0:T(8,128)S(1)}, u32[]{:S(2)}, u32[]{:S(2)}) collective-permute-start(f32[72,128]{1,0:T(8,128)S(1)} %add_add_fusion), channel_id=1, source_target_pairs={{0,4},{1,5},{2,6},{3,7},{4,0},{5,1},{6,2},{7,3},{8,12},{9,13},{10,... | collective-permute-start | bytes 110600 | tf_op jit(solution)/shard_map/ppermute | solution.py:226
  59.0 1.0 %collective-permute-start.12 = (f32[72,128]{1,0:T(8,128)S(1)}, f32[72,128]{1,0:T(8,128)S(1)}, u32[]{:S(2)}, u32[]{:S(2)}) collective-permute-start(f32[72,128]{1,0:T(8,128)S(1)} %add_add_fusion), channel_id=1, source_target_pairs={{0,2},{1,3},{2,0},{3,1},{4,6},{5,7},{6,4},{7,5},{8,10},{9,11},{10,... | collective-permute-start | bytes 110600 | tf_op jit(solution)/shard_map/ppermute | solution.py:226
  60.0 1.1 %collective-permute-done.14 = f32[72,128]{1,0:T(8,128)S(1)} collective-permute-done((f32[72,128]{1,0:T(8,128)S(1)}, f32[72,128]{1,0:T(8,128)S(1)}, u32[]{:S(2)}, u32[]{:S(2)}) %collective-permute-start.14) | collective-permute-done | bytes 36896 | tf_op jit(solution)/shard_map/ppermute | solution.py:226
  61.0 1.9 %collective-permute-done.13 = f32[72,128]{1,0:T(8,128)S(1)} collective-permute-done((f32[72,128]{1,0:T(8,128)S(1)}, f32[72,128]{1,0:T(8,128)S(1)}, u32[]{:S(2)}, u32[]{:S(2)}) %collective-permute-start.13) | collective-permute-done | bytes 36896 | tf_op jit(solution)/shard_map/ppermute | solution.py:226
  63.0 0.0 collective-permute-done.12
  63.0 0.1 collective-permute-start.15
  63.1 1.4 %collective-permute-done.15.other_ref = f32[4,72,128]{2,1,0:T(8,128)S(1)} collective-permute-done((f32[4,72,128]{2,1,0:T(8,128)S(1)}, f32[4,72,128]{2,1,0:T(8,128)S(1)}, u32[]{:S(2)}, u32[]{:S(2)}) %collective-permute-start.15) | collective-permute-done | bytes 147488 | tf_op jit(solution)/shard_map/ppermute | solution.py:226
  64.5 0.0 copy-done.3
  64.5 4.1 %basis.1 = (f32[64,1024]{1,0:T(8,128)}, bf16[1024,128]{1,0:T(8,128)(2,1)S(1)}, f32[64,128]{1,0:T(8,128)S(1)}, f32[64,256]{1,0:T(8,128)S(1)}, f32[64,256]{1,0:T(8,128)S(1)}) custom-call(f32[4,72,128]{2,1,0:T(8,128)S(1)} %pad_maximum_fusion.own_ref, f32[4,72,128]{2,1,0:T(8,128)S(1)} %collective-permute-done.15.other_ref, f32[64,1024]{1,0:T(8,128)S(1)} %bitcast.26, ...), custom_call_target="tpu_custom_call" | custom-call | tf_op jit(solution)/shard_map/basis/pallas_call | solution.py:337
  68.6 3.3 %collective-permute-start.16 = (f32[64,256]{1,0:T(8,128)S(1)}, f32[64,256]{1,0:T(8,128)S(1)}, u32[]{:S(2)}, u32[]{:S(2)}) collective-permute-start(f32[64,256]{1,0:T(8,128)S(1)} %get-tuple-element.21.tail_ref), channel_id=1, source_target_pairs={{0,1},{1,2},{2,3},{3,4},{4,5},{5,6},{6,7},{7,8},{8,9},{9,10},{10,1... | collective-permute-start | bytes 196616 | tf_op jit(solution)/shard_map/ppermute | solution.py:364
  71.9 5.6 %collective-permute-start.17 = (f32[64,256]{1,0:T(8,128)S(1)}, f32[64,256]{1,0:T(8,128)S(1)}, u32[]{:S(2)}, u32[]{:S(2)}) collective-permute-start(f32[64,256]{1,0:T(8,128)S(1)} %get-tuple-element.20.head_ref), channel_id=1, source_target_pairs={{1,0},{2,1},{3,2},{4,3},{5,4},{6,5},{7,6},{8,7},{9,8},{10,9},{11,1... | collective-permute-start | bytes 196616 | tf_op jit(solution)/shard_map/ppermute | solution.py:365
  77.5 8.6 %project.1.whole_ref = f32[64,4096]{1,0:T(8,128)} custom-call(s32[1]{0:T(128)S(6)} %copy.9.valid_ref, bf16[4096,1024]{1,0:T(8,128)(2,1)} %get-tuple-element.23.token_ref, bf16[1024,128]{1,0:T(8,128)(2,1)S(1)} %get-tuple-element.24.pair_ref, f32[64,128]{1,0:T(8,128)S(1)} %get-tuple-element.22.shift_ref), custom_call_target="tpu_custom_call" | custom-call | tf_op jit(solution)/shard_map/project/pallas_call | solution.py:366
  86.1 0.0 collective-permute-done.16.before_ref
  86.1 0.0 collective-permute-done.17.after_ref
  86.1 1.3 %blend.1 = f32[64,4096]{1,0:T(8,128)} custom-call(s32[128]{0:T(128)S(1)} %copy-done.4, s32[1]{0:T(128)S(6)} %copy.9.valid_ref, f32[64,256]{1,0:T(8,128)S(1)} %get-tuple-element.20.head_ref, f32[64,256]{1,0:T(8,128)S(1)} %get-tuple-element.21.tail_ref, f32[64,256]{1,0:T(8,128)S(1)} %collective-permute-done.16.before_ref, ...), custom_call_target="tpu_custom_call", output_to_operand_aliasing={{}: (7, {})} | custom-call | tf_op jit(solution)/shard_map/blend/pallas_call | solution.py:380
  (7 shorter events, 0.1 us)
Async XLA Ops:
  1.3 0.9 %copy-start = (f32[8,4096]{1,0:T(8,128)S(1)}, f32[8,4096]{1,0:T(8,128)}, u32[]{:S(2)}) copy-start(f32[8,4096]{1,0:T(8,128)} %scale_ref.1) | copy-start | bytes 393220
  2.2 0.9 %copy-start.2 = (f32[1024,64]{0,1:T(8,128)S(1)}, f32[1024,64]{0,1:T(8,128)}, u32[]{:S(2)}) copy-start(f32[1024,64]{0,1:T(8,128)} %param.9) | copy-start | bytes 786436
  3.1 11.8 %copy-start.1 = (f32[8,4096]{1,0:T(8,128)S(1)}, f32[8,4096]{1,0:T(8,128)}, u32[]{:S(2)}) copy-start(f32[8,4096]{1,0:T(8,128)} %scale_ref.1) | copy-start | bytes 393220
  3.1 11.8 %copy-start.4 = (s32[128]{0:T(128)S(1)}, s32[128]{0:T(128)}, u32[]{:S(2)}) copy-start(s32[128]{0:T(128)} %width_ref.5) | copy-start | bytes 1540
  5.9 58.6 %copy-start.3 = (f32[1024,64]{0,1:T(8,128)S(1)}, f32[1024,64]{0,1:T(8,128)}, u32[]{:S(2)}) copy-start(f32[1024,64]{0,1:T(8,128)} %param.9) | copy-start | bytes 786436
  5.9 25.2 %collective-permute-start = (f32[72,256]{1,0:T(8,128)S(1)}, f32[72,256]{1,0:T(8,128)S(1)}, u32[]{:S(2)}, u32[]{:S(2)}) collective-permute-start(f32[72,256]{1,0:T(8,128)S(1)} %get-tuple-element.18.forward_ref), channel_id=1, source_target_pairs={{0,1},{1,2},{2,3},{3,4},{4,5},{5,6},{6,7},{7,8},{8,9},{9,10},{10,1... | collective-permute-start | bytes 221192 | tf_op jit(solution)/shard_map/ppermute | solution.py:297
  9.8 21.3 %collective-permute-start.1 = (f32[64,256]{1,0:T(8,128)S(1)}, f32[64,256]{1,0:T(8,128)S(1)}, u32[]{:S(2)}, u32[]{:S(2)}) collective-permute-start(f32[64,256]{1,0:T(8,128)S(1)} %get-tuple-element.19.backward_ref), channel_id=1, source_target_pairs={{1,0},{2,1},{3,2},{4,3},{5,4},{6,5},{7,6},{8,7},{9,8},{10,9},{11,1... | collective-permute-start | bytes 196616 | tf_op jit(solution)/shard_map/ppermute | solution.py:298
  32.1 1.5 %collective-permute-start.2 = (f32[4,72,128]{2,1,0:T(8,128)S(1)}, f32[4,72,128]{2,1,0:T(8,128)S(1)}, u32[]{:S(2)}, u32[]{:S(2)}) collective-permute-start(f32[4,72,128]{2,1,0:T(8,128)S(1)} %dynamic-slice_bitcast_fusion), channel_id=1, source_target_pairs={{0,32},{1,33},{2,34},{3,35},{4,36},{5,37},{6,38},{7,39},{8,40},{9,... | collective-permute-start | bytes 442376 | tf_op jit(solution)/shard_map/ppermute | solution.py:226
  33.6 5.6 %collective-permute-start.5 = (f32[72,128]{1,0:T(8,128)S(1)}, f32[72,128]{1,0:T(8,128)S(1)}, u32[]{:S(2)}, u32[]{:S(2)}) collective-permute-start(f32[72,128]{1,0:T(8,128)S(1)} %get-tuple-element.27), channel_id=1, source_target_pairs={{0,6},{1,7},{2,4},{3,5},{4,2},{5,3},{6,0},{7,1},{8,14},{9,15},{10,... | collective-permute-start | bytes 110600 | tf_op jit(solution)/shard_map/ppermute | solution.py:226
  34.6 5.5 %collective-permute-start.4 = (f32[72,128]{1,0:T(8,128)S(1)}, f32[72,128]{1,0:T(8,128)S(1)}, u32[]{:S(2)}, u32[]{:S(2)}) collective-permute-start(f32[72,128]{1,0:T(8,128)S(1)} %get-tuple-element.28), channel_id=1, source_target_pairs={{0,4},{1,5},{2,6},{3,7},{4,0},{5,1},{6,2},{7,3},{8,12},{9,13},{10,... | collective-permute-start | bytes 110600 | tf_op jit(solution)/shard_map/ppermute | solution.py:226
  35.2 4.9 %collective-permute-start.3 = (f32[72,128]{1,0:T(8,128)S(1)}, f32[72,128]{1,0:T(8,128)S(1)}, u32[]{:S(2)}, u32[]{:S(2)}) collective-permute-start(f32[72,128]{1,0:T(8,128)S(1)} %get-tuple-element.26), channel_id=1, source_target_pairs={{0,2},{1,3},{2,0},{3,1},{4,6},{5,7},{6,4},{7,5},{8,10},{9,11},{10,... | collective-permute-start | bytes 110600 | tf_op jit(solution)/shard_map/ppermute | solution.py:226
  40.1 4.2 %collective-permute-start.8 = (f32[72,128]{1,0:T(8,128)S(1)}, f32[72,128]{1,0:T(8,128)S(1)}, u32[]{:S(2)}, u32[]{:S(2)}) collective-permute-start(f32[72,128]{1,0:T(8,128)S(1)} %fusion.1), channel_id=1, source_target_pairs={{0,24},{1,25},{2,26},{3,27},{4,28},{5,29},{6,30},{7,31},{8,16},{9,... | collective-permute-start | bytes 110600 | tf_op jit(solution)/shard_map/ppermute | solution.py:226
  41.7 5.5 %collective-permute-start.7 = (f32[72,128]{1,0:T(8,128)S(1)}, f32[72,128]{1,0:T(8,128)S(1)}, u32[]{:S(2)}, u32[]{:S(2)}) collective-permute-start(f32[72,128]{1,0:T(8,128)S(1)} %fusion.1), channel_id=1, source_target_pairs={{0,16},{1,17},{2,18},{3,19},{4,20},{5,21},{6,22},{7,23},{8,24},{9,... | collective-permute-start | bytes 110600 | tf_op jit(solution)/shard_map/ppermute | solution.py:226
  42.7 4.4 %collective-permute-start.6 = (f32[72,128]{1,0:T(8,128)S(1)}, f32[72,128]{1,0:T(8,128)S(1)}, u32[]{:S(2)}, u32[]{:S(2)}) collective-permute-start(f32[72,128]{1,0:T(8,128)S(1)} %fusion.1), channel_id=1, source_target_pairs={{0,8},{1,9},{2,10},{3,11},{4,12},{5,13},{6,14},{7,15},{8,0},{9,1},... | collective-permute-start | bytes 110600 | tf_op jit(solution)/shard_map/ppermute | solution.py:226
  47.1 5.2 %collective-permute-start.11 = (f32[72,128]{1,0:T(8,128)S(1)}, f32[72,128]{1,0:T(8,128)S(1)}, u32[]{:S(2)}, u32[]{:S(2)}) collective-permute-start(f32[72,128]{1,0:T(8,128)S(1)} %add_add_fusion.1), channel_id=1, source_target_pairs={{0,65},{1,64},{2,67},{3,66},{4,69},{5,68},{6,71},{7,70},{8,73},{9,... | collective-permute-start | bytes 110600 | tf_op jit(solution)/shard_map/ppermute | solution.py:226
  50.3 5.5 %collective-permute-start.10 = (f32[72,128]{1,0:T(8,128)S(1)}, f32[72,128]{1,0:T(8,128)S(1)}, u32[]{:S(2)}, u32[]{:S(2)}) collective-permute-start(f32[72,128]{1,0:T(8,128)S(1)} %add_add_fusion.1), channel_id=1, source_target_pairs={{0,64},{1,65},{2,66},{3,67},{4,68},{5,69},{6,70},{7,71},{8,72},{9,... | collective-permute-start | bytes 110600 | tf_op jit(solution)/shard_map/ppermute | solution.py:226
  51.2 4.6 %collective-permute-start.9 = (f32[72,128]{1,0:T(8,128)S(1)}, f32[72,128]{1,0:T(8,128)S(1)}, u32[]{:S(2)}, u32[]{:S(2)}) collective-permute-start(f32[72,128]{1,0:T(8,128)S(1)} %add_add_fusion.1), channel_id=1, source_target_pairs={{0,1},{1,0},{2,3},{3,2},{4,5},{5,4},{6,7},{7,6},{8,9},{9,8},{10,11... | collective-permute-start | bytes 110600 | tf_op jit(solution)/shard_map/ppermute | solution.py:226
  55.8 5.2 %collective-permute-start.14 = (f32[72,128]{1,0:T(8,128)S(1)}, f32[72,128]{1,0:T(8,128)S(1)}, u32[]{:S(2)}, u32[]{:S(2)}) collective-permute-start(f32[72,128]{1,0:T(8,128)S(1)} %add_add_fusion), channel_id=1, source_target_pairs={{0,6},{1,7},{2,4},{3,5},{4,2},{5,3},{6,0},{7,1},{8,14},{9,15},{10,... | collective-permute-start | bytes 110600 | tf_op jit(solution)/shard_map/ppermute | solution.py:226
  57.5 5.5 %collective-permute-start.13 = (f32[72,128]{1,0:T(8,128)S(1)}, f32[72,128]{1,0:T(8,128)S(1)}, u32[]{:S(2)}, u32[]{:S(2)}) collective-permute-start(f32[72,128]{1,0:T(8,128)S(1)} %add_add_fusion), channel_id=1, source_target_pairs={{0,4},{1,5},{2,6},{3,7},{4,0},{5,1},{6,2},{7,3},{8,12},{9,13},{10,... | collective-permute-start | bytes 110600 | tf_op jit(solution)/shard_map/ppermute | solution.py:226
  59.0 4.0 %collective-permute-start.12 = (f32[72,128]{1,0:T(8,128)S(1)}, f32[72,128]{1,0:T(8,128)S(1)}, u32[]{:S(2)}, u32[]{:S(2)}) collective-permute-start(f32[72,128]{1,0:T(8,128)S(1)} %add_add_fusion), channel_id=1, source_target_pairs={{0,2},{1,3},{2,0},{3,1},{4,6},{5,7},{6,4},{7,5},{8,10},{9,11},{10,... | collective-permute-start | bytes 110600 | tf_op jit(solution)/shard_map/ppermute | solution.py:226
  63.0 1.5 %collective-permute-start.15 = (f32[4,72,128]{2,1,0:T(8,128)S(1)}, f32[4,72,128]{2,1,0:T(8,128)S(1)}, u32[]{:S(2)}, u32[]{:S(2)}) collective-permute-start(f32[4,72,128]{2,1,0:T(8,128)S(1)} %pad_maximum_fusion.own_ref), channel_id=1, source_target_pairs={{0,32},{1,33},{2,34},{3,35},{4,36},{5,37},{6,38},{7,39},{8,40},{9,... | collective-permute-start | bytes 442376 | tf_op jit(solution)/shard_map/ppermute | solution.py:226
  68.6 17.5 %collective-permute-start.16 = (f32[64,256]{1,0:T(8,128)S(1)}, f32[64,256]{1,0:T(8,128)S(1)}, u32[]{:S(2)}, u32[]{:S(2)}) collective-permute-start(f32[64,256]{1,0:T(8,128)S(1)} %get-tuple-element.21.tail_ref), channel_id=1, source_target_pairs={{0,1},{1,2},{2,3},{3,4},{4,5},{5,6},{6,7},{7,8},{8,9},{9,10},{10,1... | collective-permute-start | bytes 196616 | tf_op jit(solution)/shard_map/ppermute | solution.py:364
  71.9 14.2 %collective-permute-start.17 = (f32[64,256]{1,0:T(8,128)S(1)}, f32[64,256]{1,0:T(8,128)S(1)}, u32[]{:S(2)}, u32[]{:S(2)}) collective-permute-start(f32[64,256]{1,0:T(8,128)S(1)} %get-tuple-element.20.head_ref), channel_id=1, source_target_pairs={{1,0},{2,1},{3,2},{4,3},{5,4},{6,5},{7,6},{8,7},{9,8},{10,9},{11,1... | collective-permute-start | bytes 196616 | tf_op jit(solution)/shard_map/ppermute | solution.py:365

commit v3 on v2

--- a/solution.py
+++ b/solution.py
@@ -7,8 +7,9 @@
 from jax.experimental.pallas import tpu as pltpu
 from jax.sharding import PartitionSpec as P
 
+
 BAND = 256
-STEP = 512
+STEP = 1024
 ROWS = 72
 AXES = ("region", "tile")
 F32 = jnp.float32
@@ -26,11 +27,14 @@
 
 
 def dequantize(quant, scales):
-    by_token = scales.T
+    rows = quant.shape[0]
     groups = scales.shape[0]
     width = quant.shape[1] // groups
     return [
-        (quant[:, b * width : (b + 1) * width].astype(F32) * by_token[:, b : b + 1]).astype(BF16)
+        (
+            quant[:, b * width : (b + 1) * width].astype(F32)
+            * jnp.broadcast_to(scales[b : b + 1], (width, rows)).T
+        ).astype(BF16)
         for b in range(groups)
     ]
 
@@ -67,29 +71,43 @@
 
 
 def bulk_kernel(width_ref, valid_ref, quant_ref, scale_ref, prior3_ref,
-                token_ref, sum_ref, *, tok_rows, n_tile):
-    step = pl.program_id(0)
+                token_ref, sum_ref, raw_ref, held_ref, in_sem, out_sem, *, tok_rows, n_tile):
+    steps = tok_rows // STEP
+    chunks = [pl.ds(step * STEP, STEP) for step in range(steps)]
+    arrive = [
+        pltpu.make_async_copy(quant_ref.at[rows], raw_ref.at[rows], in_sem.at[step])
+        for step, rows in enumerate(chunks)
+    ]
+    leave = [
+        pltpu.make_async_copy(held_ref.at[rows], token_ref.at[rows], out_sem.at[step])
+        for step, rows in enumerate(chunks)
+    ]
+    for copy in arrive:
+        copy.start()
     left, right = widths(width_ref, n_tile)
-    for b, block in enumerate(dequantize(quant_ref[...], scale_ref[...])):
-        token_ref[:, b * block.shape[1] : (b + 1) * block.shape[1]] = block
-    tokens = token_ref[...]
-    reduced = reduced_rows(prior3_ref[...], tokens)
-    place = step * STEP + lax.broadcasted_iota(jnp.int32, (1, STEP), 1)
-    inner = (place >= left) & (place < tok_rows - right) & (place < valid_ref[0])
-    weight = jnp.where(inner, 1.0, 0.0)
-    reduced = reduced * weight
-    high = reduced.astype(BF16)
-    low = (reduced - high.astype(F32)).astype(BF16)
-    extra = jnp.broadcast_to(weight, (16, STEP)).astype(BF16)
-    part = lax.dot_general(jnp.concatenate([high, low, extra], 0), tokens, NN, preferred_element_type=F32)
-
-    @pl.when(step == 0)
-    def _():
-        sum_ref[...] = part
-
-    @pl.when(step > 0)
-    def _():
-        sum_ref[...] += part
+    for step in range(steps + 1):
+        if step < steps:
+            arrive[step].wait()
+            blocks = dequantize(raw_ref[chunks[step], :], scale_ref[:, chunks[step]])
+            for b, block in enumerate(blocks):
+                held_ref[chunks[step], b * block.shape[1] : (b + 1) * block.shape[1]] = block
+        if step > 0:
+            tokens = held_ref[chunks[step - 1], :]
+            reduced = reduced_rows(prior3_ref[...], tokens)
+            place = (step - 1) * STEP + lax.broadcasted_iota(jnp.int32, (1, STEP), 1)
+            inner = (place >= left) & (place < tok_rows - right) & (place < valid_ref[0])
+            weight = jnp.where(inner, 1.0, 0.0)
+            reduced = reduced * weight
+            high = reduced.astype(BF16)
+            low = (reduced - high.astype(F32)).astype(BF16)
+            extra = jnp.broadcast_to(weight, (16, STEP)).astype(BF16)
+            part = lax.dot_general(
+                jnp.concatenate([high, low, extra], 0), tokens, NN, preferred_element_type=F32
+            )
+            sum_ref[...] = part if step == 1 else sum_ref[...] + part
+            leave[step - 1].start()
+    for copy in leave:
+        copy.wait()
 
 
 def join_kernel(width_ref, valid_ref, head_ref, tail_ref, sum_ref, forward_ref, backward_ref,
@@ -156,8 +174,21 @@
     return jnp.concatenate(done, 0)[:, size:]
 
 
-def basis_kernel(own_ref, other_ref, prior_ref, head_ref, tail_ref,
-                 basis_ref, pair_ref, shift_ref, head_out_ref, tail_out_ref):
+def finish_kernel(width_ref, valid_ref, own_ref, other_ref, prior_ref, before_ref, after_ref, token_ref,
+                  basis_ref, out_ref, held_ref, value_ref, in_sem, out_sem, *, tok_rows, n_tile):
+    steps = tok_rows // STEP
+    chunks = [pl.ds(step * STEP, STEP) for step in range(steps)]
+    arrive = [
+        pltpu.make_async_copy(token_ref.at[rows], held_ref.at[rows], in_sem.at[step])
+        for step, rows in enumerate(chunks)
+    ]
+    leave = [
+        pltpu.make_async_copy(value_ref.at[:, rows], out_ref.at[:, rows], out_sem.at[step])
+        for step, rows in enumerate(chunks)
+    ]
+    for copy in arrive:
+        copy.start()
+    left, right = widths(width_ref, n_tile)
     core = lax.rem(lax.axis_index("region"), 2)
     y = lax.rem(lax.div(lax.axis_index("tile"), 2), 4)
     keep = prior_ref.shape[0]
@@ -177,44 +208,44 @@
     high = basis.astype(BF16)
     low = (basis - high.astype(F32)).astype(BF16)
     pair = jnp.concatenate([high, low], 0).T
-    pair_ref[...] = pair
-    shift_ref[...] = jnp.broadcast_to(jnp.sum(basis * average, axis=1, keepdims=True), shift_ref.shape)
-    for rows, out in ((head_ref, head_out_ref), (tail_ref, tail_out_ref)):
-        wide = lax.dot_general(rows[...], pair, NN, preferred_element_type=F32).T
-        out[...] = wide[:keep] + wide[keep:]
-
-
-def project_kernel(valid_ref, token_ref, pair_ref, shift_ref, out_ref):
-    step = pl.program_id(0)
-    keep = shift_ref.shape[0]
-    wide = lax.dot_general(token_ref[...], pair_ref[...], NN, preferred_element_type=F32).T
-    place = step * STEP + lax.broadcasted_iota(jnp.int32, (1, STEP), 1)
-    value = wide[:keep] + wide[keep:] - shift_ref[:, :1]
-    out_ref[...] = jnp.where(place < valid_ref[0], value, 0.0)
-
-
-def blend_kernel(width_ref, valid_ref, head_ref, tail_ref, before_ref, after_ref, shift_ref,
-                 whole_ref, out_ref, buffer_ref, sem_ref, *, tok_rows, n_tile):
-    left, right = widths(width_ref, n_tile)
-    place = lax.broadcasted_iota(jnp.int32, (1, BAND), 1)
-    shift = shift_ref[:, :1]
-    before = pltpu.roll(before_ref[...], lax.rem(left, BAND), 1)
-    after = pltpu.roll(after_ref[...], lax.rem(BAND - right, BAND), 1)
-    head = jnp.where(place < left, (head_ref[...] + before) * 0.5, head_ref[...]) - shift
-    tail = jnp.where(place >= BAND - right, (tail_ref[...] + after) * 0.5, tail_ref[...]) - shift
-    start = tok_rows - BAND
-    buffer_ref[0] = jnp.where(place < valid_ref[0], head, 0.0)
-    buffer_ref[1] = jnp.where(start + place < valid_ref[0], tail, 0.0)
-    first = pltpu.make_async_copy(buffer_ref.at[0], out_ref.at[:, pl.ds(0, BAND)], sem_ref.at[0])
-    second = pltpu.make_async_copy(buffer_ref.at[1], out_ref.at[:, pl.ds(start, BAND)], sem_ref.at[1])
-    first.start()
-    second.start()
-    first.wait()
-    second.wait()
+    shift = jnp.sum(basis * average, axis=1, keepdims=True)
+
+    def project(rows):
+        wide = lax.dot_general(rows, pair, NN, preferred_element_type=F32).T
+        return wide[:keep] + wide[keep:]
+
+    before = pltpu.roll(project(before_ref[...]), lax.rem(left, BAND), 1)
+    after = pltpu.roll(project(after_ref[...]), lax.rem(BAND - right, BAND), 1)
+    near = lax.broadcasted_iota(jnp.int32, (1, BAND), 1)
+    for step in range(steps):
+        arrive[step].wait()
+        value = project(held_ref[chunks[step], :])
+        if step == 0:
+            head = jnp.where(near < left, (value[:, :BAND] + before) * 0.5, value[:, :BAND])
+            value = jnp.concatenate([head, value[:, BAND:]], 1)
+        if step == steps - 1:
+            edge = STEP - BAND
+            tail = jnp.where(near >= BAND - right, (value[:, edge:] + after) * 0.5, value[:, edge:])
+            value = jnp.concatenate([value[:, :edge], tail], 1)
+        place = step * STEP + lax.broadcasted_iota(jnp.int32, (1, STEP), 1)
+        value_ref[:, chunks[step]] = jnp.where(place < valid_ref[0], value - shift, 0.0)
+        if step > 0:
+            leave[step - 1].start()
+    leave[steps - 1].start()
+    for copy in leave:
+        copy.wait()
 
 
 def smem():
     return pl.BlockSpec(memory_space=pltpu.SMEM)
+
+
+def near():
+    return pl.BlockSpec(memory_space=pltpu.VMEM)
+
+
+def far():
+    return pl.BlockSpec(memory_space=pltpu.HBM)
 
 
 def params(mib):
@@ -266,6 +297,8 @@
 
     quantized = pltpu.with_memory_space_constraint(quantized, pltpu.HBM)
     prior = prior_basis.T
+    prior_far = pltpu.with_memory_space_constraint(prior, pltpu.HBM)
+    scales_far = pltpu.with_memory_space_constraint(block_scales, pltpu.HBM)
     forward, backward, prior3, head_tokens, tail_tokens = pl.pallas_call(
         functools.partial(band_kernel, tok_rows=tok_rows),
         grid=(1,),
@@ -293,27 +326,29 @@
         ],
         compiler_params=params(24),
         name="band",
-    )(valid_count, quantized, quantized, block_scales, block_scales, prior)
+    )(valid_count, quantized, quantized, scales_far, scales_far, prior_far)
     before = lax.ppermute(forward, "tile", forward_pairs)
     after = lax.ppermute(backward, "tile", backward_pairs)
-    tokens, sums = pl.pallas_call(
+    before_rows = lax.ppermute(tail_tokens, "tile", forward_pairs)
+    after_rows = lax.ppermute(head_tokens, "tile", backward_pairs)
+    bulk = pl.pallas_call(
         functools.partial(bulk_kernel, tok_rows=tok_rows, n_tile=n_tile),
-        grid=(steps,),
-        in_specs=[
-            smem(),
-            smem(),
-            pl.BlockSpec((STEP, feat_dim), lambda i: (i, 0)),
-            pl.BlockSpec((groups, STEP), lambda i: (0, i)),
-            whole(feat_dim, 4 * keep),
-        ],
-        out_specs=[pl.BlockSpec((STEP, feat_dim), lambda i: (i, 0)), whole(2 * keep + 16, feat_dim)],
+        in_specs=[smem(), smem(), far(), near(), near()],
+        out_specs=[far(), near()],
         out_shape=[
             pltpu.HBM((tok_rows, feat_dim), BF16),
             jax.ShapeDtypeStruct((2 * keep + 16, feat_dim), F32),
         ],
-        compiler_params=params(32),
+        scratch_shapes=[
+            pltpu.VMEM((tok_rows, feat_dim), BF16),
+            pltpu.VMEM((tok_rows, feat_dim), BF16),
+            pltpu.SemaphoreType.DMA((steps,)),
+            pltpu.SemaphoreType.DMA((steps,)),
+        ],
+        compiler_params=params(40),
         name="bulk",
-    )(band_width, valid_count, quantized, block_scales, prior3)
+    )
+    tokens, sums = bulk(band_width, valid_count, quantized, block_scales, prior3)
     pieces = pl.pallas_call(
         functools.partial(join_kernel, tok_rows=tok_rows, n_tile=n_tile),
         grid=(1,),
@@ -334,61 +369,32 @@
         name="join",
     )(band_width, valid_count, head_tokens, tail_tokens, sums, forward, backward, before, after)
     own, other = reduce_all(pieces)
-    basis, pair, shift, head, tail = pl.pallas_call(
-        basis_kernel,
-        grid=(1,),
-        in_specs=[
-            whole(4, ROWS, 128),
-            whole(4, ROWS, 128),
-            whole(keep, feat_dim),
-            whole(BAND, feat_dim),
-            whole(BAND, feat_dim),
-        ],
-        out_specs=[
-            whole(keep, feat_dim),
-            whole(feat_dim, 2 * keep),
-            whole(keep, 128),
-            whole(keep, BAND),
-            whole(keep, BAND),
-        ],
+    basis, projected = pl.pallas_call(
+        functools.partial(finish_kernel, tok_rows=tok_rows, n_tile=n_tile),
+        in_specs=[smem(), smem()] + [near()] * 5 + [far()],
+        out_specs=[near(), far()],
         out_shape=[
             jax.ShapeDtypeStruct((keep, feat_dim), F32),
-            jax.ShapeDtypeStruct((feat_dim, 2 * keep), BF16),
-            jax.ShapeDtypeStruct((keep, 128), F32),
-            jax.ShapeDtypeStruct((keep, BAND), F32),
-            jax.ShapeDtypeStruct((keep, BAND), F32),
-        ],
-        compiler_params=params(24),
-        name="basis",
-    )(own, other, prior, head_tokens, tail_tokens)
-    before = lax.ppermute(tail, "tile", forward_pairs)
-    after = lax.ppermute(head, "tile", backward_pairs)
-    raw = pl.pallas_call(
-        project_kernel,
-        grid=(steps,),
-        in_specs=[
-            smem(),
-            pl.BlockSpec((STEP, feat_dim), lambda i: (i, 0)),
-            whole(feat_dim, 2 * keep),
-            whole(keep, 128),
-        ],
-        out_specs=pl.BlockSpec((keep, STEP), lambda i: (0, i)),
-        out_shape=jax.ShapeDtypeStruct((keep, tok_rows), F32),
-        compiler_params=params(24),
-        name="project",
-    )(valid_count, pltpu.with_memory_space_constraint(tokens, pltpu.HBM), pair, shift)
-    projected = pl.pallas_call(
-        functools.partial(blend_kernel, tok_rows=tok_rows, n_tile=n_tile),
-        in_specs=[smem(), smem()]
-        + [pl.BlockSpec(memory_space=pltpu.VMEM)] * 5
-        + [pl.BlockSpec(memory_space=pl.ANY)],
-        out_specs=pl.BlockSpec(memory_space=pl.ANY),
-        out_shape=jax.ShapeDtypeStruct((keep, tok_rows), F32),
-        scratch_shapes=[pltpu.VMEM((2, keep, BAND), F32), pltpu.SemaphoreType.DMA((2,))],
-        input_output_aliases={7: 0},
-        compiler_params=params(8),
-        name="blend",
-    )(band_width, valid_count, head, tail, before, after, shift, raw)
+            pltpu.HBM((keep, tok_rows), F32),
+        ],
+        scratch_shapes=[
+            pltpu.VMEM((tok_rows, feat_dim), BF16),
+            pltpu.VMEM((keep, tok_rows), F32),
+            pltpu.SemaphoreType.DMA((steps,)),
+            pltpu.SemaphoreType.DMA((steps,)),
+        ],
+        compiler_params=params(32),
+        name="finish",
+    )(
+        band_width,
+        valid_count,
+        own,
+        other,
+        prior,
+        before_rows,
+        after_rows,
+        pltpu.with_memory_space_constraint(tokens, pltpu.HBM),
+    )
     return projected, basis.T
 
 

time: 88.2 us -> 83.6 us (0.948)
  Pallas kernels: 34 us -> 25.6 us
  waiting for transfers between devices: 15.3 us -> 20.7 us
  local copies, waits for them, and re-layouts: 1.9 us -> 0.05 us
    pallas_call x4 -> x2, Pallas kernels: 30.3 us -> 22.4 us  [the longest x1 11.3 us: per_device(): pl.pallas_call(functools.partial(finish_kernel, tok_rows=tok_rows, n_tile...]
    ppermute x2, waiting for transfers between devices: 0.01 us -> 6.36 us  [the longest x1 3.33 us: per_device(): after_rows = lax.ppermute(head_tokens, 'tile', backward_pairs)]
    unnamed x10 -> x6, local copies, waits for them, and re-layouts: 1.86 us -> 0.01 us
    ppermute x2, starting transfers between devices: 8.84 us -> 9.94 us  [the longest x1 6.14 us: per_device(): after_rows = lax.ppermute(head_tokens, 'tile', backward_pairs)]
    ppermute x14, waiting for transfers between devices: 15.3 us -> 14.3 us  [flip(): return lax.ppermute(value, AXES, pairs)]
  transfers between devices with their start and end apart: 18 -> 18, of which waited for: 10 -> 11; matrix products, arithmetic and copies ran while one was open for 0% -> 0% of each run, Pallas kernels for 28% -> 13%
where the time goes in v3:
time: 83.6 us; the launch traced here: 83.4 us
  starting transfers between devices  35.2 us (42%)
  Pallas kernels  25.6 us (31%)
  waiting for transfers between devices  20.7 us (25%)
  between operations  1.71 us (2%)
    ppermute x14, starting transfers between devices, flip(): return lax.ppermute(value, AXES, pairs)  16.3 us
    ppermute x14, waiting for transfers between devices, flip(): return lax.ppermute(value, AXES, pairs)  14.3 us
    pallas_call x1, Pallas kernels, per_device(): pl.pallas_call(functools.partial(finish_kernel, tok_rows=tok_rows, n_tile...  11.3 us
    pallas_call x1, Pallas kernels, per_device(): bulk(band_width, valid_count, quantized, block_scales, prior3)  11 us
    ppermute x1, starting transfers between devices, per_device(): after_rows = lax.ppermute(head_tokens, 'tile', backward_pairs)  6.14 us
    ppermute x1, starting transfers between devices, per_device(): after = lax.ppermute(backward, 'tile', backward_pairs)  5.02 us
    ppermute x1, starting transfers between devices, per_device(): before = lax.ppermute(forward, 'tile', forward_pairs)  3.96 us
    ppermute x1, starting transfers between devices, per_device(): before_rows = lax.ppermute(tail_tokens, 'tile', forward_pairs)  3.8 us
  transfers between devices with their start and end apart: 18, of which 11 were waited for; matrix products, arithmetic and copies ran while one was open for 0% of the time, Pallas kernels for 13%

profile of v3, /device:TPU:2, one launch (start us, length us, event | category | flops | bytes accessed | tf_op | source)
XLA Modules:
  0.0 83.4 jit_solution(14507892431808151166)
XLA Ops:
  1.3 0.0 copy-start
  1.3 0.0 copy-start.2
  1.3 2.4 %band.1 = (f32[72,256]{1,0:T(8,128)S(1)}, f32[64,256]{1,0:T(8,128)S(1)}, bf16[1024,256]{1,0:T(8,128)(2,1)S(1)}, bf16[256,1024]{1,0:T(8,128)(2,1)S(1)}, bf16[256,1024]{1,0:T(8,128)(2,1)S(1)}) custom-call(s32[1]{0:T(128)S(6)} %copy.7.valid_ref, bf16[4096,1024]{1,0:T(8,128)(2,1)} %quant_ref.1, bf16[4096,1024]{1,0:T(8,128)(2,1)} %quant_ref.1, ...), custom_call_target="tpu_custom_call" | custom-call | tf_op jit(solution)/shard_map/band/pallas_call | solution.py:302
  3.7 0.0 copy-start.1
  3.7 4.0 %collective-permute-start = (f32[72,256]{1,0:T(8,128)S(1)}, f32[72,256]{1,0:T(8,128)S(1)}, u32[]{:S(2)}, u32[]{:S(2)}) collective-permute-start(f32[72,256]{1,0:T(8,128)S(1)} %get-tuple-element.15.forward_ref), channel_id=1, source_target_pairs={{0,1},{1,2},{2,3},{3,4},{4,5},{5,6},{6,7},{7,8},{8,9},{9,10},{10,1... | collective-permute-start | bytes 221192 | tf_op jit(solution)/shard_map/ppermute | solution.py:330
  7.6 5.0 %collective-permute-start.1 = (f32[64,256]{1,0:T(8,128)S(1)}, f32[64,256]{1,0:T(8,128)S(1)}, u32[]{:S(2)}, u32[]{:S(2)}) collective-permute-start(f32[64,256]{1,0:T(8,128)S(1)} %get-tuple-element.16.backward_ref), channel_id=1, source_target_pairs={{1,0},{2,1},{3,2},{4,3},{5,4},{6,5},{7,6},{8,7},{9,8},{10,9},{11,1... | collective-permute-start | bytes 196616 | tf_op jit(solution)/shard_map/ppermute | solution.py:331
  12.7 0.0 copy-done
  12.7 0.0 copy-done.2
  12.7 11.0 %bulk.1 = (bf16[4096,1024]{1,0:T(8,128)(2,1)}, f32[144,1024]{1,0:T(8,128)S(1)}) custom-call(s32[128]{0:T(128)S(1)} %copy-done.2, s32[1]{0:T(128)S(6)} %copy.7.valid_ref, bf16[4096,1024]{1,0:T(8,128)(2,1)} %quant_ref.1, f32[8,4096]{1,0:T(8,128)S(1)} %copy-done, bf16[1024,256]{1,0:T(8,128)(2,1)S(1)} %get-tuple-element.13.prior3_ref), custom_call_target="tpu_custom_call" | custom-call | tf_op jit(solution)/shard_map/bulk/pallas_call | solution.py:351
  23.7 0.0 collective-permute-done.1.after_ref
  23.8 0.0 collective-permute-done.before_ref
  23.8 0.9 %join.1 = f32[8,72,128]{2,1,0:T(8,128)S(1)} custom-call(s32[128]{0:T(128)S(1)} %copy-done.2, s32[1]{0:T(128)S(6)} %copy.7.valid_ref, bf16[256,1024]{1,0:T(8,128)(2,1)S(1)} %get-tuple-element.11.head_ref, bf16[256,1024]{1,0:T(8,128)(2,1)S(1)} %get-tuple-element.12.tail_ref, f32[144,1024]{1,0:T(8,128)S(1)} %get-tuple-element.14.sum_ref, ...), custom_call_target="tpu_custom_call" | custom-call | tf_op jit(solution)/shard_map/join/pallas_call | solution.py:352
  24.7 0.1 collective-permute-start.2
  24.9 1.3 %collective-permute-done.2 = f32[4,72,128]{2,1,0:T(8,128)S(1)} collective-permute-done((f32[4,72,128]{2,1,0:T(8,128)S(1)}, f32[4,72,128]{2,1,0:T(8,128)S(1)}, u32[]{:S(2)}, u32[]{:S(2)}) %collective-permute-start.2) | collective-permute-done | bytes 147488 | tf_op jit(solution)/shard_map/ppermute | solution.py:257
  26.2 0.1 collective-permute-start.3
  26.3 2.3 %collective-permute-start.4 = (f32[72,128]{1,0:T(8,128)S(1)}, f32[72,128]{1,0:T(8,128)S(1)}, u32[]{:S(2)}, u32[]{:S(2)}) collective-permute-start(f32[72,128]{1,0:T(8,128)S(1)} %get-tuple-element.22), channel_id=1, source_target_pairs={{0,4},{1,5},{2,6},{3,7},{4,0},{5,1},{6,2},{7,3},{8,12},{9,13},{10,... | collective-permute-start | bytes 110600 | tf_op jit(solution)/shard_map/ppermute | solution.py:257
  28.7 2.3 %collective-permute-start.5 = (f32[72,128]{1,0:T(8,128)S(1)}, f32[72,128]{1,0:T(8,128)S(1)}, u32[]{:S(2)}, u32[]{:S(2)}) collective-permute-start(f32[72,128]{1,0:T(8,128)S(1)} %get-tuple-element.21), channel_id=1, source_target_pairs={{0,6},{1,7},{2,4},{3,5},{4,2},{5,3},{6,0},{7,1},{8,14},{9,15},{10,... | collective-permute-start | bytes 110600 | tf_op jit(solution)/shard_map/ppermute | solution.py:257
  31.0 0.0 collective-permute-done.3
  31.0 0.9 %collective-permute-done.4 = f32[72,128]{1,0:T(8,128)S(1)} collective-permute-done((f32[72,128]{1,0:T(8,128)S(1)}, f32[72,128]{1,0:T(8,128)S(1)}, u32[]{:S(2)}, u32[]{:S(2)}) %collective-permute-start.4) | collective-permute-done | bytes 36896 | tf_op jit(solution)/shard_map/ppermute | solution.py:257
  31.9 2.0 %collective-permute-done.5 = f32[72,128]{1,0:T(8,128)S(1)} collective-permute-done((f32[72,128]{1,0:T(8,128)S(1)}, f32[72,128]{1,0:T(8,128)S(1)}, u32[]{:S(2)}, u32[]{:S(2)}) %collective-permute-start.5) | collective-permute-done | bytes 36896 | tf_op jit(solution)/shard_map/ppermute | solution.py:257
  33.9 0.6 collective-permute-start.6
  34.5 2.4 %collective-permute-start.7 = (f32[72,128]{1,0:T(8,128)S(1)}, f32[72,128]{1,0:T(8,128)S(1)}, u32[]{:S(2)}, u32[]{:S(2)}) collective-permute-start(f32[72,128]{1,0:T(8,128)S(1)} %fusion.1), channel_id=1, source_target_pairs={{0,16},{1,17},{2,18},{3,19},{4,20},{5,21},{6,22},{7,23},{8,24},{9,... | collective-permute-start | bytes 110600 | tf_op jit(solution)/shard_map/ppermute | solution.py:257
  36.9 0.5 collective-permute-start.8
  37.4 0.8 collective-permute-done.6
  38.2 1.7 %collective-permute-done.7 = f32[72,128]{1,0:T(8,128)S(1)} collective-permute-done((f32[72,128]{1,0:T(8,128)S(1)}, f32[72,128]{1,0:T(8,128)S(1)}, u32[]{:S(2)}, u32[]{:S(2)}) %collective-permute-start.7) | collective-permute-done | bytes 36896 | tf_op jit(solution)/shard_map/ppermute | solution.py:257
  39.9 0.9 %collective-permute-done.8 = f32[72,128]{1,0:T(8,128)S(1)} collective-permute-done((f32[72,128]{1,0:T(8,128)S(1)}, f32[72,128]{1,0:T(8,128)S(1)}, u32[]{:S(2)}, u32[]{:S(2)}) %collective-permute-start.8) | collective-permute-done | bytes 36896 | tf_op jit(solution)/shard_map/ppermute | solution.py:257
  40.9 4.0 %collective-permute-start.10 = (f32[72,128]{1,0:T(8,128)S(1)}, f32[72,128]{1,0:T(8,128)S(1)}, u32[]{:S(2)}, u32[]{:S(2)}) collective-permute-start(f32[72,128]{1,0:T(8,128)S(1)} %add_add_fusion.1), channel_id=1, source_target_pairs={{0,64},{1,65},{2,66},{3,67},{4,68},{5,69},{6,70},{7,71},{8,72},{9,... | collective-permute-start | bytes 110600 | tf_op jit(solution)/shard_map/ppermute | solution.py:257
  44.8 0.0 collective-permute-start.11
  44.8 0.1 collective-permute-start.9
  45.0 3.8 %collective-permute-start.16 = (bf16[256,1024]{1,0:T(8,128)(2,1)S(1)}, bf16[256,1024]{1,0:T(8,128)(2,1)S(1)}, u32[]{:S(2)}, u32[]{:S(2)}) collective-permute-start(bf16[256,1024]{1,0:T(8,128)(2,1)S(1)} %get-tuple-element.12.tail_ref), channel_id=1, source_target_pairs={{0,1},{1,2},{2,3},{3,4},{4,5},{5,6},{6,7},{7,8},{8,9},{9,10},{10,1... | collective-permute-start | bytes 1572872 | tf_op jit(solution)/shard_map/ppermute | solution.py:332
  48.8 6.1 %collective-permute-start.17 = (bf16[256,1024]{1,0:T(8,128)(2,1)S(1)}, bf16[256,1024]{1,0:T(8,128)(2,1)S(1)}, u32[]{:S(2)}, u32[]{:S(2)}) collective-permute-start(bf16[256,1024]{1,0:T(8,128)(2,1)S(1)} %get-tuple-element.11.head_ref), channel_id=1, source_target_pairs={{1,0},{2,1},{3,2},{4,3},{5,4},{6,5},{7,6},{8,7},{9,8},{10,9},{11,1... | collective-permute-start | bytes 1572872 | tf_op jit(solution)/shard_map/ppermute | solution.py:333
  54.9 0.0 collective-permute-done.10
  54.9 0.0 collective-permute-done.11
  54.9 0.0 collective-permute-done.9
  55.0 1.8 %collective-permute-start.13 = (f32[72,128]{1,0:T(8,128)S(1)}, f32[72,128]{1,0:T(8,128)S(1)}, u32[]{:S(2)}, u32[]{:S(2)}) collective-permute-start(f32[72,128]{1,0:T(8,128)S(1)} %add_add_fusion), channel_id=1, source_target_pairs={{0,4},{1,5},{2,6},{3,7},{4,0},{5,1},{6,2},{7,3},{8,12},{9,13},{10,... | collective-permute-start | bytes 110600 | tf_op jit(solution)/shard_map/ppermute | solution.py:257
  56.7 2.0 %collective-permute-start.14 = (f32[72,128]{1,0:T(8,128)S(1)}, f32[72,128]{1,0:T(8,128)S(1)}, u32[]{:S(2)}, u32[]{:S(2)}) collective-permute-start(f32[72,128]{1,0:T(8,128)S(1)} %add_add_fusion), channel_id=1, source_target_pairs={{0,6},{1,7},{2,4},{3,5},{4,2},{5,3},{6,0},{7,1},{8,14},{9,15},{10,... | collective-permute-start | bytes 110600 | tf_op jit(solution)/shard_map/ppermute | solution.py:257
  58.7 0.0 collective-permute-start.12
  58.7 1.8 %collective-permute-done.13 = f32[72,128]{1,0:T(8,128)S(1)} collective-permute-done((f32[72,128]{1,0:T(8,128)S(1)}, f32[72,128]{1,0:T(8,128)S(1)}, u32[]{:S(2)}, u32[]{:S(2)}) %collective-permute-start.13) | collective-permute-done | bytes 36896 | tf_op jit(solution)/shard_map/ppermute | solution.py:257
  60.5 3.6 %collective-permute-done.14 = f32[72,128]{1,0:T(8,128)S(1)} collective-permute-done((f32[72,128]{1,0:T(8,128)S(1)}, f32[72,128]{1,0:T(8,128)S(1)}, u32[]{:S(2)}, u32[]{:S(2)}) %collective-permute-start.14) | collective-permute-done | bytes 36896 | tf_op jit(solution)/shard_map/ppermute | solution.py:257
  64.1 0.0 collective-permute-done.12
  64.1 0.1 collective-permute-start.15
  64.2 1.4 %collective-permute-done.15.other_ref = f32[4,72,128]{2,1,0:T(8,128)S(1)} collective-permute-done((f32[4,72,128]{2,1,0:T(8,128)S(1)}, f32[4,72,128]{2,1,0:T(8,128)S(1)}, u32[]{:S(2)}, u32[]{:S(2)}) %collective-permute-start.15) | collective-permute-done | bytes 147488 | tf_op jit(solution)/shard_map/ppermute | solution.py:257
  65.5 3.0 %collective-permute-done.16.before_ref = bf16[256,1024]{1,0:T(8,128)(2,1)S(1)} collective-permute-done((bf16[256,1024]{1,0:T(8,128)(2,1)S(1)}, bf16[256,1024]{1,0:T(8,128)(2,1)S(1)}, u32[]{:S(2)}, u32[]{:S(2)}) %collective-permute-start.16) | collective-permute-done | bytes 524320 | tf_op jit(solution)/shard_map/ppermute | solution.py:332
  68.6 3.3 %collective-permute-done.17.after_ref = bf16[256,1024]{1,0:T(8,128)(2,1)S(1)} collective-permute-done((bf16[256,1024]{1,0:T(8,128)(2,1)S(1)}, bf16[256,1024]{1,0:T(8,128)(2,1)S(1)}, u32[]{:S(2)}, u32[]{:S(2)}) %collective-permute-start.17) | collective-permute-done | bytes 524320 | tf_op jit(solution)/shard_map/ppermute | solution.py:333
  71.9 0.0 copy-done.1
  71.9 11.3 %finish.1 = (f32[64,1024]{1,0:T(8,128)}, f32[64,4096]{1,0:T(8,128)}) custom-call(s32[128]{0:T(128)S(1)} %copy-done.2, s32[1]{0:T(128)S(6)} %copy.7.valid_ref, f32[4,72,128]{2,1,0:T(8,128)S(1)} %pad_maximum_fusion.own_ref, f32[4,72,128]{2,1,0:T(8,128)S(1)} %collective-permute-done.15.other_ref, f32[64,1024]{1,0:T(8,128)S(1)} %bitcast.26, ...), custom_call_target="tpu_custom_call" | custom-call | tf_op jit(solution)/shard_map/finish/pallas_call | solution.py:372
  (7 shorter events, 0.1 us)
Async XLA Ops:
  1.3 11.4 %copy-start = (f32[8,4096]{1,0:T(8,128)S(1)}, f32[8,4096]{1,0:T(8,128)}, u32[]{:S(2)}) copy-start(f32[8,4096]{1,0:T(8,128)} %scale_ref.1) | copy-start | bytes 393220
  1.3 11.4 %copy-start.2 = (s32[128]{0:T(128)S(1)}, s32[128]{0:T(128)}, u32[]{:S(2)}) copy-start(s32[128]{0:T(128)} %width_ref.5) | copy-start | bytes 1540
  3.7 68.2 %copy-start.1 = (f32[1024,64]{0,1:T(8,128)S(1)}, f32[1024,64]{0,1:T(8,128)}, u32[]{:S(2)}) copy-start(f32[1024,64]{0,1:T(8,128)} %param.9) | copy-start | bytes 786436
  3.7 20.1 %collective-permute-start = (f32[72,256]{1,0:T(8,128)S(1)}, f32[72,256]{1,0:T(8,128)S(1)}, u32[]{:S(2)}, u32[]{:S(2)}) collective-permute-start(f32[72,256]{1,0:T(8,128)S(1)} %get-tuple-element.15.forward_ref), channel_id=1, source_target_pairs={{0,1},{1,2},{2,3},{3,4},{4,5},{5,6},{6,7},{7,8},{8,9},{9,10},{10,1... | collective-permute-start | bytes 221192 | tf_op jit(solution)/shard_map/ppermute | solution.py:330
  7.6 16.1 %collective-permute-start.1 = (f32[64,256]{1,0:T(8,128)S(1)}, f32[64,256]{1,0:T(8,128)S(1)}, u32[]{:S(2)}, u32[]{:S(2)}) collective-permute-start(f32[64,256]{1,0:T(8,128)S(1)} %get-tuple-element.16.backward_ref), channel_id=1, source_target_pairs={{1,0},{2,1},{3,2},{4,3},{5,4},{6,5},{7,6},{8,7},{9,8},{10,9},{11,1... | collective-permute-start | bytes 196616 | tf_op jit(solution)/shard_map/ppermute | solution.py:331
  24.7 1.5 %collective-permute-start.2 = (f32[4,72,128]{2,1,0:T(8,128)S(1)}, f32[4,72,128]{2,1,0:T(8,128)S(1)}, u32[]{:S(2)}, u32[]{:S(2)}) collective-permute-start(f32[4,72,128]{2,1,0:T(8,128)S(1)} %dynamic-slice_bitcast_fusion), channel_id=1, source_target_pairs={{0,32},{1,33},{2,34},{3,35},{4,36},{5,37},{6,38},{7,39},{8,40},{9,... | collective-permute-start | bytes 442376 | tf_op jit(solution)/shard_map/ppermute | solution.py:257
  26.2 4.8 %collective-permute-start.3 = (f32[72,128]{1,0:T(8,128)S(1)}, f32[72,128]{1,0:T(8,128)S(1)}, u32[]{:S(2)}, u32[]{:S(2)}) collective-permute-start(f32[72,128]{1,0:T(8,128)S(1)} %get-tuple-element.20), channel_id=1, source_target_pairs={{0,2},{1,3},{2,0},{3,1},{4,6},{5,7},{6,4},{7,5},{8,10},{9,11},{10,... | collective-permute-start | bytes 110600 | tf_op jit(solution)/shard_map/ppermute | solution.py:257
  26.3 5.5 %collective-permute-start.4 = (f32[72,128]{1,0:T(8,128)S(1)}, f32[72,128]{1,0:T(8,128)S(1)}, u32[]{:S(2)}, u32[]{:S(2)}) collective-permute-start(f32[72,128]{1,0:T(8,128)S(1)} %get-tuple-element.22), channel_id=1, source_target_pairs={{0,4},{1,5},{2,6},{3,7},{4,0},{5,1},{6,2},{7,3},{8,12},{9,13},{10,... | collective-permute-start | bytes 110600 | tf_op jit(solution)/shard_map/ppermute | solution.py:257
  28.7 5.2 %collective-permute-start.5 = (f32[72,128]{1,0:T(8,128)S(1)}, f32[72,128]{1,0:T(8,128)S(1)}, u32[]{:S(2)}, u32[]{:S(2)}) collective-permute-start(f32[72,128]{1,0:T(8,128)S(1)} %get-tuple-element.21), channel_id=1, source_target_pairs={{0,6},{1,7},{2,4},{3,5},{4,2},{5,3},{6,0},{7,1},{8,14},{9,15},{10,... | collective-permute-start | bytes 110600 | tf_op jit(solution)/shard_map/ppermute | solution.py:257
  33.9 4.4 %collective-permute-start.6 = (f32[72,128]{1,0:T(8,128)S(1)}, f32[72,128]{1,0:T(8,128)S(1)}, u32[]{:S(2)}, u32[]{:S(2)}) collective-permute-start(f32[72,128]{1,0:T(8,128)S(1)} %fusion.1), channel_id=1, source_target_pairs={{0,8},{1,9},{2,10},{3,11},{4,12},{5,13},{6,14},{7,15},{8,0},{9,1},... | collective-permute-start | bytes 110600 | tf_op jit(solution)/shard_map/ppermute | solution.py:257
  34.5 5.5 %collective-permute-start.7 = (f32[72,128]{1,0:T(8,128)S(1)}, f32[72,128]{1,0:T(8,128)S(1)}, u32[]{:S(2)}, u32[]{:S(2)}) collective-permute-start(f32[72,128]{1,0:T(8,128)S(1)} %fusion.1), channel_id=1, source_target_pairs={{0,16},{1,17},{2,18},{3,19},{4,20},{5,21},{6,22},{7,23},{8,24},{9,... | collective-permute-start | bytes 110600 | tf_op jit(solution)/shard_map/ppermute | solution.py:257
  36.9 4.0 %collective-permute-start.8 = (f32[72,128]{1,0:T(8,128)S(1)}, f32[72,128]{1,0:T(8,128)S(1)}, u32[]{:S(2)}, u32[]{:S(2)}) collective-permute-start(f32[72,128]{1,0:T(8,128)S(1)} %fusion.1), channel_id=1, source_target_pairs={{0,24},{1,25},{2,26},{3,27},{4,28},{5,29},{6,30},{7,31},{8,16},{9,... | collective-permute-start | bytes 110600 | tf_op jit(solution)/shard_map/ppermute | solution.py:257
  40.9 14.0 %collective-permute-start.10 = (f32[72,128]{1,0:T(8,128)S(1)}, f32[72,128]{1,0:T(8,128)S(1)}, u32[]{:S(2)}, u32[]{:S(2)}) collective-permute-start(f32[72,128]{1,0:T(8,128)S(1)} %add_add_fusion.1), channel_id=1, source_target_pairs={{0,64},{1,65},{2,66},{3,67},{4,68},{5,69},{6,70},{7,71},{8,72},{9,... | collective-permute-start | bytes 110600 | tf_op jit(solution)/shard_map/ppermute | solution.py:257
  44.8 10.1 %collective-permute-start.11 = (f32[72,128]{1,0:T(8,128)S(1)}, f32[72,128]{1,0:T(8,128)S(1)}, u32[]{:S(2)}, u32[]{:S(2)}) collective-permute-start(f32[72,128]{1,0:T(8,128)S(1)} %add_add_fusion.1), channel_id=1, source_target_pairs={{0,65},{1,64},{2,67},{3,66},{4,69},{5,68},{6,71},{7,70},{8,73},{9,... | collective-permute-start | bytes 110600 | tf_op jit(solution)/shard_map/ppermute | solution.py:257
  44.8 10.1 %collective-permute-start.9 = (f32[72,128]{1,0:T(8,128)S(1)}, f32[72,128]{1,0:T(8,128)S(1)}, u32[]{:S(2)}, u32[]{:S(2)}) collective-permute-start(f32[72,128]{1,0:T(8,128)S(1)} %add_add_fusion.1), channel_id=1, source_target_pairs={{0,1},{1,0},{2,3},{3,2},{4,5},{5,4},{6,7},{7,6},{8,9},{9,8},{10,11... | collective-permute-start | bytes 110600 | tf_op jit(solution)/shard_map/ppermute | solution.py:257
  45.0 23.6 %collective-permute-start.16 = (bf16[256,1024]{1,0:T(8,128)(2,1)S(1)}, bf16[256,1024]{1,0:T(8,128)(2,1)S(1)}, u32[]{:S(2)}, u32[]{:S(2)}) collective-permute-start(bf16[256,1024]{1,0:T(8,128)(2,1)S(1)} %get-tuple-element.12.tail_ref), channel_id=1, source_target_pairs={{0,1},{1,2},{2,3},{3,4},{4,5},{5,6},{6,7},{7,8},{8,9},{9,10},{10,1... | collective-permute-start | bytes 1572872 | tf_op jit(solution)/shard_map/ppermute | solution.py:332
  48.8 23.1 %collective-permute-start.17 = (bf16[256,1024]{1,0:T(8,128)(2,1)S(1)}, bf16[256,1024]{1,0:T(8,128)(2,1)S(1)}, u32[]{:S(2)}, u32[]{:S(2)}) collective-permute-start(bf16[256,1024]{1,0:T(8,128)(2,1)S(1)} %get-tuple-element.11.head_ref), channel_id=1, source_target_pairs={{1,0},{2,1},{3,2},{4,3},{5,4},{6,5},{7,6},{8,7},{9,8},{10,9},{11,1... | collective-permute-start | bytes 1572872 | tf_op jit(solution)/shard_map/ppermute | solution.py:333
  55.0 5.5 %collective-permute-start.13 = (f32[72,128]{1,0:T(8,128)S(1)}, f32[72,128]{1,0:T(8,128)S(1)}, u32[]{:S(2)}, u32[]{:S(2)}) collective-permute-start(f32[72,128]{1,0:T(8,128)S(1)} %add_add_fusion), channel_id=1, source_target_pairs={{0,4},{1,5},{2,6},{3,7},{4,0},{5,1},{6,2},{7,3},{8,12},{9,13},{10,... | collective-permute-start | bytes 110600 | tf_op jit(solution)/shard_map/ppermute | solution.py:257
  56.7 7.4 %collective-permute-start.14 = (f32[72,128]{1,0:T(8,128)S(1)}, f32[72,128]{1,0:T(8,128)S(1)}, u32[]{:S(2)}, u32[]{:S(2)}) collective-permute-start(f32[72,128]{1,0:T(8,128)S(1)} %add_add_fusion), channel_id=1, source_target_pairs={{0,6},{1,7},{2,4},{3,5},{4,2},{5,3},{6,0},{7,1},{8,14},{9,15},{10,... | collective-permute-start | bytes 110600 | tf_op jit(solution)/shard_map/ppermute | solution.py:257
  58.7 5.4 %collective-permute-start.12 = (f32[72,128]{1,0:T(8,128)S(1)}, f32[72,128]{1,0:T(8,128)S(1)}, u32[]{:S(2)}, u32[]{:S(2)}) collective-permute-start(f32[72,128]{1,0:T(8,128)S(1)} %add_add_fusion), channel_id=1, source_target_pairs={{0,2},{1,3},{2,0},{3,1},{4,6},{5,7},{6,4},{7,5},{8,10},{9,11},{10,... | collective-permute-start | bytes 110600 | tf_op jit(solution)/shard_map/ppermute | solution.py:257
  64.1 1.5 %collective-permute-start.15 = (f32[4,72,128]{2,1,0:T(8,128)S(1)}, f32[4,72,128]{2,1,0:T(8,128)S(1)}, u32[]{:S(2)}, u32[]{:S(2)}) collective-permute-start(f32[4,72,128]{2,1,0:T(8,128)S(1)} %pad_maximum_fusion.own_ref), channel_id=1, source_target_pairs={{0,32},{1,33},{2,34},{3,35},{4,36},{5,37},{6,38},{7,39},{8,40},{9,... | collective-permute-start | bytes 442376 | tf_op jit(solution)/shard_map/ppermute | solution.py:257

commit v4 on v3

--- a/solution.py
+++ b/solution.py
@@ -174,21 +174,15 @@
     return jnp.concatenate(done, 0)[:, size:]
 
 
-def finish_kernel(width_ref, valid_ref, own_ref, other_ref, prior_ref, before_ref, after_ref, token_ref,
-                  basis_ref, out_ref, held_ref, value_ref, in_sem, out_sem, *, tok_rows, n_tile):
-    steps = tok_rows // STEP
-    chunks = [pl.ds(step * STEP, STEP) for step in range(steps)]
+def basis_kernel(own_ref, other_ref, prior_ref, head_ref, tail_ref, far_ref,
+                 basis_ref, pair_ref, shift_ref, head_out_ref, tail_out_ref, token_ref, sem):
+    size = token_ref.shape[0] // sem.shape[0]
     arrive = [
-        pltpu.make_async_copy(token_ref.at[rows], held_ref.at[rows], in_sem.at[step])
-        for step, rows in enumerate(chunks)
-    ]
-    leave = [
-        pltpu.make_async_copy(value_ref.at[:, rows], out_ref.at[:, rows], out_sem.at[step])
-        for step, rows in enumerate(chunks)
+        pltpu.make_async_copy(far_ref.at[pl.ds(i * size, size)], token_ref.at[pl.ds(i * size, size)], sem.at[i])
+        for i in range(sem.shape[0])
     ]
     for copy in arrive:
         copy.start()
-    left, right = widths(width_ref, n_tile)
     core = lax.rem(lax.axis_index("region"), 2)
     y = lax.rem(lax.div(lax.axis_index("tile"), 2), 4)
     keep = prior_ref.shape[0]
@@ -208,32 +202,51 @@
     high = basis.astype(BF16)
     low = (basis - high.astype(F32)).astype(BF16)
     pair = jnp.concatenate([high, low], 0).T
-    shift = jnp.sum(basis * average, axis=1, keepdims=True)
-
-    def project(rows):
-        wide = lax.dot_general(rows, pair, NN, preferred_element_type=F32).T
-        return wide[:keep] + wide[keep:]
-
-    before = pltpu.roll(project(before_ref[...]), lax.rem(left, BAND), 1)
-    after = pltpu.roll(project(after_ref[...]), lax.rem(BAND - right, BAND), 1)
-    near = lax.broadcasted_iota(jnp.int32, (1, BAND), 1)
+    pair_ref[...] = pair
+    shift_ref[...] = jnp.broadcast_to(jnp.sum(basis * average, axis=1, keepdims=True), shift_ref.shape)
+    for rows, out in ((head_ref, head_out_ref), (tail_ref, tail_out_ref)):
+        wide = lax.dot_general(rows[...], pair, NN, preferred_element_type=F32).T
+        out[...] = wide[:keep] + wide[keep:]
+    for copy in arrive:
+        copy.wait()
+
+
+def project_kernel(valid_ref, token_ref, pair_ref, shift_ref, out_ref, value_ref, out_sem, *, tok_rows):
+    keep = shift_ref.shape[0]
+    steps = tok_rows // STEP
+    leave = []
     for step in range(steps):
-        arrive[step].wait()
-        value = project(held_ref[chunks[step], :])
-        if step == 0:
-            head = jnp.where(near < left, (value[:, :BAND] + before) * 0.5, value[:, :BAND])
-            value = jnp.concatenate([head, value[:, BAND:]], 1)
-        if step == steps - 1:
-            edge = STEP - BAND
-            tail = jnp.where(near >= BAND - right, (value[:, edge:] + after) * 0.5, value[:, edge:])
-            value = jnp.concatenate([value[:, :edge], tail], 1)
+        rows = pl.ds(step * STEP, STEP)
+        wide = lax.dot_general(token_ref[rows, :], pair_ref[...], NN, preferred_element_type=F32).T
         place = step * STEP + lax.broadcasted_iota(jnp.int32, (1, STEP), 1)
-        value_ref[:, chunks[step]] = jnp.where(place < valid_ref[0], value - shift, 0.0)
+        value = wide[:keep] + wide[keep:] - shift_ref[:, :1]
+        value_ref[:, rows] = jnp.where(place < valid_ref[0], value, 0.0)
+        leave.append(pltpu.make_async_copy(value_ref.at[:, rows], out_ref.at[:, rows], out_sem.at[step]))
         if step > 0:
             leave[step - 1].start()
     leave[steps - 1].start()
     for copy in leave:
         copy.wait()
+
+
+def blend_kernel(width_ref, valid_ref, head_ref, tail_ref, before_ref, after_ref, shift_ref,
+                 whole_ref, out_ref, buffer_ref, sem_ref, *, tok_rows, n_tile):
+    left, right = widths(width_ref, n_tile)
+    place = lax.broadcasted_iota(jnp.int32, (1, BAND), 1)
+    shift = shift_ref[:, :1]
+    before = pltpu.roll(before_ref[...], lax.rem(left, BAND), 1)
+    after = pltpu.roll(after_ref[...], lax.rem(BAND - right, BAND), 1)
+    head = jnp.where(place < left, (head_ref[...] + before) * 0.5, head_ref[...]) - shift
+    tail = jnp.where(place >= BAND - right, (tail_ref[...] + after) * 0.5, tail_ref[...]) - shift
+    start = tok_rows - BAND
+    buffer_ref[0] = jnp.where(place < valid_ref[0], head, 0.0)
+    buffer_ref[1] = jnp.where(start + place < valid_ref[0], tail, 0.0)
+    first = pltpu.make_async_copy(buffer_ref.at[0], out_ref.at[:, pl.ds(0, BAND)], sem_ref.at[0])
+    second = pltpu.make_async_copy(buffer_ref.at[1], out_ref.at[:, pl.ds(start, BAND)], sem_ref.at[1])
+    first.start()
+    second.start()
+    first.wait()
+    second.wait()
 
 
 def smem():
@@ -295,7 +308,7 @@
     def whole(*shape):
         return pl.BlockSpec(shape, lambda i: (0,) * len(shape))
 
-    quantized = pltpu.with_memory_space_constraint(quantized, pltpu.HBM)
+    quant_far = pltpu.with_memory_space_constraint(quantized, pltpu.HBM)
     prior = prior_basis.T
     prior_far = pltpu.with_memory_space_constraint(prior, pltpu.HBM)
     scales_far = pltpu.with_memory_space_constraint(block_scales, pltpu.HBM)
@@ -326,11 +339,9 @@
         ],
         compiler_params=params(24),
         name="band",
-    )(valid_count, quantized, quantized, scales_far, scales_far, prior_far)
+    )(valid_count, quant_far, quant_far, scales_far, scales_far, prior_far)
     before = lax.ppermute(forward, "tile", forward_pairs)
     after = lax.ppermute(backward, "tile", backward_pairs)
-    before_rows = lax.ppermute(tail_tokens, "tile", forward_pairs)
-    after_rows = lax.ppermute(head_tokens, "tile", backward_pairs)
     bulk = pl.pallas_call(
         functools.partial(bulk_kernel, tok_rows=tok_rows, n_tile=n_tile),
         in_specs=[smem(), smem(), far(), near(), near()],
@@ -345,10 +356,10 @@
             pltpu.SemaphoreType.DMA((steps,)),
             pltpu.SemaphoreType.DMA((steps,)),
         ],
-        compiler_params=params(40),
+        compiler_params=params(32),
         name="bulk",
     )
-    tokens, sums = bulk(band_width, valid_count, quantized, block_scales, prior3)
+    tokens, sums = bulk(band_width, valid_count, quant_far, block_scales, prior3)
     pieces = pl.pallas_call(
         functools.partial(join_kernel, tok_rows=tok_rows, n_tile=n_tile),
         grid=(1,),
@@ -369,32 +380,45 @@
         name="join",
     )(band_width, valid_count, head_tokens, tail_tokens, sums, forward, backward, before, after)
     own, other = reduce_all(pieces)
-    basis, projected = pl.pallas_call(
-        functools.partial(finish_kernel, tok_rows=tok_rows, n_tile=n_tile),
-        in_specs=[smem(), smem()] + [near()] * 5 + [far()],
-        out_specs=[near(), far()],
+    basis, pair, shift, head, tail, tokens = pl.pallas_call(
+        basis_kernel,
+        in_specs=[near()] * 5 + [far()],
+        out_specs=[near()] * 6,
         out_shape=[
             jax.ShapeDtypeStruct((keep, feat_dim), F32),
-            pltpu.HBM((keep, tok_rows), F32),
-        ],
-        scratch_shapes=[
-            pltpu.VMEM((tok_rows, feat_dim), BF16),
-            pltpu.VMEM((keep, tok_rows), F32),
-            pltpu.SemaphoreType.DMA((steps,)),
-            pltpu.SemaphoreType.DMA((steps,)),
-        ],
-        compiler_params=params(32),
-        name="finish",
-    )(
-        band_width,
-        valid_count,
-        own,
-        other,
-        prior,
-        before_rows,
-        after_rows,
-        pltpu.with_memory_space_constraint(tokens, pltpu.HBM),
-    )
+            jax.ShapeDtypeStruct((feat_dim, 2 * keep), BF16),
+            jax.ShapeDtypeStruct((keep, 128), F32),
+            jax.ShapeDtypeStruct((keep, BAND), F32),
+            jax.ShapeDtypeStruct((keep, BAND), F32),
+            jax.ShapeDtypeStruct((tok_rows, feat_dim), BF16),
+        ],
+        scratch_shapes=[pltpu.SemaphoreType.DMA((8,))],
+        compiler_params=params(24),
+        name="basis",
+    )(own, other, prior, head_tokens, tail_tokens, pltpu.with_memory_space_constraint(tokens, pltpu.HBM))
+    before = lax.ppermute(tail, "tile", forward_pairs)
+    after = lax.ppermute(head, "tile", backward_pairs)
+    raw = pl.pallas_call(
+        functools.partial(project_kernel, tok_rows=tok_rows),
+        in_specs=[smem(), near(), near(), near()],
+        out_specs=far(),
+        out_shape=pltpu.HBM((keep, tok_rows), F32),
+        scratch_shapes=[pltpu.VMEM((keep, tok_rows), F32), pltpu.SemaphoreType.DMA((steps,))],
+        compiler_params=params(20),
+        name="project",
+    )(valid_count, tokens, pair, shift)
+    projected = pl.pallas_call(
+        functools.partial(blend_kernel, tok_rows=tok_rows, n_tile=n_tile),
+        in_specs=[smem(), smem()]
+        + [pl.BlockSpec(memory_space=pltpu.VMEM)] * 5
+        + [pl.BlockSpec(memory_space=pl.ANY)],
+        out_specs=pl.BlockSpec(memory_space=pl.ANY),
+        out_shape=jax.ShapeDtypeStruct((keep, tok_rows), F32),
+        scratch_shapes=[pltpu.VMEM((2, keep, BAND), F32), pltpu.SemaphoreType.DMA((2,))],
+        input_output_aliases={7: 0},
+        compiler_params=params(8),
+        name="blend",
+    )(band_width, valid_count, head, tail, before, after, shift, raw)
     return projected, basis.T
 
 

time: 83.6 us -> 80.5 us (0.963)
  starting transfers between devices: 35.2 us -> 33.4 us
  waiting for transfers between devices: 20.7 us -> 19.6 us
    ppermute x2, waiting for transfers between devices: 6.36 us -> 3.91 us  [the longest x1 3.91 us: per_device(): before = lax.ppermute(tail, 'tile', forward_pairs)]
    ppermute x2, starting transfers between devices: 9.94 us -> 7.53 us  [the longest x1 5.61 us: per_device(): after = lax.ppermute(head, 'tile', backward_pairs)]
    ppermute x14, waiting for transfers between devices: 14.3 us -> 15.7 us  [flip(): return lax.ppermute(value, AXES, pairs)]
    pallas_call x2 -> x4, Pallas kernels: 22.4 us -> 22.2 us  [the longest x1 11 us: per_device(): bulk(band_width, valid_count, quant_far, block_scales, prior3)]
  transfers between devices with their start and end apart: 18 -> 18, of which waited for: 11 -> 12; matrix products, arithmetic and copies ran while one was open for 0% -> 0% of each run, Pallas kernels for 13% -> 18%
where the time goes in v4:
time: 80.5 us; the launch traced here: 80.3 us
  starting transfers between devices  33.4 us (41%)
  Pallas kernels  25.5 us (32%)
  waiting for transfers between devices  19.6 us (24%)
  between operations  1.71 us (2%)
    ppermute x14, starting transfers between devices, flip(): return lax.ppermute(value, AXES, pairs)  16.9 us
    ppermute x14, waiting for transfers between devices, flip(): return lax.ppermute(value, AXES, pairs)  15.7 us
    pallas_call x1, Pallas kernels, per_device(): bulk(band_width, valid_count, quant_far, block_scales, prior3)  11 us
    pallas_call x1, Pallas kernels, per_device(): pl.pallas_call(basis_kernel, in_specs=[near()] * 5 + [far()], out_specs=[...  6.57 us
    ppermute x1, starting transfers between devices, per_device(): after = lax.ppermute(head, 'tile', backward_pairs)  5.61 us
    ppermute x1, starting transfers between devices, per_device(): after = lax.ppermute(backward, 'tile', backward_pairs)  5.02 us
    ppermute x1, starting transfers between devices, per_device(): before = lax.ppermute(forward, 'tile', forward_pairs)  3.96 us
    ppermute x1, waiting for transfers between devices, per_device(): before = lax.ppermute(tail, 'tile', forward_pairs)  3.91 us
  transfers between devices with their start and end apart: 18, of which 12 were waited for; matrix products, arithmetic and copies ran while one was open for 0% of the time, Pallas kernels for 18%

profile of v4, /device:TPU:2, one launch (start us, length us, event | category | flops | bytes accessed | tf_op | source)
XLA Modules:
  0.0 80.3 jit_solution(12900219033257545483)
XLA Ops:
  1.3 0.0 copy-start
  1.3 0.0 copy-start.2
  1.3 2.4 %band.1 = (f32[72,256]{1,0:T(8,128)S(1)}, f32[64,256]{1,0:T(8,128)S(1)}, bf16[1024,256]{1,0:T(8,128)(2,1)S(1)}, bf16[256,1024]{1,0:T(8,128)(2,1)S(1)}, bf16[256,1024]{1,0:T(8,128)(2,1)S(1)}) custom-call(s32[1]{0:T(128)S(6)} %copy.9.valid_ref, bf16[4096,1024]{1,0:T(8,128)(2,1)} %quant_ref.1, bf16[4096,1024]{1,0:T(8,128)(2,1)} %quant_ref.1, ...), custom_call_target="tpu_custom_call" | custom-call | tf_op jit(solution)/shard_map/band/pallas_call | solution.py:315
  3.7 0.0 copy-start.1
  3.7 4.0 %collective-permute-start = (f32[72,256]{1,0:T(8,128)S(1)}, f32[72,256]{1,0:T(8,128)S(1)}, u32[]{:S(2)}, u32[]{:S(2)}) collective-permute-start(f32[72,256]{1,0:T(8,128)S(1)} %get-tuple-element.19.forward_ref), channel_id=1, source_target_pairs={{0,1},{1,2},{2,3},{3,4},{4,5},{5,6},{6,7},{7,8},{8,9},{9,10},{10,1... | collective-permute-start | bytes 221192 | tf_op jit(solution)/shard_map/ppermute | solution.py:343
  7.6 5.0 %collective-permute-start.1 = (f32[64,256]{1,0:T(8,128)S(1)}, f32[64,256]{1,0:T(8,128)S(1)}, u32[]{:S(2)}, u32[]{:S(2)}) collective-permute-start(f32[64,256]{1,0:T(8,128)S(1)} %get-tuple-element.20.backward_ref), channel_id=1, source_target_pairs={{1,0},{2,1},{3,2},{4,3},{5,4},{6,5},{7,6},{8,7},{9,8},{10,9},{11,1... | collective-permute-start | bytes 196616 | tf_op jit(solution)/shard_map/ppermute | solution.py:344
  12.7 0.0 copy-done
  12.7 0.0 copy-done.2
  12.7 11.0 %bulk.1 = (bf16[4096,1024]{1,0:T(8,128)(2,1)}, f32[144,1024]{1,0:T(8,128)S(1)}) custom-call(s32[128]{0:T(128)S(1)} %copy-done.2, s32[1]{0:T(128)S(6)} %copy.9.valid_ref, bf16[4096,1024]{1,0:T(8,128)(2,1)} %quant_ref.1, f32[8,4096]{1,0:T(8,128)S(1)} %copy-done, bf16[1024,256]{1,0:T(8,128)(2,1)S(1)} %get-tuple-element.17.prior3_ref), custom_call_target="tpu_custom_call" | custom-call | tf_op jit(solution)/shard_map/bulk/pallas_call | solution.py:362
  23.7 0.0 collective-permute-done.1.after_ref
  23.8 0.0 collective-permute-done.before_ref
  23.8 0.9 %join.1 = f32[8,72,128]{2,1,0:T(8,128)S(1)} custom-call(s32[128]{0:T(128)S(1)} %copy-done.2, s32[1]{0:T(128)S(6)} %copy.9.valid_ref, bf16[256,1024]{1,0:T(8,128)(2,1)S(1)} %get-tuple-element.15.head_ref, bf16[256,1024]{1,0:T(8,128)(2,1)S(1)} %get-tuple-element.16.tail_ref, f32[144,1024]{1,0:T(8,128)S(1)} %get-tuple-element.18.sum_ref, ...), custom_call_target="tpu_custom_call" | custom-call | tf_op jit(solution)/shard_map/join/pallas_call | solution.py:363
  24.7 0.1 collective-permute-start.2
  24.9 1.3 %collective-permute-done.2 = f32[4,72,128]{2,1,0:T(8,128)S(1)} collective-permute-done((f32[4,72,128]{2,1,0:T(8,128)S(1)}, f32[4,72,128]{2,1,0:T(8,128)S(1)}, u32[]{:S(2)}, u32[]{:S(2)}) %collective-permute-start.2) | collective-permute-done | bytes 147488 | tf_op jit(solution)/shard_map/ppermute | solution.py:270
  26.2 0.1 collective-permute-start.3
  26.3 1.6 %collective-permute-start.5 = (f32[72,128]{1,0:T(8,128)S(1)}, f32[72,128]{1,0:T(8,128)S(1)}, u32[]{:S(2)}, u32[]{:S(2)}) collective-permute-start(f32[72,128]{1,0:T(8,128)S(1)} %get-tuple-element.29), channel_id=1, source_target_pairs={{0,6},{1,7},{2,4},{3,5},{4,2},{5,3},{6,0},{7,1},{8,14},{9,15},{10,... | collective-permute-start | bytes 110600 | tf_op jit(solution)/shard_map/ppermute | solution.py:270
  28.0 2.5 %collective-permute-start.4 = (f32[72,128]{1,0:T(8,128)S(1)}, f32[72,128]{1,0:T(8,128)S(1)}, u32[]{:S(2)}, u32[]{:S(2)}) collective-permute-start(f32[72,128]{1,0:T(8,128)S(1)} %get-tuple-element.30), channel_id=1, source_target_pairs={{0,4},{1,5},{2,6},{3,7},{4,0},{5,1},{6,2},{7,3},{8,12},{9,13},{10,... | collective-permute-start | bytes 110600 | tf_op jit(solution)/shard_map/ppermute | solution.py:270
  30.4 0.0 collective-permute-done.3
  30.4 1.2 %collective-permute-done.5 = f32[72,128]{1,0:T(8,128)S(1)} collective-permute-done((f32[72,128]{1,0:T(8,128)S(1)}, f32[72,128]{1,0:T(8,128)S(1)}, u32[]{:S(2)}, u32[]{:S(2)}) %collective-permute-start.5) | collective-permute-done | bytes 36896 | tf_op jit(solution)/shard_map/ppermute | solution.py:270
  31.6 1.8 %collective-permute-done.4 = f32[72,128]{1,0:T(8,128)S(1)} collective-permute-done((f32[72,128]{1,0:T(8,128)S(1)}, f32[72,128]{1,0:T(8,128)S(1)}, u32[]{:S(2)}, u32[]{:S(2)}) %collective-permute-start.4) | collective-permute-done | bytes 36896 | tf_op jit(solution)/shard_map/ppermute | solution.py:270
  33.4 1.6 %collective-permute-start.8 = (f32[72,128]{1,0:T(8,128)S(1)}, f32[72,128]{1,0:T(8,128)S(1)}, u32[]{:S(2)}, u32[]{:S(2)}) collective-permute-start(f32[72,128]{1,0:T(8,128)S(1)} %fusion.1), channel_id=1, source_target_pairs={{0,24},{1,25},{2,26},{3,27},{4,28},{5,29},{6,30},{7,31},{8,16},{9,... | collective-permute-start | bytes 110600 | tf_op jit(solution)/shard_map/ppermute | solution.py:270
  35.0 1.1 %collective-permute-start.7 = (f32[72,128]{1,0:T(8,128)S(1)}, f32[72,128]{1,0:T(8,128)S(1)}, u32[]{:S(2)}, u32[]{:S(2)}) collective-permute-start(f32[72,128]{1,0:T(8,128)S(1)} %fusion.1), channel_id=1, source_target_pairs={{0,16},{1,17},{2,18},{3,19},{4,20},{5,21},{6,22},{7,23},{8,24},{9,... | collective-permute-start | bytes 110600 | tf_op jit(solution)/shard_map/ppermute | solution.py:270
  36.1 1.5 %collective-permute-start.6 = (f32[72,128]{1,0:T(8,128)S(1)}, f32[72,128]{1,0:T(8,128)S(1)}, u32[]{:S(2)}, u32[]{:S(2)}) collective-permute-start(f32[72,128]{1,0:T(8,128)S(1)} %fusion.1), channel_id=1, source_target_pairs={{0,8},{1,9},{2,10},{3,11},{4,12},{5,13},{6,14},{7,15},{8,0},{9,1},... | collective-permute-start | bytes 110600 | tf_op jit(solution)/shard_map/ppermute | solution.py:270
  37.6 0.3 collective-permute-done.8
  37.9 2.6 %collective-permute-done.7 = f32[72,128]{1,0:T(8,128)S(1)} collective-permute-done((f32[72,128]{1,0:T(8,128)S(1)}, f32[72,128]{1,0:T(8,128)S(1)}, u32[]{:S(2)}, u32[]{:S(2)}) %collective-permute-start.7) | collective-permute-done | bytes 36896 | tf_op jit(solution)/shard_map/ppermute | solution.py:270
  40.5 0.0 collective-permute-done.6
  40.5 3.2 %collective-permute-start.11 = (f32[72,128]{1,0:T(8,128)S(1)}, f32[72,128]{1,0:T(8,128)S(1)}, u32[]{:S(2)}, u32[]{:S(2)}) collective-permute-start(f32[72,128]{1,0:T(8,128)S(1)} %add_add_fusion.1), channel_id=1, source_target_pairs={{0,65},{1,64},{2,67},{3,66},{4,69},{5,68},{6,71},{7,70},{8,73},{9,... | collective-permute-start | bytes 110600 | tf_op jit(solution)/shard_map/ppermute | solution.py:270
  43.7 0.8 %collective-permute-start.10 = (f32[72,128]{1,0:T(8,128)S(1)}, f32[72,128]{1,0:T(8,128)S(1)}, u32[]{:S(2)}, u32[]{:S(2)}) collective-permute-start(f32[72,128]{1,0:T(8,128)S(1)} %add_add_fusion.1), channel_id=1, source_target_pairs={{0,64},{1,65},{2,66},{3,67},{4,68},{5,69},{6,70},{7,71},{8,72},{9,... | collective-permute-start | bytes 110600 | tf_op jit(solution)/shard_map/ppermute | solution.py:270
  44.5 0.1 collective-permute-start.9
  44.7 1.1 %collective-permute-done.11 = f32[72,128]{1,0:T(8,128)S(1)} collective-permute-done((f32[72,128]{1,0:T(8,128)S(1)}, f32[72,128]{1,0:T(8,128)S(1)}, u32[]{:S(2)}, u32[]{:S(2)}) %collective-permute-start.11) | collective-permute-done | bytes 36896 | tf_op jit(solution)/shard_map/ppermute | solution.py:270
  45.7 3.4 %collective-permute-done.10 = f32[72,128]{1,0:T(8,128)S(1)} collective-permute-done((f32[72,128]{1,0:T(8,128)S(1)}, f32[72,128]{1,0:T(8,128)S(1)}, u32[]{:S(2)}, u32[]{:S(2)}) %collective-permute-start.10) | collective-permute-done | bytes 36896 | tf_op jit(solution)/shard_map/ppermute | solution.py:270
  49.2 0.0 collective-permute-done.9
  49.2 1.1 %collective-permute-start.14 = (f32[72,128]{1,0:T(8,128)S(1)}, f32[72,128]{1,0:T(8,128)S(1)}, u32[]{:S(2)}, u32[]{:S(2)}) collective-permute-start(f32[72,128]{1,0:T(8,128)S(1)} %add_add_fusion), channel_id=1, source_target_pairs={{0,6},{1,7},{2,4},{3,5},{4,2},{5,3},{6,0},{7,1},{8,14},{9,15},{10,... | collective-permute-start | bytes 110600 | tf_op jit(solution)/shard_map/ppermute | solution.py:270
  50.3 1.7 %collective-permute-start.13 = (f32[72,128]{1,0:T(8,128)S(1)}, f32[72,128]{1,0:T(8,128)S(1)}, u32[]{:S(2)}, u32[]{:S(2)}) collective-permute-start(f32[72,128]{1,0:T(8,128)S(1)} %add_add_fusion), channel_id=1, source_target_pairs={{0,4},{1,5},{2,6},{3,7},{4,0},{5,1},{6,2},{7,3},{8,12},{9,13},{10,... | collective-permute-start | bytes 110600 | tf_op jit(solution)/shard_map/ppermute | solution.py:270
  52.0 1.3 %collective-permute-start.12 = (f32[72,128]{1,0:T(8,128)S(1)}, f32[72,128]{1,0:T(8,128)S(1)}, u32[]{:S(2)}, u32[]{:S(2)}) collective-permute-start(f32[72,128]{1,0:T(8,128)S(1)} %add_add_fusion), channel_id=1, source_target_pairs={{0,2},{1,3},{2,0},{3,1},{4,6},{5,7},{6,4},{7,5},{8,10},{9,11},{10,... | collective-permute-start | bytes 110600 | tf_op jit(solution)/shard_map/ppermute | solution.py:270
  53.4 1.1 %collective-permute-done.14 = f32[72,128]{1,0:T(8,128)S(1)} collective-permute-done((f32[72,128]{1,0:T(8,128)S(1)}, f32[72,128]{1,0:T(8,128)S(1)}, u32[]{:S(2)}, u32[]{:S(2)}) %collective-permute-start.14) | collective-permute-done | bytes 36896 | tf_op jit(solution)/shard_map/ppermute | solution.py:270
  54.4 1.3 %collective-permute-done.13 = f32[72,128]{1,0:T(8,128)S(1)} collective-permute-done((f32[72,128]{1,0:T(8,128)S(1)}, f32[72,128]{1,0:T(8,128)S(1)}, u32[]{:S(2)}, u32[]{:S(2)}) %collective-permute-start.13) | collective-permute-done | bytes 36896 | tf_op jit(solution)/shard_map/ppermute | solution.py:270
  55.8 0.2 collective-permute-done.12
  56.0 0.1 collective-permute-start.15
  56.1 1.4 %collective-permute-done.15.other_ref = f32[4,72,128]{2,1,0:T(8,128)S(1)} collective-permute-done((f32[4,72,128]{2,1,0:T(8,128)S(1)}, f32[4,72,128]{2,1,0:T(8,128)S(1)}, u32[]{:S(2)}, u32[]{:S(2)}) %collective-permute-start.15) | collective-permute-done | bytes 147488 | tf_op jit(solution)/shard_map/ppermute | solution.py:270
  57.4 0.0 copy-done.1
  57.4 6.6 %basis.1 = (f32[64,1024]{1,0:T(8,128)}, bf16[1024,128]{1,0:T(8,128)(2,1)S(1)}, f32[64,128]{1,0:T(8,128)S(1)}, f32[64,256]{1,0:T(8,128)S(1)}, f32[64,256]{1,0:T(8,128)S(1)}, /*index=5*/bf16[4096,1024]{1,0:T(8,128)(2,1)S(1)}) custom-call(f32[4,72,128]{2,1,0:T(8,128)S(1)} %pad_maximum_fusion.own_ref, f32[4,72,128]{2,1,0:T(8,128)S(1)} %collective-permute-done.15.other_ref, ...), custom_call_target="tpu_custom_call" | custom-call | tf_op jit(solution)/shard_map/basis/pallas_call | solution.py:383
  64.0 5.6 %collective-permute-start.17 = (f32[64,256]{1,0:T(8,128)S(1)}, f32[64,256]{1,0:T(8,128)S(1)}, u32[]{:S(2)}, u32[]{:S(2)}) collective-permute-start(f32[64,256]{1,0:T(8,128)S(1)} %get-tuple-element.22.head_ref), channel_id=1, source_target_pairs={{1,0},{2,1},{3,2},{4,3},{5,4},{6,5},{7,6},{8,7},{9,8},{10,9},{11,1... | collective-permute-start | bytes 196616 | tf_op jit(solution)/shard_map/ppermute | solution.py:400
  69.6 1.9 %collective-permute-start.16 = (f32[64,256]{1,0:T(8,128)S(1)}, f32[64,256]{1,0:T(8,128)S(1)}, u32[]{:S(2)}, u32[]{:S(2)}) collective-permute-start(f32[64,256]{1,0:T(8,128)S(1)} %get-tuple-element.23.tail_ref), channel_id=1, source_target_pairs={{0,1},{1,2},{2,3},{3,4},{4,5},{5,6},{6,7},{7,8},{8,9},{9,10},{10,1... | collective-permute-start | bytes 196616 | tf_op jit(solution)/shard_map/ppermute | solution.py:399
  71.6 3.3 %project.1.whole_ref = f32[64,4096]{1,0:T(8,128)} custom-call(s32[1]{0:T(128)S(6)} %copy.9.valid_ref, bf16[4096,1024]{1,0:T(8,128)(2,1)S(1)} %get-tuple-element.25.token_ref, bf16[1024,128]{1,0:T(8,128)(2,1)S(1)} %get-tuple-element.26.pair_ref, f32[64,128]{1,0:T(8,128)S(1)} %get-tuple-element.24.shift_ref), custom_call_target="tpu_custom_call" | custom-call | tf_op jit(solution)/shard_map/project/pallas_call | solution.py:401
  74.9 0.0 collective-permute-done.17.after_ref
  74.9 3.9 %collective-permute-done.16.before_ref = f32[64,256]{1,0:T(8,128)S(1)} collective-permute-done((f32[64,256]{1,0:T(8,128)S(1)}, f32[64,256]{1,0:T(8,128)S(1)}, u32[]{:S(2)}, u32[]{:S(2)}) %collective-permute-start.16) | collective-permute-done | bytes 65568 | tf_op jit(solution)/shard_map/ppermute | solution.py:399
  78.8 1.3 %blend.1 = f32[64,4096]{1,0:T(8,128)} custom-call(s32[128]{0:T(128)S(1)} %copy-done.2, s32[1]{0:T(128)S(6)} %copy.9.valid_ref, f32[64,256]{1,0:T(8,128)S(1)} %get-tuple-element.22.head_ref, f32[64,256]{1,0:T(8,128)S(1)} %get-tuple-element.23.tail_ref, f32[64,256]{1,0:T(8,128)S(1)} %collective-permute-done.16.before_ref, ...), custom_call_target="tpu_custom_call", output_to_operand_aliasing={{}: (7, {})} | custom-call | tf_op jit(solution)/shard_map/blend/pallas_call | solution.py:410
  (7 shorter events, 0.1 us)
Async XLA Ops:
  1.3 11.4 %copy-start = (f32[8,4096]{1,0:T(8,128)S(1)}, f32[8,4096]{1,0:T(8,128)}, u32[]{:S(2)}) copy-start(f32[8,4096]{1,0:T(8,128)} %scale_ref.1) | copy-start | bytes 393220
  1.3 11.4 %copy-start.2 = (s32[128]{0:T(128)S(1)}, s32[128]{0:T(128)}, u32[]{:S(2)}) copy-start(s32[128]{0:T(128)} %width_ref.5) | copy-start | bytes 1540
  3.7 53.8 %copy-start.1 = (f32[1024,64]{0,1:T(8,128)S(1)}, f32[1024,64]{0,1:T(8,128)}, u32[]{:S(2)}) copy-start(f32[1024,64]{0,1:T(8,128)} %param.9) | copy-start | bytes 786436
  3.7 20.1 %collective-permute-start = (f32[72,256]{1,0:T(8,128)S(1)}, f32[72,256]{1,0:T(8,128)S(1)}, u32[]{:S(2)}, u32[]{:S(2)}) collective-permute-start(f32[72,256]{1,0:T(8,128)S(1)} %get-tuple-element.19.forward_ref), channel_id=1, source_target_pairs={{0,1},{1,2},{2,3},{3,4},{4,5},{5,6},{6,7},{7,8},{8,9},{9,10},{10,1... | collective-permute-start | bytes 221192 | tf_op jit(solution)/shard_map/ppermute | solution.py:343
  7.6 16.1 %collective-permute-start.1 = (f32[64,256]{1,0:T(8,128)S(1)}, f32[64,256]{1,0:T(8,128)S(1)}, u32[]{:S(2)}, u32[]{:S(2)}) collective-permute-start(f32[64,256]{1,0:T(8,128)S(1)} %get-tuple-element.20.backward_ref), channel_id=1, source_target_pairs={{1,0},{2,1},{3,2},{4,3},{5,4},{6,5},{7,6},{8,7},{9,8},{10,9},{11,1... | collective-permute-start | bytes 196616 | tf_op jit(solution)/shard_map/ppermute | solution.py:344
  24.7 1.5 %collective-permute-start.2 = (f32[4,72,128]{2,1,0:T(8,128)S(1)}, f32[4,72,128]{2,1,0:T(8,128)S(1)}, u32[]{:S(2)}, u32[]{:S(2)}) collective-permute-start(f32[4,72,128]{2,1,0:T(8,128)S(1)} %dynamic-slice_bitcast_fusion), channel_id=1, source_target_pairs={{0,32},{1,33},{2,34},{3,35},{4,36},{5,37},{6,38},{7,39},{8,40},{9,... | collective-permute-start | bytes 442376 | tf_op jit(solution)/shard_map/ppermute | solution.py:270
  26.2 4.2 %collective-permute-start.3 = (f32[72,128]{1,0:T(8,128)S(1)}, f32[72,128]{1,0:T(8,128)S(1)}, u32[]{:S(2)}, u32[]{:S(2)}) collective-permute-start(f32[72,128]{1,0:T(8,128)S(1)} %get-tuple-element.28), channel_id=1, source_target_pairs={{0,2},{1,3},{2,0},{3,1},{4,6},{5,7},{6,4},{7,5},{8,10},{9,11},{10,... | collective-permute-start | bytes 110600 | tf_op jit(solution)/shard_map/ppermute | solution.py:270
  26.3 5.2 %collective-permute-start.5 = (f32[72,128]{1,0:T(8,128)S(1)}, f32[72,128]{1,0:T(8,128)S(1)}, u32[]{:S(2)}, u32[]{:S(2)}) collective-permute-start(f32[72,128]{1,0:T(8,128)S(1)} %get-tuple-element.29), channel_id=1, source_target_pairs={{0,6},{1,7},{2,4},{3,5},{4,2},{5,3},{6,0},{7,1},{8,14},{9,15},{10,... | collective-permute-start | bytes 110600 | tf_op jit(solution)/shard_map/ppermute | solution.py:270
  28.0 5.5 %collective-permute-start.4 = (f32[72,128]{1,0:T(8,128)S(1)}, f32[72,128]{1,0:T(8,128)S(1)}, u32[]{:S(2)}, u32[]{:S(2)}) collective-permute-start(f32[72,128]{1,0:T(8,128)S(1)} %get-tuple-element.30), channel_id=1, source_target_pairs={{0,4},{1,5},{2,6},{3,7},{4,0},{5,1},{6,2},{7,3},{8,12},{9,13},{10,... | collective-permute-start | bytes 110600 | tf_op jit(solution)/shard_map/ppermute | solution.py:270
  33.4 4.4 %collective-permute-start.8 = (f32[72,128]{1,0:T(8,128)S(1)}, f32[72,128]{1,0:T(8,128)S(1)}, u32[]{:S(2)}, u32[]{:S(2)}) collective-permute-start(f32[72,128]{1,0:T(8,128)S(1)} %fusion.1), channel_id=1, source_target_pairs={{0,24},{1,25},{2,26},{3,27},{4,28},{5,29},{6,30},{7,31},{8,16},{9,... | collective-permute-start | bytes 110600 | tf_op jit(solution)/shard_map/ppermute | solution.py:270
  35.0 5.5 %collective-permute-start.7 = (f32[72,128]{1,0:T(8,128)S(1)}, f32[72,128]{1,0:T(8,128)S(1)}, u32[]{:S(2)}, u32[]{:S(2)}) collective-permute-start(f32[72,128]{1,0:T(8,128)S(1)} %fusion.1), channel_id=1, source_target_pairs={{0,16},{1,17},{2,18},{3,19},{4,20},{5,21},{6,22},{7,23},{8,24},{9,... | collective-permute-start | bytes 110600 | tf_op jit(solution)/shard_map/ppermute | solution.py:270
  36.1 4.3 %collective-permute-start.6 = (f32[72,128]{1,0:T(8,128)S(1)}, f32[72,128]{1,0:T(8,128)S(1)}, u32[]{:S(2)}, u32[]{:S(2)}) collective-permute-start(f32[72,128]{1,0:T(8,128)S(1)} %fusion.1), channel_id=1, source_target_pairs={{0,8},{1,9},{2,10},{3,11},{4,12},{5,13},{6,14},{7,15},{8,0},{9,1},... | collective-permute-start | bytes 110600 | tf_op jit(solution)/shard_map/ppermute | solution.py:270
  40.5 5.2 %collective-permute-start.11 = (f32[72,128]{1,0:T(8,128)S(1)}, f32[72,128]{1,0:T(8,128)S(1)}, u32[]{:S(2)}, u32[]{:S(2)}) collective-permute-start(f32[72,128]{1,0:T(8,128)S(1)} %add_add_fusion.1), channel_id=1, source_target_pairs={{0,65},{1,64},{2,67},{3,66},{4,69},{5,68},{6,71},{7,70},{8,73},{9,... | collective-permute-start | bytes 110600 | tf_op jit(solution)/shard_map/ppermute | solution.py:270
  43.7 5.5 %collective-permute-start.10 = (f32[72,128]{1,0:T(8,128)S(1)}, f32[72,128]{1,0:T(8,128)S(1)}, u32[]{:S(2)}, u32[]{:S(2)}) collective-permute-start(f32[72,128]{1,0:T(8,128)S(1)} %add_add_fusion.1), channel_id=1, source_target_pairs={{0,64},{1,65},{2,66},{3,67},{4,68},{5,69},{6,70},{7,71},{8,72},{9,... | collective-permute-start | bytes 110600 | tf_op jit(solution)/shard_map/ppermute | solution.py:270
  44.5 4.6 %collective-permute-start.9 = (f32[72,128]{1,0:T(8,128)S(1)}, f32[72,128]{1,0:T(8,128)S(1)}, u32[]{:S(2)}, u32[]{:S(2)}) collective-permute-start(f32[72,128]{1,0:T(8,128)S(1)} %add_add_fusion.1), channel_id=1, source_target_pairs={{0,1},{1,0},{2,3},{3,2},{4,5},{5,4},{6,7},{7,6},{8,9},{9,8},{10,11... | collective-permute-start | bytes 110600 | tf_op jit(solution)/shard_map/ppermute | solution.py:270
  49.2 5.2 %collective-permute-start.14 = (f32[72,128]{1,0:T(8,128)S(1)}, f32[72,128]{1,0:T(8,128)S(1)}, u32[]{:S(2)}, u32[]{:S(2)}) collective-permute-start(f32[72,128]{1,0:T(8,128)S(1)} %add_add_fusion), channel_id=1, source_target_pairs={{0,6},{1,7},{2,4},{3,5},{4,2},{5,3},{6,0},{7,1},{8,14},{9,15},{10,... | collective-permute-start | bytes 110600 | tf_op jit(solution)/shard_map/ppermute | solution.py:270
  50.3 5.5 %collective-permute-start.13 = (f32[72,128]{1,0:T(8,128)S(1)}, f32[72,128]{1,0:T(8,128)S(1)}, u32[]{:S(2)}, u32[]{:S(2)}) collective-permute-start(f32[72,128]{1,0:T(8,128)S(1)} %add_add_fusion), channel_id=1, source_target_pairs={{0,4},{1,5},{2,6},{3,7},{4,0},{5,1},{6,2},{7,3},{8,12},{9,13},{10,... | collective-permute-start | bytes 110600 | tf_op jit(solution)/shard_map/ppermute | solution.py:270
  52.0 4.0 %collective-permute-start.12 = (f32[72,128]{1,0:T(8,128)S(1)}, f32[72,128]{1,0:T(8,128)S(1)}, u32[]{:S(2)}, u32[]{:S(2)}) collective-permute-start(f32[72,128]{1,0:T(8,128)S(1)} %add_add_fusion), channel_id=1, source_target_pairs={{0,2},{1,3},{2,0},{3,1},{4,6},{5,7},{6,4},{7,5},{8,10},{9,11},{10,... | collective-permute-start | bytes 110600 | tf_op jit(solution)/shard_map/ppermute | solution.py:270
  56.0 1.5 %collective-permute-start.15 = (f32[4,72,128]{2,1,0:T(8,128)S(1)}, f32[4,72,128]{2,1,0:T(8,128)S(1)}, u32[]{:S(2)}, u32[]{:S(2)}) collective-permute-start(f32[4,72,128]{2,1,0:T(8,128)S(1)} %pad_maximum_fusion.own_ref), channel_id=1, source_target_pairs={{0,32},{1,33},{2,34},{3,35},{4,36},{5,37},{6,38},{7,39},{8,40},{9,... | collective-permute-start | bytes 442376 | tf_op jit(solution)/shard_map/ppermute | solution.py:270
  64.0 10.9 %collective-permute-start.17 = (f32[64,256]{1,0:T(8,128)S(1)}, f32[64,256]{1,0:T(8,128)S(1)}, u32[]{:S(2)}, u32[]{:S(2)}) collective-permute-start(f32[64,256]{1,0:T(8,128)S(1)} %get-tuple-element.22.head_ref), channel_id=1, source_target_pairs={{1,0},{2,1},{3,2},{4,3},{5,4},{6,5},{7,6},{8,7},{9,8},{10,9},{11,1... | collective-permute-start | bytes 196616 | tf_op jit(solution)/shard_map/ppermute | solution.py:400
  69.6 9.2 %collective-permute-start.16 = (f32[64,256]{1,0:T(8,128)S(1)}, f32[64,256]{1,0:T(8,128)S(1)}, u32[]{:S(2)}, u32[]{:S(2)}) collective-permute-start(f32[64,256]{1,0:T(8,128)S(1)} %get-tuple-element.23.tail_ref), channel_id=1, source_target_pairs={{0,1},{1,2},{2,3},{3,4},{4,5},{5,6},{6,7},{7,8},{8,9},{9,10},{10,1... | collective-permute-start | bytes 196616 | tf_op jit(solution)/shard_map/ppermute | solution.py:399

commit v5 on v4

--- a/solution.py
+++ b/solution.py
@@ -43,6 +43,14 @@
     wide = lax.dot_general(tokens, prior, NN, preferred_element_type=F32)
     half = (wide[:, :128] + wide[:, 128:]).T
     return half[:64] + half[64:]
+
+
+def begin(fetch, count):
+    def one(i, carry):
+        fetch(i).start()
+        return carry
+
+    lax.fori_loop(0, count, one, 0)
 
 
 def widths(width_ref, n_tile):
@@ -74,20 +82,20 @@
                 token_ref, sum_ref, raw_ref, held_ref, in_sem, out_sem, *, tok_rows, n_tile):
     steps = tok_rows // STEP
     chunks = [pl.ds(step * STEP, STEP) for step in range(steps)]
-    arrive = [
-        pltpu.make_async_copy(quant_ref.at[rows], raw_ref.at[rows], in_sem.at[step])
-        for step, rows in enumerate(chunks)
-    ]
+
+    def fetch(i):
+        rows = pl.ds(pl.multiple_of(i * STEP, STEP), STEP)
+        return pltpu.make_async_copy(quant_ref.at[rows], raw_ref.at[rows], in_sem.at[i])
+
+    begin(fetch, steps)
     leave = [
         pltpu.make_async_copy(held_ref.at[rows], token_ref.at[rows], out_sem.at[step])
         for step, rows in enumerate(chunks)
     ]
-    for copy in arrive:
-        copy.start()
     left, right = widths(width_ref, n_tile)
     for step in range(steps + 1):
         if step < steps:
-            arrive[step].wait()
+            fetch(step).wait()
             blocks = dequantize(raw_ref[chunks[step], :], scale_ref[:, chunks[step]])
             for b, block in enumerate(blocks):
                 held_ref[chunks[step], b * block.shape[1] : (b + 1) * block.shape[1]] = block
@@ -131,11 +139,16 @@
             jnp.concatenate([high, low, extra], 0), rows[...], NN, preferred_element_type=F32
         )
     update = total[:keep] + total[keep : 2 * keep]
-    row = lax.broadcasted_iota(jnp.int32, (ROWS - keep, total.shape[1]), 0)
-    extra = jnp.where(row == 0, total[2 * keep : 2 * keep + ROWS - keep], valid_ref[0].astype(F32))
-    for c in range(out_ref.shape[0]):
-        out_ref[c, :keep, :] = update[:, c * 128 : (c + 1) * 128]
-        out_ref[c, keep:, :] = extra[:, c * 128 : (c + 1) * 128]
+    row = lax.broadcasted_iota(jnp.int32, (8, 128), 0)
+    parts = out_ref.shape[0]
+    share = total.shape[1] // 128 // parts
+    for part in range(parts):
+        extra = jnp.where(row == share, valid_ref[0].astype(F32), 0.0)
+        for c in range(share):
+            lanes = slice((part * share + c) * 128, (part * share + c + 1) * 128)
+            out_ref[part, c * keep : (c + 1) * keep, :] = update[:, lanes]
+            extra = jnp.where(row == c, total[2 * keep : 2 * keep + 1, lanes], extra)
+        out_ref[part, share * keep :, :] = extra
 
 
 def inverse_factor(square):
@@ -177,24 +190,24 @@
 def basis_kernel(own_ref, other_ref, prior_ref, head_ref, tail_ref, far_ref,
                  basis_ref, pair_ref, shift_ref, head_out_ref, tail_out_ref, token_ref, sem):
     size = token_ref.shape[0] // sem.shape[0]
-    arrive = [
-        pltpu.make_async_copy(far_ref.at[pl.ds(i * size, size)], token_ref.at[pl.ds(i * size, size)], sem.at[i])
-        for i in range(sem.shape[0])
-    ]
-    for copy in arrive:
-        copy.start()
+
+    def fetch(i):
+        rows = pl.ds(pl.multiple_of(i * size, size), size)
+        return pltpu.make_async_copy(far_ref.at[rows], token_ref.at[rows], sem.at[i])
+
+    begin(fetch, sem.shape[0])
     core = lax.rem(lax.axis_index("region"), 2)
-    y = lax.rem(lax.div(lax.axis_index("tile"), 2), 4)
     keep = prior_ref.shape[0]
-    pieces = []
-    for c in range(8):
-        slot = jnp.bitwise_xor(c % 4, y)
-        pieces.append(jnp.where(core == c // 4, own_ref[slot], other_ref[slot]))
-    full = jnp.concatenate(pieces, 1)
-    sums = full[keep : keep + 1]
-    average = sums / full[keep + 1 : keep + 2]
+    share = prior_ref.shape[1] // 256
+    own, other = own_ref[...], other_ref[...]
+    halves = [jnp.where(core == part, own, other) for part in range(2)]
+    update = jnp.concatenate([half[c * keep : (c + 1) * keep] for half in halves for c in range(share)], 1)
+    base = share * keep
+    sums = jnp.concatenate([half[base + c : base + c + 1] for half in halves for c in range(share)], 1)
+    count = own[base + share : base + share + 1, :1]
+    average = sums / count
     image = jnp.sum(prior_ref[...] * average, axis=1, keepdims=True)
-    update = full[:keep] - image * sums
+    update = update - image * sums
     square = lax.dot_general(update, update, NT, precision=lax.Precision.HIGHEST, preferred_element_type=F32)
     inverse = inverse_factor(square)
     basis = lax.dot_general(inverse, update, NN, precision=lax.Precision.HIGHEST, preferred_element_type=F32)
@@ -207,8 +220,8 @@
     for rows, out in ((head_ref, head_out_ref), (tail_ref, tail_out_ref)):
         wide = lax.dot_general(rows[...], pair, NN, preferred_element_type=F32).T
         out[...] = wide[:keep] + wide[keep:]
-    for copy in arrive:
-        copy.wait()
+    for i in range(sem.shape[0]):
+        fetch(i).wait()
 
 
 def project_kernel(valid_ref, token_ref, pair_ref, shift_ref, out_ref, value_ref, out_sem, *, tok_rows):
@@ -274,23 +287,13 @@
     return lax.dynamic_index_in_dim(stack, index, 0, keepdims=False)
 
 
-def reduce_all(pieces):
+def reduce_all(halves):
     core = lax.axis_index("region") % 2
-    y = (lax.axis_index("tile") // 2) % 4
-    halves = pieces.reshape(2, 4, *pieces.shape[1:])
-    half = pick(halves, core) + flip(pick(halves, 1 - core), 32)
-    arrived = [flip(pick(half, y ^ k), k << 1) for k in range(1, 4)]
-    mine = pick(half, y)
-    for piece in arrived:
-        mine = mine + piece
-    arrived = [flip(mine, k << 3) for k in range(1, 4)]
-    for piece in arrived:
-        mine = mine + piece
-    arrived = [flip(mine, mask) for mask in (1, 64, 65)]
-    for piece in arrived:
-        mine = mine + piece
-    own = jnp.stack([mine] + [flip(mine, k << 1) for k in range(1, 4)])
-    return own, flip(own, 32)
+    mine = pick(halves, core) + flip(pick(halves, 1 - core), 32)
+    for masks in ((2, 4, 6), (8, 16, 24), (1, 64, 65)):
+        near_one, far_one, across = [flip(mine, mask) for mask in masks]
+        mine = (mine + near_one) + (far_one + across)
+    return mine, flip(mine, 32)
 
 
 def per_device(quantized, block_scales, band_width, valid_count, prior_basis):
@@ -374,8 +377,8 @@
             whole(ROWS, BAND),
             whole(keep, BAND),
         ],
-        out_specs=whole(feat_dim // 128, ROWS, 128),
-        out_shape=jax.ShapeDtypeStruct((feat_dim // 128, ROWS, 128), F32),
+        out_specs=whole(2, feat_dim // 256 * keep + 8, 128),
+        out_shape=jax.ShapeDtypeStruct((2, feat_dim // 256 * keep + 8, 128), F32),
         compiler_params=params(24),
         name="join",
     )(band_width, valid_count, head_tokens, tail_tokens, sums, forward, backward, before, after)

time: 80.5 us -> 76.5 us (0.950)
  starting transfers between devices: 33.4 us -> 28.2 us
  waiting for transfers between devices: 19.6 us -> 22.9 us
  Pallas kernels: 25.5 us -> 23.4 us
    ppermute x14 -> x11, starting transfers between devices: 16.9 us -> 12.9 us  [flip(): return lax.ppermute(value, AXES, pairs)]
    ppermute x14 -> x11, waiting for transfers between devices: 15.7 us -> 19 us  [flip(): return lax.ppermute(value, AXES, pairs)]
    pallas_call x1, Pallas kernels: 6.57 us -> 4.36 us  [per_device(): pl.pallas_call(basis_kernel, in_specs=[near()] * 5 + [far()], out_specs=[...]
    ppermute x1, starting transfers between devices: 5.61 us -> 4.46 us  [per_device(): after = lax.ppermute(head, 'tile', backward_pairs)]
  transfers between devices with their start and end apart: 18 -> 15, of which waited for: 12 -> 11; matrix products, arithmetic and copies ran while one was open for 0% -> 0% of each run, Pallas kernels for 18% -> 19%
where the time goes in v5:
time: 76.5 us; the launch traced here: 76.3 us
  starting transfers between devices  28.2 us (37%)
  Pallas kernels  23.4 us (31%)
  waiting for transfers between devices  22.9 us (30%)
  between operations  1.64 us (2%)
    ppermute x11, waiting for transfers between devices, flip(): return lax.ppermute(value, AXES, pairs)  19 us
    ppermute x11, starting transfers between devices, flip(): return lax.ppermute(value, AXES, pairs)  12.9 us
    pallas_call x1, Pallas kernels, per_device(): bulk(band_width, valid_count, quant_far, block_scales, prior3)  11.1 us
    ppermute x1, starting transfers between devices, per_device(): after = lax.ppermute(backward, 'tile', backward_pairs)  5.02 us
    ppermute x1, starting transfers between devices, per_device(): after = lax.ppermute(head, 'tile', backward_pairs)  4.46 us
    pallas_call x1, Pallas kernels, per_device(): pl.pallas_call(basis_kernel, in_specs=[near()] * 5 + [far()], out_specs=[...  4.36 us
    ppermute x1, starting transfers between devices, per_device(): before = lax.ppermute(forward, 'tile', forward_pairs)  3.96 us
    ppermute x1, waiting for transfers between devices, per_device(): before = lax.ppermute(tail, 'tile', forward_pairs)  3.9 us
  transfers between devices with their start and end apart: 15, of which 11 were waited for; matrix products, arithmetic and copies ran while one was open for 0% of the time, Pallas kernels for 19%

profile of v5, /device:TPU:2, one launch (start us, length us, event | category | flops | bytes accessed | tf_op | source)
XLA Modules:
  0.0 76.3 jit_solution(16928919875165775367)
XLA Ops:
  1.3 0.0 copy-start
  1.3 0.0 copy-start.2
  1.3 2.4 %band.1 = (f32[72,256]{1,0:T(8,128)S(1)}, f32[64,256]{1,0:T(8,128)S(1)}, bf16[1024,256]{1,0:T(8,128)(2,1)S(1)}, bf16[256,1024]{1,0:T(8,128)(2,1)S(1)}, bf16[256,1024]{1,0:T(8,128)(2,1)S(1)}) custom-call(s32[1]{0:T(128)S(6)} %copy.9.valid_ref, bf16[4096,1024]{1,0:T(8,128)(2,1)} %quant_ref.1, bf16[4096,1024]{1,0:T(8,128)(2,1)} %quant_ref.1, ...), custom_call_target="tpu_custom_call" | custom-call | tf_op jit(solution)/shard_map/band/pallas_call | solution.py:318
  3.7 0.0 copy-start.1
  3.7 4.0 %collective-permute-start = (f32[72,256]{1,0:T(8,128)S(1)}, f32[72,256]{1,0:T(8,128)S(1)}, u32[]{:S(2)}, u32[]{:S(2)}) collective-permute-start(f32[72,256]{1,0:T(8,128)S(1)} %get-tuple-element.19.forward_ref), channel_id=1, source_target_pairs={{0,1},{1,2},{2,3},{3,4},{4,5},{5,6},{6,7},{7,8},{8,9},{9,10},{10,1... | collective-permute-start | bytes 221192 | tf_op jit(solution)/shard_map/ppermute | solution.py:346
  7.6 5.0 %collective-permute-start.1 = (f32[64,256]{1,0:T(8,128)S(1)}, f32[64,256]{1,0:T(8,128)S(1)}, u32[]{:S(2)}, u32[]{:S(2)}) collective-permute-start(f32[64,256]{1,0:T(8,128)S(1)} %get-tuple-element.20.backward_ref), channel_id=1, source_target_pairs={{1,0},{2,1},{3,2},{4,3},{5,4},{6,5},{7,6},{8,7},{9,8},{10,9},{11,1... | collective-permute-start | bytes 196616 | tf_op jit(solution)/shard_map/ppermute | solution.py:347
  12.7 0.0 copy-done
  12.7 0.0 copy-done.2
  12.7 11.1 %bulk.1 = (bf16[4096,1024]{1,0:T(8,128)(2,1)}, f32[144,1024]{1,0:T(8,128)S(1)}) custom-call(s32[128]{0:T(128)S(1)} %copy-done.2, s32[1]{0:T(128)S(6)} %copy.9.valid_ref, bf16[4096,1024]{1,0:T(8,128)(2,1)} %quant_ref.1, f32[8,4096]{1,0:T(8,128)S(1)} %copy-done, bf16[1024,256]{1,0:T(8,128)(2,1)S(1)} %get-tuple-element.17.prior3_ref), custom_call_target="tpu_custom_call" | custom-call | tf_op jit(solution)/shard_map/bulk/pallas_call | solution.py:365
  23.8 0.0 collective-permute-done.1.after_ref
  23.8 0.0 collective-permute-done.before_ref
  23.8 0.9 %join.1 = f32[2,264,128]{2,1,0:T(8,128)S(1)} custom-call(s32[128]{0:T(128)S(1)} %copy-done.2, s32[1]{0:T(128)S(6)} %copy.9.valid_ref, bf16[256,1024]{1,0:T(8,128)(2,1)S(1)} %get-tuple-element.15.head_ref, bf16[256,1024]{1,0:T(8,128)(2,1)S(1)} %get-tuple-element.16.tail_ref, f32[144,1024]{1,0:T(8,128)S(1)} %get-tuple-element.18.sum_ref, ...), custom_call_target="tpu_custom_call" | custom-call | tf_op jit(solution)/shard_map/join/pallas_call | solution.py:366
  24.8 0.1 collective-permute-start.2
  24.9 1.3 %collective-permute-done.2 = f32[264,128]{1,0:T(8,128)S(1)} collective-permute-done((f32[264,128]{1,0:T(8,128)S(1)}, f32[264,128]{1,0:T(8,128)S(1)}, u32[]{:S(2)}, u32[]{:S(2)}) %collective-permute-start.2) | collective-permute-done | bytes 135200 | tf_op jit(solution)/shard_map/ppermute | solution.py:283
  26.2 1.0 %collective-permute-start.5 = (f32[264,128]{1,0:T(8,128)S(1)}, f32[264,128]{1,0:T(8,128)S(1)}, u32[]{:S(2)}, u32[]{:S(2)}) collective-permute-start(f32[264,128]{1,0:T(8,128)S(1)} %bitcast_add_fusion), channel_id=1, source_target_pairs={{0,6},{1,7},{2,4},{3,5},{4,2},{5,3},{6,0},{7,1},{8,14},{9,15},{10,... | collective-permute-start | bytes 405512 | tf_op jit(solution)/shard_map/ppermute | solution.py:283
  27.2 0.6 collective-permute-start.4
  27.8 2.6 %collective-permute-start.3 = (f32[264,128]{1,0:T(8,128)S(1)}, f32[264,128]{1,0:T(8,128)S(1)}, u32[]{:S(2)}, u32[]{:S(2)}) collective-permute-start(f32[264,128]{1,0:T(8,128)S(1)} %bitcast_add_fusion), channel_id=1, source_target_pairs={{0,2},{1,3},{2,0},{3,1},{4,6},{5,7},{6,4},{7,5},{8,10},{9,11},{10,... | collective-permute-start | bytes 405512 | tf_op jit(solution)/shard_map/ppermute | solution.py:283
  30.4 5.6 %collective-permute-done.5 = f32[264,128]{1,0:T(8,128)S(1)} collective-permute-done((f32[264,128]{1,0:T(8,128)S(1)}, f32[264,128]{1,0:T(8,128)S(1)}, u32[]{:S(2)}, u32[]{:S(2)}) %collective-permute-start.5) | collective-permute-done | bytes 135200 | tf_op jit(solution)/shard_map/ppermute | solution.py:283
  36.0 0.0 collective-permute-done.4
  36.0 0.6 collective-permute-done.3
  36.7 1.6 %collective-permute-start.8 = (f32[264,128]{1,0:T(8,128)S(1)}, f32[264,128]{1,0:T(8,128)S(1)}, u32[]{:S(2)}, u32[]{:S(2)}) collective-permute-start(f32[264,128]{1,0:T(8,128)S(1)} %add_add_fusion.2), channel_id=1, source_target_pairs={{0,24},{1,25},{2,26},{3,27},{4,28},{5,29},{6,30},{7,31},{8,16},{9,... | collective-permute-start | bytes 405512 | tf_op jit(solution)/shard_map/ppermute | solution.py:283
  38.3 0.7 collective-permute-start.7
  39.0 1.9 %collective-permute-start.6 = (f32[264,128]{1,0:T(8,128)S(1)}, f32[264,128]{1,0:T(8,128)S(1)}, u32[]{:S(2)}, u32[]{:S(2)}) collective-permute-start(f32[264,128]{1,0:T(8,128)S(1)} %add_add_fusion.2), channel_id=1, source_target_pairs={{0,8},{1,9},{2,10},{3,11},{4,12},{5,13},{6,14},{7,15},{8,0},{9,1},... | collective-permute-start | bytes 405512 | tf_op jit(solution)/shard_map/ppermute | solution.py:283
  40.9 2.4 %collective-permute-done.8 = f32[264,128]{1,0:T(8,128)S(1)} collective-permute-done((f32[264,128]{1,0:T(8,128)S(1)}, f32[264,128]{1,0:T(8,128)S(1)}, u32[]{:S(2)}, u32[]{:S(2)}) %collective-permute-start.8) | collective-permute-done | bytes 135200 | tf_op jit(solution)/shard_map/ppermute | solution.py:283
  43.2 2.3 %collective-permute-done.7 = f32[264,128]{1,0:T(8,128)S(1)} collective-permute-done((f32[264,128]{1,0:T(8,128)S(1)}, f32[264,128]{1,0:T(8,128)S(1)}, u32[]{:S(2)}, u32[]{:S(2)}) %collective-permute-start.7) | collective-permute-done | bytes 135200 | tf_op jit(solution)/shard_map/ppermute | solution.py:283
  45.5 0.5 collective-permute-done.6
  46.0 1.4 %collective-permute-start.11 = (f32[264,128]{1,0:T(8,128)S(1)}, f32[264,128]{1,0:T(8,128)S(1)}, u32[]{:S(2)}, u32[]{:S(2)}) collective-permute-start(f32[264,128]{1,0:T(8,128)S(1)} %add_add_fusion.1), channel_id=1, source_target_pairs={{0,65},{1,64},{2,67},{3,66},{4,69},{5,68},{6,71},{7,70},{8,73},{9,... | collective-permute-start | bytes 405512 | tf_op jit(solution)/shard_map/ppermute | solution.py:283
  47.4 2.7 %collective-permute-start.10 = (f32[264,128]{1,0:T(8,128)S(1)}, f32[264,128]{1,0:T(8,128)S(1)}, u32[]{:S(2)}, u32[]{:S(2)}) collective-permute-start(f32[264,128]{1,0:T(8,128)S(1)} %add_add_fusion.1), channel_id=1, source_target_pairs={{0,64},{1,65},{2,66},{3,67},{4,68},{5,69},{6,70},{7,71},{8,72},{9,... | collective-permute-start | bytes 405512 | tf_op jit(solution)/shard_map/ppermute | solution.py:283
  50.1 0.1 collective-permute-start.9
  50.2 2.1 %collective-permute-done.11 = f32[264,128]{1,0:T(8,128)S(1)} collective-permute-done((f32[264,128]{1,0:T(8,128)S(1)}, f32[264,128]{1,0:T(8,128)S(1)}, u32[]{:S(2)}, u32[]{:S(2)}) %collective-permute-start.11) | collective-permute-done | bytes 135200 | tf_op jit(solution)/shard_map/ppermute | solution.py:283
  52.3 2.6 %collective-permute-done.10 = f32[264,128]{1,0:T(8,128)S(1)} collective-permute-done((f32[264,128]{1,0:T(8,128)S(1)}, f32[264,128]{1,0:T(8,128)S(1)}, u32[]{:S(2)}, u32[]{:S(2)}) %collective-permute-start.10) | collective-permute-done | bytes 135200 | tf_op jit(solution)/shard_map/ppermute | solution.py:283
  54.9 0.2 collective-permute-done.9
  55.1 0.3 collective-permute-start.12
  55.4 1.3 %collective-permute-done.12.other_ref = f32[264,128]{1,0:T(8,128)S(1)} collective-permute-done((f32[264,128]{1,0:T(8,128)S(1)}, f32[264,128]{1,0:T(8,128)S(1)}, u32[]{:S(2)}, u32[]{:S(2)}) %collective-permute-start.12) | collective-permute-done | bytes 135200 | tf_op jit(solution)/shard_map/ppermute | solution.py:283
  56.8 0.0 copy-done.1
  56.8 4.4 %basis.1 = (f32[64,1024]{1,0:T(8,128)}, bf16[1024,128]{1,0:T(8,128)(2,1)S(1)}, f32[64,128]{1,0:T(8,128)S(1)}, f32[64,256]{1,0:T(8,128)S(1)}, f32[64,256]{1,0:T(8,128)S(1)}, /*index=5*/bf16[4096,1024]{1,0:T(8,128)(2,1)S(1)}) custom-call(f32[264,128]{1,0:T(8,128)S(1)} %add_add_fusion.own_ref, f32[264,128]{1,0:T(8,128)S(1)} %collective-permute-done.12.other_ref, ...), custom_call_target="tpu_custom_call" | custom-call | tf_op jit(solution)/shard_map/basis/pallas_call | solution.py:386
  61.1 4.5 %collective-permute-start.14 = (f32[64,256]{1,0:T(8,128)S(1)}, f32[64,256]{1,0:T(8,128)S(1)}, u32[]{:S(2)}, u32[]{:S(2)}) collective-permute-start(f32[64,256]{1,0:T(8,128)S(1)} %get-tuple-element.22.head_ref), channel_id=1, source_target_pairs={{1,0},{2,1},{3,2},{4,3},{5,4},{6,5},{7,6},{8,7},{9,8},{10,9},{11,1... | collective-permute-start | bytes 196616 | tf_op jit(solution)/shard_map/ppermute | solution.py:403
  65.6 1.9 %collective-permute-start.13 = (f32[64,256]{1,0:T(8,128)S(1)}, f32[64,256]{1,0:T(8,128)S(1)}, u32[]{:S(2)}, u32[]{:S(2)}) collective-permute-start(f32[64,256]{1,0:T(8,128)S(1)} %get-tuple-element.23.tail_ref), channel_id=1, source_target_pairs={{0,1},{1,2},{2,3},{3,4},{4,5},{5,6},{6,7},{7,8},{8,9},{9,10},{10,1... | collective-permute-start | bytes 196616 | tf_op jit(solution)/shard_map/ppermute | solution.py:402
  67.5 3.3 %project.1.whole_ref = f32[64,4096]{1,0:T(8,128)} custom-call(s32[1]{0:T(128)S(6)} %copy.9.valid_ref, bf16[4096,1024]{1,0:T(8,128)(2,1)S(1)} %get-tuple-element.25.token_ref, bf16[1024,128]{1,0:T(8,128)(2,1)S(1)} %get-tuple-element.26.pair_ref, f32[64,128]{1,0:T(8,128)S(1)} %get-tuple-element.24.shift_ref), custom_call_target="tpu_custom_call" | custom-call | tf_op jit(solution)/shard_map/project/pallas_call | solution.py:404
  70.9 0.0 collective-permute-done.14.after_ref
  70.9 3.9 %collective-permute-done.13.before_ref = f32[64,256]{1,0:T(8,128)S(1)} collective-permute-done((f32[64,256]{1,0:T(8,128)S(1)}, f32[64,256]{1,0:T(8,128)S(1)}, u32[]{:S(2)}, u32[]{:S(2)}) %collective-permute-start.13) | collective-permute-done | bytes 65568 | tf_op jit(solution)/shard_map/ppermute | solution.py:402
  74.8 1.3 %blend.1 = f32[64,4096]{1,0:T(8,128)} custom-call(s32[128]{0:T(128)S(1)} %copy-done.2, s32[1]{0:T(128)S(6)} %copy.9.valid_ref, f32[64,256]{1,0:T(8,128)S(1)} %get-tuple-element.22.head_ref, f32[64,256]{1,0:T(8,128)S(1)} %get-tuple-element.23.tail_ref, f32[64,256]{1,0:T(8,128)S(1)} %collective-permute-done.13.before_ref, ...), custom_call_target="tpu_custom_call", output_to_operand_aliasing={{}: (7, {})} | custom-call | tf_op jit(solution)/shard_map/blend/pallas_call | solution.py:413
  (5 shorter events, 0.1 us)
Async XLA Ops:
  1.3 11.4 %copy-start = (f32[8,4096]{1,0:T(8,128)S(1)}, f32[8,4096]{1,0:T(8,128)}, u32[]{:S(2)}) copy-start(f32[8,4096]{1,0:T(8,128)} %scale_ref.1) | copy-start | bytes 393220
  1.3 11.4 %copy-start.2 = (s32[128]{0:T(128)S(1)}, s32[128]{0:T(128)}, u32[]{:S(2)}) copy-start(s32[128]{0:T(128)} %width_ref.5) | copy-start | bytes 1540
  3.7 53.1 %copy-start.1 = (f32[1024,64]{0,1:T(8,128)S(1)}, f32[1024,64]{0,1:T(8,128)}, u32[]{:S(2)}) copy-start(f32[1024,64]{0,1:T(8,128)} %param.9) | copy-start | bytes 786436
  3.7 20.1 %collective-permute-start = (f32[72,256]{1,0:T(8,128)S(1)}, f32[72,256]{1,0:T(8,128)S(1)}, u32[]{:S(2)}, u32[]{:S(2)}) collective-permute-start(f32[72,256]{1,0:T(8,128)S(1)} %get-tuple-element.19.forward_ref), channel_id=1, source_target_pairs={{0,1},{1,2},{2,3},{3,4},{4,5},{5,6},{6,7},{7,8},{8,9},{9,10},{10,1... | collective-permute-start | bytes 221192 | tf_op jit(solution)/shard_map/ppermute | solution.py:346
  7.6 16.1 %collective-permute-start.1 = (f32[64,256]{1,0:T(8,128)S(1)}, f32[64,256]{1,0:T(8,128)S(1)}, u32[]{:S(2)}, u32[]{:S(2)}) collective-permute-start(f32[64,256]{1,0:T(8,128)S(1)} %get-tuple-element.20.backward_ref), channel_id=1, source_target_pairs={{1,0},{2,1},{3,2},{4,3},{5,4},{6,5},{7,6},{8,7},{9,8},{10,9},{11,1... | collective-permute-start | bytes 196616 | tf_op jit(solution)/shard_map/ppermute | solution.py:347
  24.8 1.4 %collective-permute-start.2 = (f32[264,128]{1,0:T(8,128)S(1)}, f32[264,128]{1,0:T(8,128)S(1)}, u32[]{:S(2)}, u32[]{:S(2)}) collective-permute-start(f32[264,128]{1,0:T(8,128)S(1)} %dynamic-slice_bitcast_fusion), channel_id=1, source_target_pairs={{0,32},{1,33},{2,34},{3,35},{4,36},{5,37},{6,38},{7,39},{8,40},{9,... | collective-permute-start | bytes 405512 | tf_op jit(solution)/shard_map/ppermute | solution.py:283
  26.2 9.8 %collective-permute-start.5 = (f32[264,128]{1,0:T(8,128)S(1)}, f32[264,128]{1,0:T(8,128)S(1)}, u32[]{:S(2)}, u32[]{:S(2)}) collective-permute-start(f32[264,128]{1,0:T(8,128)S(1)} %bitcast_add_fusion), channel_id=1, source_target_pairs={{0,6},{1,7},{2,4},{3,5},{4,2},{5,3},{6,0},{7,1},{8,14},{9,15},{10,... | collective-permute-start | bytes 405512 | tf_op jit(solution)/shard_map/ppermute | solution.py:283
  27.2 8.8 %collective-permute-start.4 = (f32[264,128]{1,0:T(8,128)S(1)}, f32[264,128]{1,0:T(8,128)S(1)}, u32[]{:S(2)}, u32[]{:S(2)}) collective-permute-start(f32[264,128]{1,0:T(8,128)S(1)} %bitcast_add_fusion), channel_id=1, source_target_pairs={{0,4},{1,5},{2,6},{3,7},{4,0},{5,1},{6,2},{7,3},{8,12},{9,13},{10,... | collective-permute-start | bytes 405512 | tf_op jit(solution)/shard_map/ppermute | solution.py:283
  27.8 8.8 %collective-permute-start.3 = (f32[264,128]{1,0:T(8,128)S(1)}, f32[264,128]{1,0:T(8,128)S(1)}, u32[]{:S(2)}, u32[]{:S(2)}) collective-permute-start(f32[264,128]{1,0:T(8,128)S(1)} %bitcast_add_fusion), channel_id=1, source_target_pairs={{0,2},{1,3},{2,0},{3,1},{4,6},{5,7},{6,4},{7,5},{8,10},{9,11},{10,... | collective-permute-start | bytes 405512 | tf_op jit(solution)/shard_map/ppermute | solution.py:283
  36.7 6.5 %collective-permute-start.8 = (f32[264,128]{1,0:T(8,128)S(1)}, f32[264,128]{1,0:T(8,128)S(1)}, u32[]{:S(2)}, u32[]{:S(2)}) collective-permute-start(f32[264,128]{1,0:T(8,128)S(1)} %add_add_fusion.2), channel_id=1, source_target_pairs={{0,24},{1,25},{2,26},{3,27},{4,28},{5,29},{6,30},{7,31},{8,16},{9,... | collective-permute-start | bytes 405512 | tf_op jit(solution)/shard_map/ppermute | solution.py:283
  38.3 7.3 %collective-permute-start.7 = (f32[264,128]{1,0:T(8,128)S(1)}, f32[264,128]{1,0:T(8,128)S(1)}, u32[]{:S(2)}, u32[]{:S(2)}) collective-permute-start(f32[264,128]{1,0:T(8,128)S(1)} %add_add_fusion.2), channel_id=1, source_target_pairs={{0,16},{1,17},{2,18},{3,19},{4,20},{5,21},{6,22},{7,23},{8,24},{9,... | collective-permute-start | bytes 405512 | tf_op jit(solution)/shard_map/ppermute | solution.py:283
  39.0 7.0 %collective-permute-start.6 = (f32[264,128]{1,0:T(8,128)S(1)}, f32[264,128]{1,0:T(8,128)S(1)}, u32[]{:S(2)}, u32[]{:S(2)}) collective-permute-start(f32[264,128]{1,0:T(8,128)S(1)} %add_add_fusion.2), channel_id=1, source_target_pairs={{0,8},{1,9},{2,10},{3,11},{4,12},{5,13},{6,14},{7,15},{8,0},{9,1},... | collective-permute-start | bytes 405512 | tf_op jit(solution)/shard_map/ppermute | solution.py:283
  46.0 6.3 %collective-permute-start.11 = (f32[264,128]{1,0:T(8,128)S(1)}, f32[264,128]{1,0:T(8,128)S(1)}, u32[]{:S(2)}, u32[]{:S(2)}) collective-permute-start(f32[264,128]{1,0:T(8,128)S(1)} %add_add_fusion.1), channel_id=1, source_target_pairs={{0,65},{1,64},{2,67},{3,66},{4,69},{5,68},{6,71},{7,70},{8,73},{9,... | collective-permute-start | bytes 405512 | tf_op jit(solution)/shard_map/ppermute | solution.py:283
  47.4 7.5 %collective-permute-start.10 = (f32[264,128]{1,0:T(8,128)S(1)}, f32[264,128]{1,0:T(8,128)S(1)}, u32[]{:S(2)}, u32[]{:S(2)}) collective-permute-start(f32[264,128]{1,0:T(8,128)S(1)} %add_add_fusion.1), channel_id=1, source_target_pairs={{0,64},{1,65},{2,66},{3,67},{4,68},{5,69},{6,70},{7,71},{8,72},{9,... | collective-permute-start | bytes 405512 | tf_op jit(solution)/shard_map/ppermute | solution.py:283
  50.1 5.0 %collective-permute-start.9 = (f32[264,128]{1,0:T(8,128)S(1)}, f32[264,128]{1,0:T(8,128)S(1)}, u32[]{:S(2)}, u32[]{:S(2)}) collective-permute-start(f32[264,128]{1,0:T(8,128)S(1)} %add_add_fusion.1), channel_id=1, source_target_pairs={{0,1},{1,0},{2,3},{3,2},{4,5},{5,4},{6,7},{7,6},{8,9},{9,8},{10,11... | collective-permute-start | bytes 405512 | tf_op jit(solution)/shard_map/ppermute | solution.py:283
  55.1 1.6 %collective-permute-start.12 = (f32[264,128]{1,0:T(8,128)S(1)}, f32[264,128]{1,0:T(8,128)S(1)}, u32[]{:S(2)}, u32[]{:S(2)}) collective-permute-start(f32[264,128]{1,0:T(8,128)S(1)} %add_add_fusion.own_ref), channel_id=1, source_target_pairs={{0,32},{1,33},{2,34},{3,35},{4,36},{5,37},{6,38},{7,39},{8,40},{9,... | collective-permute-start | bytes 405512 | tf_op jit(solution)/shard_map/ppermute | solution.py:283
  61.1 9.7 %collective-permute-start.14 = (f32[64,256]{1,0:T(8,128)S(1)}, f32[64,256]{1,0:T(8,128)S(1)}, u32[]{:S(2)}, u32[]{:S(2)}) collective-permute-start(f32[64,256]{1,0:T(8,128)S(1)} %get-tuple-element.22.head_ref), channel_id=1, source_target_pairs={{1,0},{2,1},{3,2},{4,3},{5,4},{6,5},{7,6},{8,7},{9,8},{10,9},{11,1... | collective-permute-start | bytes 196616 | tf_op jit(solution)/shard_map/ppermute | solution.py:403
  65.6 9.2 %collective-permute-start.13 = (f32[64,256]{1,0:T(8,128)S(1)}, f32[64,256]{1,0:T(8,128)S(1)}, u32[]{:S(2)}, u32[]{:S(2)}) collective-permute-start(f32[64,256]{1,0:T(8,128)S(1)} %get-tuple-element.23.tail_ref), channel_id=1, source_target_pairs={{0,1},{1,2},{2,3},{3,4},{4,5},{5,6},{6,7},{7,8},{8,9},{9,10},{10,1... | collective-permute-start | bytes 196616 | tf_op jit(solution)/shard_map/ppermute | solution.py:402

commit v6 on v5

--- a/solution.py
+++ b/solution.py
@@ -45,9 +45,10 @@
     return half[:64] + half[64:]
 
 
-def begin(fetch, count):
+def begin(count, *makers):
     def one(i, carry):
-        fetch(i).start()
+        for make in makers:
+            make(i).start()
         return carry
 
     lax.fori_loop(0, count, one, 0)
@@ -82,20 +83,30 @@
                 token_ref, sum_ref, raw_ref, held_ref, in_sem, out_sem, *, tok_rows, n_tile):
     steps = tok_rows // STEP
     chunks = [pl.ds(step * STEP, STEP) for step in range(steps)]
-
-    def fetch(i):
-        rows = pl.ds(pl.multiple_of(i * STEP, STEP), STEP)
-        return pltpu.make_async_copy(quant_ref.at[rows], raw_ref.at[rows], in_sem.at[i])
-
-    begin(fetch, steps)
-    leave = [
-        pltpu.make_async_copy(held_ref.at[rows], token_ref.at[rows], out_sem.at[step])
-        for step, rows in enumerate(chunks)
-    ]
+    part = STEP // 2
+
+    def mover(source, target, sems, step):
+        def make(i):
+            rows = pl.ds(pl.multiple_of(step * STEP + i * part, part), part)
+            return pltpu.make_async_copy(source.at[rows], target.at[rows], sems.at[2 * step + i])
+
+        return make
+
+    arrive = [mover(quant_ref, raw_ref, in_sem, step) for step in range(steps)]
+    leave = [mover(held_ref, token_ref, out_sem, step) for step in range(steps)]
+    begin(2, arrive[0])
+    begin(2, arrive[1])
     left, right = widths(width_ref, n_tile)
     for step in range(steps + 1):
         if step < steps:
-            fetch(step).wait()
+            for i in range(2):
+                arrive[step](i).wait()
+        makers = [leave[step - 1]] if step > 0 else []
+        if step + 2 < steps:
+            makers.append(arrive[step + 2])
+        if makers:
+            begin(2, *makers)
+        if step < steps:
             blocks = dequantize(raw_ref[chunks[step], :], scale_ref[:, chunks[step]])
             for b, block in enumerate(blocks):
                 held_ref[chunks[step], b * block.shape[1] : (b + 1) * block.shape[1]] = block
@@ -109,13 +120,13 @@
             high = reduced.astype(BF16)
             low = (reduced - high.astype(F32)).astype(BF16)
             extra = jnp.broadcast_to(weight, (16, STEP)).astype(BF16)
-            part = lax.dot_general(
+            total = lax.dot_general(
                 jnp.concatenate([high, low, extra], 0), tokens, NN, preferred_element_type=F32
             )
-            sum_ref[...] = part if step == 1 else sum_ref[...] + part
-            leave[step - 1].start()
-    for copy in leave:
-        copy.wait()
+            sum_ref[...] = total if step == 1 else sum_ref[...] + total
+    for copies in leave:
+        for i in range(2):
+            copies(i).wait()
 
 
 def join_kernel(width_ref, valid_ref, head_ref, tail_ref, sum_ref, forward_ref, backward_ref,
@@ -195,7 +206,7 @@
         rows = pl.ds(pl.multiple_of(i * size, size), size)
         return pltpu.make_async_copy(far_ref.at[rows], token_ref.at[rows], sem.at[i])
 
-    begin(fetch, sem.shape[0])
+    begin(sem.shape[0], fetch)
     core = lax.rem(lax.axis_index("region"), 2)
     keep = prior_ref.shape[0]
     share = prior_ref.shape[1] // 256
@@ -224,20 +235,34 @@
         fetch(i).wait()
 
 
-def project_kernel(valid_ref, token_ref, pair_ref, shift_ref, out_ref, value_ref, out_sem, *, tok_rows):
+def project_kernel(valid_ref, early_ref, far_ref, pair_ref, shift_ref, basis_ref,
+                   out_ref, basis_out_ref, late_ref, value_ref, in_sem, out_sem, *, tok_rows):
     keep = shift_ref.shape[0]
     steps = tok_rows // STEP
-    leave = []
+    half = early_ref.shape[0]
+
+    def fetch(i):
+        rows = pl.multiple_of(i * STEP, STEP)
+        return pltpu.make_async_copy(far_ref.at[pl.ds(half + rows, STEP)], late_ref.at[pl.ds(rows, STEP)], in_sem.at[i])
+
+    begin((tok_rows - half) // STEP, fetch)
+    leave = [pltpu.make_async_copy(basis_ref, basis_out_ref, out_sem.at[steps])]
+    leave[0].start()
     for step in range(steps):
-        rows = pl.ds(step * STEP, STEP)
-        wide = lax.dot_general(token_ref[rows, :], pair_ref[...], NN, preferred_element_type=F32).T
+        lanes = pl.ds(step * STEP, STEP)
+        if step * STEP < half:
+            tokens = early_ref[lanes, :]
+        else:
+            fetch(step - half // STEP).wait()
+            tokens = late_ref[pl.ds(step * STEP - half, STEP), :]
+        wide = lax.dot_general(tokens, pair_ref[...], NN, preferred_element_type=F32).T
         place = step * STEP + lax.broadcasted_iota(jnp.int32, (1, STEP), 1)
         value = wide[:keep] + wide[keep:] - shift_ref[:, :1]
-        value_ref[:, rows] = jnp.where(place < valid_ref[0], value, 0.0)
-        leave.append(pltpu.make_async_copy(value_ref.at[:, rows], out_ref.at[:, rows], out_sem.at[step]))
+        value_ref[:, lanes] = jnp.where(place < valid_ref[0], value, 0.0)
+        leave.append(pltpu.make_async_copy(value_ref.at[:, lanes], out_ref.at[:, lanes], out_sem.at[step]))
         if step > 0:
-            leave[step - 1].start()
-    leave[steps - 1].start()
+            leave[step].start()
+    leave[steps].start()
     for copy in leave:
         copy.wait()
 
@@ -356,8 +381,8 @@
         scratch_shapes=[
             pltpu.VMEM((tok_rows, feat_dim), BF16),
             pltpu.VMEM((tok_rows, feat_dim), BF16),
-            pltpu.SemaphoreType.DMA((steps,)),
-            pltpu.SemaphoreType.DMA((steps,)),
+            pltpu.SemaphoreType.DMA((2 * steps,)),
+            pltpu.SemaphoreType.DMA((2 * steps,)),
         ],
         compiler_params=params(32),
         name="bulk",
@@ -383,7 +408,8 @@
         name="join",
     )(band_width, valid_count, head_tokens, tail_tokens, sums, forward, backward, before, after)
     own, other = reduce_all(pieces)
-    basis, pair, shift, head, tail, tokens = pl.pallas_call(
+    tokens = pltpu.with_memory_space_constraint(tokens, pltpu.HBM)
+    basis, pair, shift, head, tail, early = pl.pallas_call(
         basis_kernel,
         in_specs=[near()] * 5 + [far()],
         out_specs=[near()] * 6,
@@ -393,23 +419,28 @@
             jax.ShapeDtypeStruct((keep, 128), F32),
             jax.ShapeDtypeStruct((keep, BAND), F32),
             jax.ShapeDtypeStruct((keep, BAND), F32),
-            jax.ShapeDtypeStruct((tok_rows, feat_dim), BF16),
-        ],
-        scratch_shapes=[pltpu.SemaphoreType.DMA((8,))],
+            jax.ShapeDtypeStruct((tok_rows // 2, feat_dim), BF16),
+        ],
+        scratch_shapes=[pltpu.SemaphoreType.DMA((4,))],
         compiler_params=params(24),
         name="basis",
-    )(own, other, prior, head_tokens, tail_tokens, pltpu.with_memory_space_constraint(tokens, pltpu.HBM))
+    )(own, other, prior, head_tokens, tail_tokens, tokens)
     before = lax.ppermute(tail, "tile", forward_pairs)
     after = lax.ppermute(head, "tile", backward_pairs)
-    raw = pl.pallas_call(
+    raw, basis = pl.pallas_call(
         functools.partial(project_kernel, tok_rows=tok_rows),
-        in_specs=[smem(), near(), near(), near()],
-        out_specs=far(),
-        out_shape=pltpu.HBM((keep, tok_rows), F32),
-        scratch_shapes=[pltpu.VMEM((keep, tok_rows), F32), pltpu.SemaphoreType.DMA((steps,))],
-        compiler_params=params(20),
+        in_specs=[smem(), near(), far(), near(), near(), near()],
+        out_specs=[far(), far()],
+        out_shape=[pltpu.HBM((keep, tok_rows), F32), pltpu.HBM((keep, feat_dim), F32)],
+        scratch_shapes=[
+            pltpu.VMEM((tok_rows // 2, feat_dim), BF16),
+            pltpu.VMEM((keep, tok_rows), F32),
+            pltpu.SemaphoreType.DMA((steps // 2,)),
+            pltpu.SemaphoreType.DMA((steps + 1,)),
+        ],
+        compiler_params=params(24),
         name="project",
-    )(valid_count, tokens, pair, shift)
+    )(valid_count, early, tokens, pair, shift, basis)
     projected = pl.pallas_call(
         functools.partial(blend_kernel, tok_rows=tok_rows, n_tile=n_tile),
         in_specs=[smem(), smem()]

time: 76.5 us -> 75.4 us (0.986)
  waiting for transfers between devices: 22.9 us -> 21 us
  Pallas kernels: 23.4 us -> 24.2 us
    ppermute x1, waiting for transfers between devices: 3.9 us -> 2.05 us  [per_device(): before = lax.ppermute(tail, 'tile', forward_pairs)]
    pallas_call x1, Pallas kernels: 3.32 us -> 5.17 us  [per_device(): pl.pallas_call(functools.partial(project_kernel, tok_rows=tok_rows), in_s...]
  transfers between devices with their start and end apart: 15 -> 15, of which waited for: 11 -> 11; matrix products, arithmetic and copies ran while one was open for 0% -> 0% of each run, Pallas kernels for 19% -> 21%
where the time goes in v6:
time: 75.4 us; the launch traced here: 75.2 us
  starting transfers between devices  28.2 us (37%)
  Pallas kernels  24.2 us (32%)
  waiting for transfers between devices  21 us (28%)
  between operations  1.64 us (2%)
    ppermute x11, waiting for transfers between devices, flip(): return lax.ppermute(value, AXES, pairs)  19 us
    ppermute x11, starting transfers between devices, flip(): return lax.ppermute(value, AXES, pairs)  12.9 us
    pallas_call x1, Pallas kernels, per_device(): bulk(band_width, valid_count, quant_far, block_scales, prior3)  10.7 us
    pallas_call x1, Pallas kernels, per_device(): pl.pallas_call(functools.partial(project_kernel, tok_rows=tok_rows), in_s...  5.17 us
    ppermute x1, starting transfers between devices, per_device(): after = lax.ppermute(backward, 'tile', backward_pairs)  5.02 us
    ppermute x1, starting transfers between devices, per_device(): after = lax.ppermute(head, 'tile', backward_pairs)  4.48 us
    ppermute x1, starting transfers between devices, per_device(): before = lax.ppermute(forward, 'tile', forward_pairs)  3.96 us
    pallas_call x1, Pallas kernels, per_device(): pl.pallas_call(basis_kernel, in_specs=[near()] * 5 + [far()], out_specs=[...  3.62 us
  transfers between devices with their start and end apart: 15, of which 11 were waited for; matrix products, arithmetic and copies ran while one was open for 0% of the time, Pallas kernels for 21%

profile of v6, /device:TPU:2, one launch (start us, length us, event | category | flops | bytes accessed | tf_op | source)
XLA Modules:
  0.0 75.2 jit_solution(7724172545938805309)
XLA Ops:
  1.3 0.0 copy-start
  1.3 0.0 copy-start.2
  1.3 2.4 %band.1 = (f32[72,256]{1,0:T(8,128)S(1)}, f32[64,256]{1,0:T(8,128)S(1)}, bf16[1024,256]{1,0:T(8,128)(2,1)S(1)}, bf16[256,1024]{1,0:T(8,128)(2,1)S(1)}, bf16[256,1024]{1,0:T(8,128)(2,1)S(1)}) custom-call(s32[1]{0:T(128)S(6)} %copy.9.valid_ref, bf16[4096,1024]{1,0:T(8,128)(2,1)} %quant_ref.1, bf16[4096,1024]{1,0:T(8,128)(2,1)} %quant_ref.1, ...), custom_call_target="tpu_custom_call" | custom-call | tf_op jit(solution)/shard_map/band/pallas_call | solution.py:343
  3.7 0.0 copy-start.1
  3.7 4.0 %collective-permute-start = (f32[72,256]{1,0:T(8,128)S(1)}, f32[72,256]{1,0:T(8,128)S(1)}, u32[]{:S(2)}, u32[]{:S(2)}) collective-permute-start(f32[72,256]{1,0:T(8,128)S(1)} %get-tuple-element.21.forward_ref), channel_id=1, source_target_pairs={{0,1},{1,2},{2,3},{3,4},{4,5},{5,6},{6,7},{7,8},{8,9},{9,10},{10,1... | collective-permute-start | bytes 221192 | tf_op jit(solution)/shard_map/ppermute | solution.py:371
  7.6 5.0 %collective-permute-start.1 = (f32[64,256]{1,0:T(8,128)S(1)}, f32[64,256]{1,0:T(8,128)S(1)}, u32[]{:S(2)}, u32[]{:S(2)}) collective-permute-start(f32[64,256]{1,0:T(8,128)S(1)} %get-tuple-element.22.backward_ref), channel_id=1, source_target_pairs={{1,0},{2,1},{3,2},{4,3},{5,4},{6,5},{7,6},{8,7},{9,8},{10,9},{11,1... | collective-permute-start | bytes 196616 | tf_op jit(solution)/shard_map/ppermute | solution.py:372
  12.7 0.0 copy-done
  12.7 0.0 copy-done.2
  12.7 10.7 %bulk.1 = (bf16[4096,1024]{1,0:T(8,128)(2,1)}, f32[144,1024]{1,0:T(8,128)S(1)}) custom-call(s32[128]{0:T(128)S(1)} %copy-done.2, s32[1]{0:T(128)S(6)} %copy.9.valid_ref, bf16[4096,1024]{1,0:T(8,128)(2,1)} %quant_ref.1, f32[8,4096]{1,0:T(8,128)S(1)} %copy-done, bf16[1024,256]{1,0:T(8,128)(2,1)S(1)} %get-tuple-element.19.prior3_ref), custom_call_target="tpu_custom_call" | custom-call | tf_op jit(solution)/shard_map/bulk/pallas_call | solution.py:390
  23.5 0.0 collective-permute-done.1.after_ref
  23.5 0.0 collective-permute-done.before_ref
  23.5 0.9 %join.1 = f32[2,264,128]{2,1,0:T(8,128)S(1)} custom-call(s32[128]{0:T(128)S(1)} %copy-done.2, s32[1]{0:T(128)S(6)} %copy.9.valid_ref, bf16[256,1024]{1,0:T(8,128)(2,1)S(1)} %get-tuple-element.17.head_ref, bf16[256,1024]{1,0:T(8,128)(2,1)S(1)} %get-tuple-element.18.tail_ref, f32[144,1024]{1,0:T(8,128)S(1)} %get-tuple-element.20.sum_ref, ...), custom_call_target="tpu_custom_call" | custom-call | tf_op jit(solution)/shard_map/join/pallas_call | solution.py:391
  24.5 0.1 collective-permute-start.2
  24.6 1.3 %collective-permute-done.2 = f32[264,128]{1,0:T(8,128)S(1)} collective-permute-done((f32[264,128]{1,0:T(8,128)S(1)}, f32[264,128]{1,0:T(8,128)S(1)}, u32[]{:S(2)}, u32[]{:S(2)}) %collective-permute-start.2) | collective-permute-done | bytes 135200 | tf_op jit(solution)/shard_map/ppermute | solution.py:308
  25.9 1.0 %collective-permute-start.5 = (f32[264,128]{1,0:T(8,128)S(1)}, f32[264,128]{1,0:T(8,128)S(1)}, u32[]{:S(2)}, u32[]{:S(2)}) collective-permute-start(f32[264,128]{1,0:T(8,128)S(1)} %bitcast_add_fusion), channel_id=1, source_target_pairs={{0,6},{1,7},{2,4},{3,5},{4,2},{5,3},{6,0},{7,1},{8,14},{9,15},{10,... | collective-permute-start | bytes 405512 | tf_op jit(solution)/shard_map/ppermute | solution.py:308
  26.9 0.6 collective-permute-start.4
  27.5 2.6 %collective-permute-start.3 = (f32[264,128]{1,0:T(8,128)S(1)}, f32[264,128]{1,0:T(8,128)S(1)}, u32[]{:S(2)}, u32[]{:S(2)}) collective-permute-start(f32[264,128]{1,0:T(8,128)S(1)} %bitcast_add_fusion), channel_id=1, source_target_pairs={{0,2},{1,3},{2,0},{3,1},{4,6},{5,7},{6,4},{7,5},{8,10},{9,11},{10,... | collective-permute-start | bytes 405512 | tf_op jit(solution)/shard_map/ppermute | solution.py:308
  30.1 5.6 %collective-permute-done.5 = f32[264,128]{1,0:T(8,128)S(1)} collective-permute-done((f32[264,128]{1,0:T(8,128)S(1)}, f32[264,128]{1,0:T(8,128)S(1)}, u32[]{:S(2)}, u32[]{:S(2)}) %collective-permute-start.5) | collective-permute-done | bytes 135200 | tf_op jit(solution)/shard_map/ppermute | solution.py:308
  35.7 0.0 collective-permute-done.4
  35.7 0.6 collective-permute-done.3
  36.4 1.6 %collective-permute-start.8 = (f32[264,128]{1,0:T(8,128)S(1)}, f32[264,128]{1,0:T(8,128)S(1)}, u32[]{:S(2)}, u32[]{:S(2)}) collective-permute-start(f32[264,128]{1,0:T(8,128)S(1)} %add_add_fusion.2), channel_id=1, source_target_pairs={{0,24},{1,25},{2,26},{3,27},{4,28},{5,29},{6,30},{7,31},{8,16},{9,... | collective-permute-start | bytes 405512 | tf_op jit(solution)/shard_map/ppermute | solution.py:308
  38.0 0.7 collective-permute-start.7
  38.7 1.9 %collective-permute-start.6 = (f32[264,128]{1,0:T(8,128)S(1)}, f32[264,128]{1,0:T(8,128)S(1)}, u32[]{:S(2)}, u32[]{:S(2)}) collective-permute-start(f32[264,128]{1,0:T(8,128)S(1)} %add_add_fusion.2), channel_id=1, source_target_pairs={{0,8},{1,9},{2,10},{3,11},{4,12},{5,13},{6,14},{7,15},{8,0},{9,1},... | collective-permute-start | bytes 405512 | tf_op jit(solution)/shard_map/ppermute | solution.py:308
  40.6 2.4 %collective-permute-done.8 = f32[264,128]{1,0:T(8,128)S(1)} collective-permute-done((f32[264,128]{1,0:T(8,128)S(1)}, f32[264,128]{1,0:T(8,128)S(1)}, u32[]{:S(2)}, u32[]{:S(2)}) %collective-permute-start.8) | collective-permute-done | bytes 135200 | tf_op jit(solution)/shard_map/ppermute | solution.py:308
  42.9 2.3 %collective-permute-done.7 = f32[264,128]{1,0:T(8,128)S(1)} collective-permute-done((f32[264,128]{1,0:T(8,128)S(1)}, f32[264,128]{1,0:T(8,128)S(1)}, u32[]{:S(2)}, u32[]{:S(2)}) %collective-permute-start.7) | collective-permute-done | bytes 135200 | tf_op jit(solution)/shard_map/ppermute | solution.py:308
  45.2 0.5 collective-permute-done.6
  45.7 1.4 %collective-permute-start.11 = (f32[264,128]{1,0:T(8,128)S(1)}, f32[264,128]{1,0:T(8,128)S(1)}, u32[]{:S(2)}, u32[]{:S(2)}) collective-permute-start(f32[264,128]{1,0:T(8,128)S(1)} %add_add_fusion.1), channel_id=1, source_target_pairs={{0,65},{1,64},{2,67},{3,66},{4,69},{5,68},{6,71},{7,70},{8,73},{9,... | collective-permute-start | bytes 405512 | tf_op jit(solution)/shard_map/ppermute | solution.py:308
  47.1 2.7 %collective-permute-start.10 = (f32[264,128]{1,0:T(8,128)S(1)}, f32[264,128]{1,0:T(8,128)S(1)}, u32[]{:S(2)}, u32[]{:S(2)}) collective-permute-start(f32[264,128]{1,0:T(8,128)S(1)} %add_add_fusion.1), channel_id=1, source_target_pairs={{0,64},{1,65},{2,66},{3,67},{4,68},{5,69},{6,70},{7,71},{8,72},{9,... | collective-permute-start | bytes 405512 | tf_op jit(solution)/shard_map/ppermute | solution.py:308
  49.8 0.1 collective-permute-start.9
  49.9 2.1 %collective-permute-done.11 = f32[264,128]{1,0:T(8,128)S(1)} collective-permute-done((f32[264,128]{1,0:T(8,128)S(1)}, f32[264,128]{1,0:T(8,128)S(1)}, u32[]{:S(2)}, u32[]{:S(2)}) %collective-permute-start.11) | collective-permute-done | bytes 135200 | tf_op jit(solution)/shard_map/ppermute | solution.py:308
  52.0 2.6 %collective-permute-done.10 = f32[264,128]{1,0:T(8,128)S(1)} collective-permute-done((f32[264,128]{1,0:T(8,128)S(1)}, f32[264,128]{1,0:T(8,128)S(1)}, u32[]{:S(2)}, u32[]{:S(2)}) %collective-permute-start.10) | collective-permute-done | bytes 135200 | tf_op jit(solution)/shard_map/ppermute | solution.py:308
  54.6 0.2 collective-permute-done.9
  54.8 0.3 collective-permute-start.12
  55.1 1.3 %collective-permute-done.12.other_ref = f32[264,128]{1,0:T(8,128)S(1)} collective-permute-done((f32[264,128]{1,0:T(8,128)S(1)}, f32[264,128]{1,0:T(8,128)S(1)}, u32[]{:S(2)}, u32[]{:S(2)}) %collective-permute-start.12) | collective-permute-done | bytes 135200 | tf_op jit(solution)/shard_map/ppermute | solution.py:308
  56.4 0.0 copy-done.1
  56.4 3.6 %basis.1 = (f32[64,1024]{1,0:T(8,128)S(1)}, bf16[1024,128]{1,0:T(8,128)(2,1)S(1)}, f32[64,128]{1,0:T(8,128)S(1)}, f32[64,256]{1,0:T(8,128)S(1)}, f32[64,256]{1,0:T(8,128)S(1)}, /*index=5*/bf16[2048,1024]{1,0:T(8,128)(2,1)S(1)}) custom-call(f32[264,128]{1,0:T(8,128)S(1)} %add_add_fusion.own_ref, f32[264,128]{1,0:T(8,128)S(1)} %collective-permute-done.12.other_ref, ...), custom_call_target="tpu_custom_call" | custom-call | tf_op jit(solution)/shard_map/basis/pallas_call | solution.py:412
  60.1 4.5 %collective-permute-start.14 = (f32[64,256]{1,0:T(8,128)S(1)}, f32[64,256]{1,0:T(8,128)S(1)}, u32[]{:S(2)}, u32[]{:S(2)}) collective-permute-start(f32[64,256]{1,0:T(8,128)S(1)} %get-tuple-element.24.head_ref), channel_id=1, source_target_pairs={{1,0},{2,1},{3,2},{4,3},{5,4},{6,5},{7,6},{8,7},{9,8},{10,9},{11,1... | collective-permute-start | bytes 196616 | tf_op jit(solution)/shard_map/ppermute | solution.py:429
  64.6 1.9 %collective-permute-start.13 = (f32[64,256]{1,0:T(8,128)S(1)}, f32[64,256]{1,0:T(8,128)S(1)}, u32[]{:S(2)}, u32[]{:S(2)}) collective-permute-start(f32[64,256]{1,0:T(8,128)S(1)} %get-tuple-element.25.tail_ref), channel_id=1, source_target_pairs={{0,1},{1,2},{2,3},{3,4},{4,5},{5,6},{6,7},{7,8},{8,9},{9,10},{10,1... | collective-permute-start | bytes 196616 | tf_op jit(solution)/shard_map/ppermute | solution.py:428
  66.5 5.2 %project.1 = (f32[64,4096]{1,0:T(8,128)}, f32[64,1024]{1,0:T(8,128)}) custom-call(s32[1]{0:T(128)S(6)} %copy.9.valid_ref, bf16[2048,1024]{1,0:T(8,128)(2,1)S(1)} %get-tuple-element.27.early_ref, bf16[4096,1024]{1,0:T(8,128)(2,1)} %get-tuple-element.23.far_ref, bf16[1024,128]{1,0:T(8,128)(2,1)S(1)} %get-tuple-element.28.pair_ref, ...), custom_call_target="tpu_custom_call" | custom-call | tf_op jit(solution)/shard_map/project/pallas_call | solution.py:430
  71.7 0.0 collective-permute-done.14.after_ref
  71.7 2.0 %collective-permute-done.13.before_ref = f32[64,256]{1,0:T(8,128)S(1)} collective-permute-done((f32[64,256]{1,0:T(8,128)S(1)}, f32[64,256]{1,0:T(8,128)S(1)}, u32[]{:S(2)}, u32[]{:S(2)}) %collective-permute-start.13) | collective-permute-done | bytes 65568 | tf_op jit(solution)/shard_map/ppermute | solution.py:428
  73.7 1.3 %blend.1 = f32[64,4096]{1,0:T(8,128)} custom-call(s32[128]{0:T(128)S(1)} %copy-done.2, s32[1]{0:T(128)S(6)} %copy.9.valid_ref, f32[64,256]{1,0:T(8,128)S(1)} %get-tuple-element.24.head_ref, f32[64,256]{1,0:T(8,128)S(1)} %get-tuple-element.25.tail_ref, f32[64,256]{1,0:T(8,128)S(1)} %collective-permute-done.13.before_ref, ...), custom_call_target="tpu_custom_call", output_to_operand_aliasing={{}: (7, {})} | custom-call | tf_op jit(solution)/shard_map/blend/pallas_call | solution.py:444
  (5 shorter events, 0.1 us)
Async XLA Ops:
  1.3 11.4 %copy-start = (f32[8,4096]{1,0:T(8,128)S(1)}, f32[8,4096]{1,0:T(8,128)}, u32[]{:S(2)}) copy-start(f32[8,4096]{1,0:T(8,128)} %scale_ref.1) | copy-start | bytes 393220
  1.3 11.4 %copy-start.2 = (s32[128]{0:T(128)S(1)}, s32[128]{0:T(128)}, u32[]{:S(2)}) copy-start(s32[128]{0:T(128)} %width_ref.5) | copy-start | bytes 1540
  3.7 52.8 %copy-start.1 = (f32[1024,64]{0,1:T(8,128)S(1)}, f32[1024,64]{0,1:T(8,128)}, u32[]{:S(2)}) copy-start(f32[1024,64]{0,1:T(8,128)} %param.9) | copy-start | bytes 786436
  3.7 19.8 %collective-permute-start = (f32[72,256]{1,0:T(8,128)S(1)}, f32[72,256]{1,0:T(8,128)S(1)}, u32[]{:S(2)}, u32[]{:S(2)}) collective-permute-start(f32[72,256]{1,0:T(8,128)S(1)} %get-tuple-element.21.forward_ref), channel_id=1, source_target_pairs={{0,1},{1,2},{2,3},{3,4},{4,5},{5,6},{6,7},{7,8},{8,9},{9,10},{10,1... | collective-permute-start | bytes 221192 | tf_op jit(solution)/shard_map/ppermute | solution.py:371
  7.6 15.8 %collective-permute-start.1 = (f32[64,256]{1,0:T(8,128)S(1)}, f32[64,256]{1,0:T(8,128)S(1)}, u32[]{:S(2)}, u32[]{:S(2)}) collective-permute-start(f32[64,256]{1,0:T(8,128)S(1)} %get-tuple-element.22.backward_ref), channel_id=1, source_target_pairs={{1,0},{2,1},{3,2},{4,3},{5,4},{6,5},{7,6},{8,7},{9,8},{10,9},{11,1... | collective-permute-start | bytes 196616 | tf_op jit(solution)/shard_map/ppermute | solution.py:372
  24.5 1.4 %collective-permute-start.2 = (f32[264,128]{1,0:T(8,128)S(1)}, f32[264,128]{1,0:T(8,128)S(1)}, u32[]{:S(2)}, u32[]{:S(2)}) collective-permute-start(f32[264,128]{1,0:T(8,128)S(1)} %dynamic-slice_bitcast_fusion), channel_id=1, source_target_pairs={{0,32},{1,33},{2,34},{3,35},{4,36},{5,37},{6,38},{7,39},{8,40},{9,... | collective-permute-start | bytes 405512 | tf_op jit(solution)/shard_map/ppermute | solution.py:308
  25.9 9.8 %collective-permute-start.5 = (f32[264,128]{1,0:T(8,128)S(1)}, f32[264,128]{1,0:T(8,128)S(1)}, u32[]{:S(2)}, u32[]{:S(2)}) collective-permute-start(f32[264,128]{1,0:T(8,128)S(1)} %bitcast_add_fusion), channel_id=1, source_target_pairs={{0,6},{1,7},{2,4},{3,5},{4,2},{5,3},{6,0},{7,1},{8,14},{9,15},{10,... | collective-permute-start | bytes 405512 | tf_op jit(solution)/shard_map/ppermute | solution.py:308
  26.9 8.8 %collective-permute-start.4 = (f32[264,128]{1,0:T(8,128)S(1)}, f32[264,128]{1,0:T(8,128)S(1)}, u32[]{:S(2)}, u32[]{:S(2)}) collective-permute-start(f32[264,128]{1,0:T(8,128)S(1)} %bitcast_add_fusion), channel_id=1, source_target_pairs={{0,4},{1,5},{2,6},{3,7},{4,0},{5,1},{6,2},{7,3},{8,12},{9,13},{10,... | collective-permute-start | bytes 405512 | tf_op jit(solution)/shard_map/ppermute | solution.py:308
  27.5 8.8 %collective-permute-start.3 = (f32[264,128]{1,0:T(8,128)S(1)}, f32[264,128]{1,0:T(8,128)S(1)}, u32[]{:S(2)}, u32[]{:S(2)}) collective-permute-start(f32[264,128]{1,0:T(8,128)S(1)} %bitcast_add_fusion), channel_id=1, source_target_pairs={{0,2},{1,3},{2,0},{3,1},{4,6},{5,7},{6,4},{7,5},{8,10},{9,11},{10,... | collective-permute-start | bytes 405512 | tf_op jit(solution)/shard_map/ppermute | solution.py:308
  36.4 6.5 %collective-permute-start.8 = (f32[264,128]{1,0:T(8,128)S(1)}, f32[264,128]{1,0:T(8,128)S(1)}, u32[]{:S(2)}, u32[]{:S(2)}) collective-permute-start(f32[264,128]{1,0:T(8,128)S(1)} %add_add_fusion.2), channel_id=1, source_target_pairs={{0,24},{1,25},{2,26},{3,27},{4,28},{5,29},{6,30},{7,31},{8,16},{9,... | collective-permute-start | bytes 405512 | tf_op jit(solution)/shard_map/ppermute | solution.py:308
  38.0 7.3 %collective-permute-start.7 = (f32[264,128]{1,0:T(8,128)S(1)}, f32[264,128]{1,0:T(8,128)S(1)}, u32[]{:S(2)}, u32[]{:S(2)}) collective-permute-start(f32[264,128]{1,0:T(8,128)S(1)} %add_add_fusion.2), channel_id=1, source_target_pairs={{0,16},{1,17},{2,18},{3,19},{4,20},{5,21},{6,22},{7,23},{8,24},{9,... | collective-permute-start | bytes 405512 | tf_op jit(solution)/shard_map/ppermute | solution.py:308
  38.7 7.0 %collective-permute-start.6 = (f32[264,128]{1,0:T(8,128)S(1)}, f32[264,128]{1,0:T(8,128)S(1)}, u32[]{:S(2)}, u32[]{:S(2)}) collective-permute-start(f32[264,128]{1,0:T(8,128)S(1)} %add_add_fusion.2), channel_id=1, source_target_pairs={{0,8},{1,9},{2,10},{3,11},{4,12},{5,13},{6,14},{7,15},{8,0},{9,1},... | collective-permute-start | bytes 405512 | tf_op jit(solution)/shard_map/ppermute | solution.py:308
  45.7 6.3 %collective-permute-start.11 = (f32[264,128]{1,0:T(8,128)S(1)}, f32[264,128]{1,0:T(8,128)S(1)}, u32[]{:S(2)}, u32[]{:S(2)}) collective-permute-start(f32[264,128]{1,0:T(8,128)S(1)} %add_add_fusion.1), channel_id=1, source_target_pairs={{0,65},{1,64},{2,67},{3,66},{4,69},{5,68},{6,71},{7,70},{8,73},{9,... | collective-permute-start | bytes 405512 | tf_op jit(solution)/shard_map/ppermute | solution.py:308
  47.1 7.5 %collective-permute-start.10 = (f32[264,128]{1,0:T(8,128)S(1)}, f32[264,128]{1,0:T(8,128)S(1)}, u32[]{:S(2)}, u32[]{:S(2)}) collective-permute-start(f32[264,128]{1,0:T(8,128)S(1)} %add_add_fusion.1), channel_id=1, source_target_pairs={{0,64},{1,65},{2,66},{3,67},{4,68},{5,69},{6,70},{7,71},{8,72},{9,... | collective-permute-start | bytes 405512 | tf_op jit(solution)/shard_map/ppermute | solution.py:308
  49.8 5.0 %collective-permute-start.9 = (f32[264,128]{1,0:T(8,128)S(1)}, f32[264,128]{1,0:T(8,128)S(1)}, u32[]{:S(2)}, u32[]{:S(2)}) collective-permute-start(f32[264,128]{1,0:T(8,128)S(1)} %add_add_fusion.1), channel_id=1, source_target_pairs={{0,1},{1,0},{2,3},{3,2},{4,5},{5,4},{6,7},{7,6},{8,9},{9,8},{10,11... | collective-permute-start | bytes 405512 | tf_op jit(solution)/shard_map/ppermute | solution.py:308
  54.8 1.6 %collective-permute-start.12 = (f32[264,128]{1,0:T(8,128)S(1)}, f32[264,128]{1,0:T(8,128)S(1)}, u32[]{:S(2)}, u32[]{:S(2)}) collective-permute-start(f32[264,128]{1,0:T(8,128)S(1)} %add_add_fusion.own_ref), channel_id=1, source_target_pairs={{0,32},{1,33},{2,34},{3,35},{4,36},{5,37},{6,38},{7,39},{8,40},{9,... | collective-permute-start | bytes 405512 | tf_op jit(solution)/shard_map/ppermute | solution.py:308
  60.1 11.6 %collective-permute-start.14 = (f32[64,256]{1,0:T(8,128)S(1)}, f32[64,256]{1,0:T(8,128)S(1)}, u32[]{:S(2)}, u32[]{:S(2)}) collective-permute-start(f32[64,256]{1,0:T(8,128)S(1)} %get-tuple-element.24.head_ref), channel_id=1, source_target_pairs={{1,0},{2,1},{3,2},{4,3},{5,4},{6,5},{7,6},{8,7},{9,8},{10,9},{11,1... | collective-permute-start | bytes 196616 | tf_op jit(solution)/shard_map/ppermute | solution.py:429
  64.6 9.2 %collective-permute-start.13 = (f32[64,256]{1,0:T(8,128)S(1)}, f32[64,256]{1,0:T(8,128)S(1)}, u32[]{:S(2)}, u32[]{:S(2)}) collective-permute-start(f32[64,256]{1,0:T(8,128)S(1)} %get-tuple-element.25.tail_ref), channel_id=1, source_target_pairs={{0,1},{1,2},{2,3},{3,4},{4,5},{5,6},{6,7},{7,8},{8,9},{9,10},{10,1... | collective-permute-start | bytes 196616 | tf_op jit(solution)/shard_map/ppermute | solution.py:428

commit v7 on v6

--- a/solution.py
+++ b/solution.py
@@ -241,11 +241,13 @@
     steps = tok_rows // STEP
     half = early_ref.shape[0]
 
+    size = (tok_rows - half) // 4
+
     def fetch(i):
-        rows = pl.multiple_of(i * STEP, STEP)
-        return pltpu.make_async_copy(far_ref.at[pl.ds(half + rows, STEP)], late_ref.at[pl.ds(rows, STEP)], in_sem.at[i])
-
-    begin((tok_rows - half) // STEP, fetch)
+        rows = pl.multiple_of(i * size, size)
+        return pltpu.make_async_copy(far_ref.at[pl.ds(half + rows, size)], late_ref.at[pl.ds(rows, size)], in_sem.at[i])
+
+    begin(4, fetch)
     leave = [pltpu.make_async_copy(basis_ref, basis_out_ref, out_sem.at[steps])]
     leave[0].start()
     for step in range(steps):
@@ -253,8 +255,9 @@
         if step * STEP < half:
             tokens = early_ref[lanes, :]
         else:
-            fetch(step - half // STEP).wait()
-            tokens = late_ref[pl.ds(step * STEP - half, STEP), :]
+            for i in range(4):
+                fetch(i).wait()
+            tokens = late_ref[...]
         wide = lax.dot_general(tokens, pair_ref[...], NN, preferred_element_type=F32).T
         place = step * STEP + lax.broadcasted_iota(jnp.int32, (1, STEP), 1)
         value = wide[:keep] + wide[keep:] - shift_ref[:, :1]
@@ -303,8 +306,8 @@
     return pltpu.CompilerParams(vmem_limit_bytes=mib << 20)
 
 
-def flip(value, mask):
-    pairs = [(g, g ^ mask) for g in range(128)]
+def flip(value, masks):
+    pairs = [(g, g ^ masks[(g >> 5) & 1]) for g in range(128)]
     return lax.ppermute(value, AXES, pairs)
 
 
@@ -314,11 +317,13 @@
 
 def reduce_all(halves):
     core = lax.axis_index("region") % 2
-    mine = pick(halves, core) + flip(pick(halves, 1 - core), 32)
-    for masks in ((2, 4, 6), (8, 16, 24), (1, 64, 65)):
-        near_one, far_one, across = [flip(mine, mask) for mask in masks]
+    both = (32, 32)
+    mine = pick(halves, core) + flip(pick(halves, 1 - core), both)
+    along_y, along_x, along_z = (2, 4, 6), (8, 16, 24), (1, 64, 65)
+    for stage in ((along_y, along_x), (along_x, along_z), (along_z, along_y)):
+        near_one, far_one, across = [flip(mine, masks) for masks in zip(*stage)]
         mine = (mine + near_one) + (far_one + across)
-    return mine, flip(mine, 32)
+    return mine, flip(mine, both)
 
 
 def per_device(quantized, block_scales, band_width, valid_count, prior_basis):
@@ -419,9 +424,9 @@
             jax.ShapeDtypeStruct((keep, 128), F32),
             jax.ShapeDtypeStruct((keep, BAND), F32),
             jax.ShapeDtypeStruct((keep, BAND), F32),
-            jax.ShapeDtypeStruct((tok_rows // 2, feat_dim), BF16),
-        ],
-        scratch_shapes=[pltpu.SemaphoreType.DMA((4,))],
+            jax.ShapeDtypeStruct((tok_rows - STEP, feat_dim), BF16),
+        ],
+        scratch_shapes=[pltpu.SemaphoreType.DMA((6,))],
         compiler_params=params(24),
         name="basis",
     )(own, other, prior, head_tokens, tail_tokens, tokens)
@@ -433,9 +438,9 @@
         out_specs=[far(), far()],
         out_shape=[pltpu.HBM((keep, tok_rows), F32), pltpu.HBM((keep, feat_dim), F32)],
         scratch_shapes=[
-            pltpu.VMEM((tok_rows // 2, feat_dim), BF16),
+            pltpu.VMEM((STEP, feat_dim), BF16),
             pltpu.VMEM((keep, tok_rows), F32),
-            pltpu.SemaphoreType.DMA((steps // 2,)),
+            pltpu.SemaphoreType.DMA((4,)),
             pltpu.SemaphoreType.DMA((steps + 1,)),
         ],
         compiler_params=params(24),

time: 75.4 us -> 73.2 us (0.971)
  waiting for transfers between devices: 21 us -> 19 us
    ppermute x11, waiting for transfers between devices: 19 us -> 16.4 us  [flip(): return lax.ppermute(value, AXES, pairs)]
where the time goes in v7:
time: 73.2 us; the launch traced here: 73 us
  starting transfers between devices  28.5 us (39%)
  Pallas kernels  23.7 us (32%)
  waiting for transfers between devices  19 us (26%)
  between operations  1.64 us (2%)
    ppermute x11, waiting for transfers between devices, flip(): return lax.ppermute(value, AXES, pairs)  16.4 us
    ppermute x11, starting transfers between devices, flip(): return lax.ppermute(value, AXES, pairs)  12.9 us
    pallas_call x1, Pallas kernels, per_device(): bulk(band_width, valid_count, quant_far, block_scales, prior3)  10.7 us
    ppermute x1, starting transfers between devices, per_device(): after = lax.ppermute(backward, 'tile', backward_pairs)  5.02 us
    ppermute x1, starting transfers between devices, per_device(): after = lax.ppermute(head, 'tile', backward_pairs)  4.75 us
    pallas_call x1, Pallas kernels, per_device(): pl.pallas_call(functools.partial(project_kernel, tok_rows=tok_rows), in_s...  4.65 us
    ppermute x1, starting transfers between devices, per_device(): before = lax.ppermute(forward, 'tile', forward_pairs)  3.96 us
    pallas_call x1, Pallas kernels, per_device(): pl.pallas_call(basis_kernel, in_specs=[near()] * 5 + [far()], out_specs=[...  3.64 us
  transfers between devices with their start and end apart: 15, of which 11 were waited for; matrix products, arithmetic and copies ran while one was open for 0% of the time, Pallas kernels for 21%

profile of v7, /device:TPU:2, one launch (start us, length us, event | category | flops | bytes accessed | tf_op | source)
XLA Modules:
  0.0 73.0 jit_solution(967173201967838059)
XLA Ops:
  1.3 0.0 copy-start
  1.3 0.0 copy-start.2
  1.3 2.4 %band.1 = (f32[72,256]{1,0:T(8,128)S(1)}, f32[64,256]{1,0:T(8,128)S(1)}, bf16[1024,256]{1,0:T(8,128)(2,1)S(1)}, bf16[256,1024]{1,0:T(8,128)(2,1)S(1)}, bf16[256,1024]{1,0:T(8,128)(2,1)S(1)}) custom-call(s32[1]{0:T(128)S(6)} %copy.9.valid_ref, bf16[4096,1024]{1,0:T(8,128)(2,1)} %quant_ref.1, bf16[4096,1024]{1,0:T(8,128)(2,1)} %quant_ref.1, ...), custom_call_target="tpu_custom_call" | custom-call | tf_op jit(solution)/shard_map/band/pallas_call | solution.py:348
  3.7 0.0 copy-start.1
  3.7 4.0 %collective-permute-start = (f32[72,256]{1,0:T(8,128)S(1)}, f32[72,256]{1,0:T(8,128)S(1)}, u32[]{:S(2)}, u32[]{:S(2)}) collective-permute-start(f32[72,256]{1,0:T(8,128)S(1)} %get-tuple-element.21.forward_ref), channel_id=1, source_target_pairs={{0,1},{1,2},{2,3},{3,4},{4,5},{5,6},{6,7},{7,8},{8,9},{9,10},{10,1... | collective-permute-start | bytes 221192 | tf_op jit(solution)/shard_map/ppermute | solution.py:376
  7.6 5.0 %collective-permute-start.1 = (f32[64,256]{1,0:T(8,128)S(1)}, f32[64,256]{1,0:T(8,128)S(1)}, u32[]{:S(2)}, u32[]{:S(2)}) collective-permute-start(f32[64,256]{1,0:T(8,128)S(1)} %get-tuple-element.22.backward_ref), channel_id=1, source_target_pairs={{1,0},{2,1},{3,2},{4,3},{5,4},{6,5},{7,6},{8,7},{9,8},{10,9},{11,1... | collective-permute-start | bytes 196616 | tf_op jit(solution)/shard_map/ppermute | solution.py:377
  12.7 0.0 copy-done
  12.7 0.0 copy-done.2
  12.7 10.7 %bulk.1 = (bf16[4096,1024]{1,0:T(8,128)(2,1)}, f32[144,1024]{1,0:T(8,128)S(1)}) custom-call(s32[128]{0:T(128)S(1)} %copy-done.2, s32[1]{0:T(128)S(6)} %copy.9.valid_ref, bf16[4096,1024]{1,0:T(8,128)(2,1)} %quant_ref.1, f32[8,4096]{1,0:T(8,128)S(1)} %copy-done, bf16[1024,256]{1,0:T(8,128)(2,1)S(1)} %get-tuple-element.19.prior3_ref), custom_call_target="tpu_custom_call" | custom-call | tf_op jit(solution)/shard_map/bulk/pallas_call | solution.py:395
  23.5 0.0 collective-permute-done.1.after_ref
  23.5 0.0 collective-permute-done.before_ref
  23.5 0.9 %join.1 = f32[2,264,128]{2,1,0:T(8,128)S(1)} custom-call(s32[128]{0:T(128)S(1)} %copy-done.2, s32[1]{0:T(128)S(6)} %copy.9.valid_ref, bf16[256,1024]{1,0:T(8,128)(2,1)S(1)} %get-tuple-element.17.head_ref, bf16[256,1024]{1,0:T(8,128)(2,1)S(1)} %get-tuple-element.18.tail_ref, f32[144,1024]{1,0:T(8,128)S(1)} %get-tuple-element.20.sum_ref, ...), custom_call_target="tpu_custom_call" | custom-call | tf_op jit(solution)/shard_map/join/pallas_call | solution.py:396
  24.5 0.1 collective-permute-start.2
  24.6 1.3 %collective-permute-done.2 = f32[264,128]{1,0:T(8,128)S(1)} collective-permute-done((f32[264,128]{1,0:T(8,128)S(1)}, f32[264,128]{1,0:T(8,128)S(1)}, u32[]{:S(2)}, u32[]{:S(2)}) %collective-permute-start.2) | collective-permute-done | bytes 135200 | tf_op jit(solution)/shard_map/ppermute | solution.py:311
  25.9 1.0 %collective-permute-start.5 = (f32[264,128]{1,0:T(8,128)S(1)}, f32[264,128]{1,0:T(8,128)S(1)}, u32[]{:S(2)}, u32[]{:S(2)}) collective-permute-start(f32[264,128]{1,0:T(8,128)S(1)} %bitcast_add_fusion), channel_id=1, source_target_pairs={{0,6},{1,7},{2,4},{3,5},{4,2},{5,3},{6,0},{7,1},{8,14},{9,15},{10,... | collective-permute-start | bytes 405512 | tf_op jit(solution)/shard_map/ppermute | solution.py:311
  26.9 0.6 collective-permute-start.4
  27.5 2.6 %collective-permute-start.3 = (f32[264,128]{1,0:T(8,128)S(1)}, f32[264,128]{1,0:T(8,128)S(1)}, u32[]{:S(2)}, u32[]{:S(2)}) collective-permute-start(f32[264,128]{1,0:T(8,128)S(1)} %bitcast_add_fusion), channel_id=1, source_target_pairs={{0,2},{1,3},{2,0},{3,1},{4,6},{5,7},{6,4},{7,5},{8,10},{9,11},{10,... | collective-permute-start | bytes 405512 | tf_op jit(solution)/shard_map/ppermute | solution.py:311
  30.1 3.6 %collective-permute-done.5 = f32[264,128]{1,0:T(8,128)S(1)} collective-permute-done((f32[264,128]{1,0:T(8,128)S(1)}, f32[264,128]{1,0:T(8,128)S(1)}, u32[]{:S(2)}, u32[]{:S(2)}) %collective-permute-start.5) | collective-permute-done | bytes 135200 | tf_op jit(solution)/shard_map/ppermute | solution.py:311
  33.7 0.0 collective-permute-done.4
  33.7 0.9 %collective-permute-done.3 = f32[264,128]{1,0:T(8,128)S(1)} collective-permute-done((f32[264,128]{1,0:T(8,128)S(1)}, f32[264,128]{1,0:T(8,128)S(1)}, u32[]{:S(2)}, u32[]{:S(2)}) %collective-permute-start.3) | collective-permute-done | bytes 135200 | tf_op jit(solution)/shard_map/ppermute | solution.py:311
  34.6 1.6 %collective-permute-start.8 = (f32[264,128]{1,0:T(8,128)S(1)}, f32[264,128]{1,0:T(8,128)S(1)}, u32[]{:S(2)}, u32[]{:S(2)}) collective-permute-start(f32[264,128]{1,0:T(8,128)S(1)} %add_add_fusion.2), channel_id=1, source_target_pairs={{0,24},{1,25},{2,26},{3,27},{4,28},{5,29},{6,30},{7,31},{8,16},{9,... | collective-permute-start | bytes 405512 | tf_op jit(solution)/shard_map/ppermute | solution.py:311
  36.1 0.7 %collective-permute-start.7 = (f32[264,128]{1,0:T(8,128)S(1)}, f32[264,128]{1,0:T(8,128)S(1)}, u32[]{:S(2)}, u32[]{:S(2)}) collective-permute-start(f32[264,128]{1,0:T(8,128)S(1)} %add_add_fusion.2), channel_id=1, source_target_pairs={{0,16},{1,17},{2,18},{3,19},{4,20},{5,21},{6,22},{7,23},{8,24},{9,... | collective-permute-start | bytes 405512 | tf_op jit(solution)/shard_map/ppermute | solution.py:311
  36.9 1.9 %collective-permute-start.6 = (f32[264,128]{1,0:T(8,128)S(1)}, f32[264,128]{1,0:T(8,128)S(1)}, u32[]{:S(2)}, u32[]{:S(2)}) collective-permute-start(f32[264,128]{1,0:T(8,128)S(1)} %add_add_fusion.2), channel_id=1, source_target_pairs={{0,8},{1,9},{2,10},{3,11},{4,12},{5,13},{6,14},{7,15},{8,0},{9,1},... | collective-permute-start | bytes 405512 | tf_op jit(solution)/shard_map/ppermute | solution.py:311
  38.7 0.9 %collective-permute-done.8 = f32[264,128]{1,0:T(8,128)S(1)} collective-permute-done((f32[264,128]{1,0:T(8,128)S(1)}, f32[264,128]{1,0:T(8,128)S(1)}, u32[]{:S(2)}, u32[]{:S(2)}) %collective-permute-start.8) | collective-permute-done | bytes 135200 | tf_op jit(solution)/shard_map/ppermute | solution.py:311
  39.6 3.0 %collective-permute-done.7 = f32[264,128]{1,0:T(8,128)S(1)} collective-permute-done((f32[264,128]{1,0:T(8,128)S(1)}, f32[264,128]{1,0:T(8,128)S(1)}, u32[]{:S(2)}, u32[]{:S(2)}) %collective-permute-start.7) | collective-permute-done | bytes 135200 | tf_op jit(solution)/shard_map/ppermute | solution.py:311
  42.6 0.5 collective-permute-done.6
  43.2 2.1 %collective-permute-start.11 = (f32[264,128]{1,0:T(8,128)S(1)}, f32[264,128]{1,0:T(8,128)S(1)}, u32[]{:S(2)}, u32[]{:S(2)}) collective-permute-start(f32[264,128]{1,0:T(8,128)S(1)} %add_add_fusion.1), channel_id=1, source_target_pairs={{0,65},{1,64},{2,67},{3,66},{4,69},{5,68},{6,71},{7,70},{8,73},{9,... | collective-permute-start | bytes 405512 | tf_op jit(solution)/shard_map/ppermute | solution.py:311
  45.3 1.9 %collective-permute-start.10 = (f32[264,128]{1,0:T(8,128)S(1)}, f32[264,128]{1,0:T(8,128)S(1)}, u32[]{:S(2)}, u32[]{:S(2)}) collective-permute-start(f32[264,128]{1,0:T(8,128)S(1)} %add_add_fusion.1), channel_id=1, source_target_pairs={{0,64},{1,65},{2,66},{3,67},{4,68},{5,69},{6,70},{7,71},{8,72},{9,... | collective-permute-start | bytes 405512 | tf_op jit(solution)/shard_map/ppermute | solution.py:311
  47.2 0.1 collective-permute-start.9
  47.4 2.1 %collective-permute-done.11 = f32[264,128]{1,0:T(8,128)S(1)} collective-permute-done((f32[264,128]{1,0:T(8,128)S(1)}, f32[264,128]{1,0:T(8,128)S(1)}, u32[]{:S(2)}, u32[]{:S(2)}) %collective-permute-start.11) | collective-permute-done | bytes 135200 | tf_op jit(solution)/shard_map/ppermute | solution.py:311
  49.5 2.3 %collective-permute-done.10 = f32[264,128]{1,0:T(8,128)S(1)} collective-permute-done((f32[264,128]{1,0:T(8,128)S(1)}, f32[264,128]{1,0:T(8,128)S(1)}, u32[]{:S(2)}, u32[]{:S(2)}) %collective-permute-start.10) | collective-permute-done | bytes 135200 | tf_op jit(solution)/shard_map/ppermute | solution.py:311
  51.8 0.4 collective-permute-done.9
  52.3 0.3 collective-permute-start.12
  52.6 1.3 %collective-permute-done.12.other_ref = f32[264,128]{1,0:T(8,128)S(1)} collective-permute-done((f32[264,128]{1,0:T(8,128)S(1)}, f32[264,128]{1,0:T(8,128)S(1)}, u32[]{:S(2)}, u32[]{:S(2)}) %collective-permute-start.12) | collective-permute-done | bytes 135200 | tf_op jit(solution)/shard_map/ppermute | solution.py:311
  53.9 0.0 copy-done.1
  53.9 3.6 %basis.1 = (f32[64,1024]{1,0:T(8,128)S(1)}, bf16[1024,128]{1,0:T(8,128)(2,1)S(1)}, f32[64,128]{1,0:T(8,128)S(1)}, f32[64,256]{1,0:T(8,128)S(1)}, f32[64,256]{1,0:T(8,128)S(1)}, /*index=5*/bf16[3072,1024]{1,0:T(8,128)(2,1)S(1)}) custom-call(f32[264,128]{1,0:T(8,128)S(1)} %add_add_fusion.own_ref, f32[264,128]{1,0:T(8,128)S(1)} %collective-permute-done.12.other_ref, ...), custom_call_target="tpu_custom_call" | custom-call | tf_op jit(solution)/shard_map/basis/pallas_call | solution.py:417
  57.6 4.7 %collective-permute-start.14 = (f32[64,256]{1,0:T(8,128)S(1)}, f32[64,256]{1,0:T(8,128)S(1)}, u32[]{:S(2)}, u32[]{:S(2)}) collective-permute-start(f32[64,256]{1,0:T(8,128)S(1)} %get-tuple-element.24.head_ref), channel_id=1, source_target_pairs={{1,0},{2,1},{3,2},{4,3},{5,4},{6,5},{7,6},{8,7},{9,8},{10,9},{11,1... | collective-permute-start | bytes 196616 | tf_op jit(solution)/shard_map/ppermute | solution.py:434
  62.3 1.9 %collective-permute-start.13 = (f32[64,256]{1,0:T(8,128)S(1)}, f32[64,256]{1,0:T(8,128)S(1)}, u32[]{:S(2)}, u32[]{:S(2)}) collective-permute-start(f32[64,256]{1,0:T(8,128)S(1)} %get-tuple-element.25.tail_ref), channel_id=1, source_target_pairs={{0,1},{1,2},{2,3},{3,4},{4,5},{5,6},{6,7},{7,8},{8,9},{9,10},{10,1... | collective-permute-start | bytes 196616 | tf_op jit(solution)/shard_map/ppermute | solution.py:433
  64.2 4.6 %project.1 = (f32[64,4096]{1,0:T(8,128)}, f32[64,1024]{1,0:T(8,128)}) custom-call(s32[1]{0:T(128)S(6)} %copy.9.valid_ref, bf16[3072,1024]{1,0:T(8,128)(2,1)S(1)} %get-tuple-element.27.early_ref, bf16[4096,1024]{1,0:T(8,128)(2,1)} %get-tuple-element.23.far_ref, bf16[1024,128]{1,0:T(8,128)(2,1)S(1)} %get-tuple-element.28.pair_ref, ...), custom_call_target="tpu_custom_call" | custom-call | tf_op jit(solution)/shard_map/project/pallas_call | solution.py:435
  68.9 0.0 collective-permute-done.14.after_ref
  68.9 2.6 %collective-permute-done.13.before_ref = f32[64,256]{1,0:T(8,128)S(1)} collective-permute-done((f32[64,256]{1,0:T(8,128)S(1)}, f32[64,256]{1,0:T(8,128)S(1)}, u32[]{:S(2)}, u32[]{:S(2)}) %collective-permute-start.13) | collective-permute-done | bytes 65568 | tf_op jit(solution)/shard_map/ppermute | solution.py:433
  71.5 1.3 %blend.1 = f32[64,4096]{1,0:T(8,128)} custom-call(s32[128]{0:T(128)S(1)} %copy-done.2, s32[1]{0:T(128)S(6)} %copy.9.valid_ref, f32[64,256]{1,0:T(8,128)S(1)} %get-tuple-element.24.head_ref, f32[64,256]{1,0:T(8,128)S(1)} %get-tuple-element.25.tail_ref, f32[64,256]{1,0:T(8,128)S(1)} %collective-permute-done.13.before_ref, ...), custom_call_target="tpu_custom_call", output_to_operand_aliasing={{}: (7, {})} | custom-call | tf_op jit(solution)/shard_map/blend/pallas_call | solution.py:449
  (5 shorter events, 0.1 us)
Async XLA Ops:
  1.3 11.4 %copy-start = (f32[8,4096]{1,0:T(8,128)S(1)}, f32[8,4096]{1,0:T(8,128)}, u32[]{:S(2)}) copy-start(f32[8,4096]{1,0:T(8,128)} %scale_ref.1) | copy-start | bytes 393220
  1.3 11.4 %copy-start.2 = (s32[128]{0:T(128)S(1)}, s32[128]{0:T(128)}, u32[]{:S(2)}) copy-start(s32[128]{0:T(128)} %width_ref.5) | copy-start | bytes 1540
  3.7 50.3 %copy-start.1 = (f32[1024,64]{0,1:T(8,128)S(1)}, f32[1024,64]{0,1:T(8,128)}, u32[]{:S(2)}) copy-start(f32[1024,64]{0,1:T(8,128)} %param.9) | copy-start | bytes 786436
  3.7 19.8 %collective-permute-start = (f32[72,256]{1,0:T(8,128)S(1)}, f32[72,256]{1,0:T(8,128)S(1)}, u32[]{:S(2)}, u32[]{:S(2)}) collective-permute-start(f32[72,256]{1,0:T(8,128)S(1)} %get-tuple-element.21.forward_ref), channel_id=1, source_target_pairs={{0,1},{1,2},{2,3},{3,4},{4,5},{5,6},{6,7},{7,8},{8,9},{9,10},{10,1... | collective-permute-start | bytes 221192 | tf_op jit(solution)/shard_map/ppermute | solution.py:376
  7.6 15.8 %collective-permute-start.1 = (f32[64,256]{1,0:T(8,128)S(1)}, f32[64,256]{1,0:T(8,128)S(1)}, u32[]{:S(2)}, u32[]{:S(2)}) collective-permute-start(f32[64,256]{1,0:T(8,128)S(1)} %get-tuple-element.22.backward_ref), channel_id=1, source_target_pairs={{1,0},{2,1},{3,2},{4,3},{5,4},{6,5},{7,6},{8,7},{9,8},{10,9},{11,1... | collective-permute-start | bytes 196616 | tf_op jit(solution)/shard_map/ppermute | solution.py:377
  24.5 1.4 %collective-permute-start.2 = (f32[264,128]{1,0:T(8,128)S(1)}, f32[264,128]{1,0:T(8,128)S(1)}, u32[]{:S(2)}, u32[]{:S(2)}) collective-permute-start(f32[264,128]{1,0:T(8,128)S(1)} %dynamic-slice_bitcast_fusion), channel_id=1, source_target_pairs={{0,32},{1,33},{2,34},{3,35},{4,36},{5,37},{6,38},{7,39},{8,40},{9,... | collective-permute-start | bytes 405512 | tf_op jit(solution)/shard_map/ppermute | solution.py:311
  25.9 7.8 %collective-permute-start.5 = (f32[264,128]{1,0:T(8,128)S(1)}, f32[264,128]{1,0:T(8,128)S(1)}, u32[]{:S(2)}, u32[]{:S(2)}) collective-permute-start(f32[264,128]{1,0:T(8,128)S(1)} %bitcast_add_fusion), channel_id=1, source_target_pairs={{0,6},{1,7},{2,4},{3,5},{4,2},{5,3},{6,0},{7,1},{8,14},{9,15},{10,... | collective-permute-start | bytes 405512 | tf_op jit(solution)/shard_map/ppermute | solution.py:311
  26.9 6.8 %collective-permute-start.4 = (f32[264,128]{1,0:T(8,128)S(1)}, f32[264,128]{1,0:T(8,128)S(1)}, u32[]{:S(2)}, u32[]{:S(2)}) collective-permute-start(f32[264,128]{1,0:T(8,128)S(1)} %bitcast_add_fusion), channel_id=1, source_target_pairs={{0,4},{1,5},{2,6},{3,7},{4,0},{5,1},{6,2},{7,3},{8,12},{9,13},{10,... | collective-permute-start | bytes 405512 | tf_op jit(solution)/shard_map/ppermute | solution.py:311
  27.5 7.0 %collective-permute-start.3 = (f32[264,128]{1,0:T(8,128)S(1)}, f32[264,128]{1,0:T(8,128)S(1)}, u32[]{:S(2)}, u32[]{:S(2)}) collective-permute-start(f32[264,128]{1,0:T(8,128)S(1)} %bitcast_add_fusion), channel_id=1, source_target_pairs={{0,2},{1,3},{2,0},{3,1},{4,6},{5,7},{6,4},{7,5},{8,10},{9,11},{10,... | collective-permute-start | bytes 405512 | tf_op jit(solution)/shard_map/ppermute | solution.py:311
  34.6 5.1 %collective-permute-start.8 = (f32[264,128]{1,0:T(8,128)S(1)}, f32[264,128]{1,0:T(8,128)S(1)}, u32[]{:S(2)}, u32[]{:S(2)}) collective-permute-start(f32[264,128]{1,0:T(8,128)S(1)} %add_add_fusion.2), channel_id=1, source_target_pairs={{0,24},{1,25},{2,26},{3,27},{4,28},{5,29},{6,30},{7,31},{8,16},{9,... | collective-permute-start | bytes 405512 | tf_op jit(solution)/shard_map/ppermute | solution.py:311
  36.1 6.5 %collective-permute-start.7 = (f32[264,128]{1,0:T(8,128)S(1)}, f32[264,128]{1,0:T(8,128)S(1)}, u32[]{:S(2)}, u32[]{:S(2)}) collective-permute-start(f32[264,128]{1,0:T(8,128)S(1)} %add_add_fusion.2), channel_id=1, source_target_pairs={{0,16},{1,17},{2,18},{3,19},{4,20},{5,21},{6,22},{7,23},{8,24},{9,... | collective-permute-start | bytes 405512 | tf_op jit(solution)/shard_map/ppermute | solution.py:311
  36.9 6.3 %collective-permute-start.6 = (f32[264,128]{1,0:T(8,128)S(1)}, f32[264,128]{1,0:T(8,128)S(1)}, u32[]{:S(2)}, u32[]{:S(2)}) collective-permute-start(f32[264,128]{1,0:T(8,128)S(1)} %add_add_fusion.2), channel_id=1, source_target_pairs={{0,8},{1,9},{2,10},{3,11},{4,12},{5,13},{6,14},{7,15},{8,0},{9,1},... | collective-permute-start | bytes 405512 | tf_op jit(solution)/shard_map/ppermute | solution.py:311
  43.2 6.3 %collective-permute-start.11 = (f32[264,128]{1,0:T(8,128)S(1)}, f32[264,128]{1,0:T(8,128)S(1)}, u32[]{:S(2)}, u32[]{:S(2)}) collective-permute-start(f32[264,128]{1,0:T(8,128)S(1)} %add_add_fusion.1), channel_id=1, source_target_pairs={{0,65},{1,64},{2,67},{3,66},{4,69},{5,68},{6,71},{7,70},{8,73},{9,... | collective-permute-start | bytes 405512 | tf_op jit(solution)/shard_map/ppermute | solution.py:311
  45.3 6.5 %collective-permute-start.10 = (f32[264,128]{1,0:T(8,128)S(1)}, f32[264,128]{1,0:T(8,128)S(1)}, u32[]{:S(2)}, u32[]{:S(2)}) collective-permute-start(f32[264,128]{1,0:T(8,128)S(1)} %add_add_fusion.1), channel_id=1, source_target_pairs={{0,64},{1,65},{2,66},{3,67},{4,68},{5,69},{6,70},{7,71},{8,72},{9,... | collective-permute-start | bytes 405512 | tf_op jit(solution)/shard_map/ppermute | solution.py:311
  47.2 5.0 %collective-permute-start.9 = (f32[264,128]{1,0:T(8,128)S(1)}, f32[264,128]{1,0:T(8,128)S(1)}, u32[]{:S(2)}, u32[]{:S(2)}) collective-permute-start(f32[264,128]{1,0:T(8,128)S(1)} %add_add_fusion.1), channel_id=1, source_target_pairs={{0,1},{1,0},{2,3},{3,2},{4,5},{5,4},{6,7},{7,6},{8,9},{9,8},{10,11... | collective-permute-start | bytes 405512 | tf_op jit(solution)/shard_map/ppermute | solution.py:311
  52.3 1.6 %collective-permute-start.12 = (f32[264,128]{1,0:T(8,128)S(1)}, f32[264,128]{1,0:T(8,128)S(1)}, u32[]{:S(2)}, u32[]{:S(2)}) collective-permute-start(f32[264,128]{1,0:T(8,128)S(1)} %add_add_fusion.own_ref), channel_id=1, source_target_pairs={{0,32},{1,33},{2,34},{3,35},{4,36},{5,37},{6,38},{7,39},{8,40},{9,... | collective-permute-start | bytes 405512 | tf_op jit(solution)/shard_map/ppermute | solution.py:311
  57.6 11.3 %collective-permute-start.14 = (f32[64,256]{1,0:T(8,128)S(1)}, f32[64,256]{1,0:T(8,128)S(1)}, u32[]{:S(2)}, u32[]{:S(2)}) collective-permute-start(f32[64,256]{1,0:T(8,128)S(1)} %get-tuple-element.24.head_ref), channel_id=1, source_target_pairs={{1,0},{2,1},{3,2},{4,3},{5,4},{6,5},{7,6},{8,7},{9,8},{10,9},{11,1... | collective-permute-start | bytes 196616 | tf_op jit(solution)/shard_map/ppermute | solution.py:434
  62.3 9.2 %collective-permute-start.13 = (f32[64,256]{1,0:T(8,128)S(1)}, f32[64,256]{1,0:T(8,128)S(1)}, u32[]{:S(2)}, u32[]{:S(2)}) collective-permute-start(f32[64,256]{1,0:T(8,128)S(1)} %get-tuple-element.25.tail_ref), channel_id=1, source_target_pairs={{0,1},{1,2},{2,3},{3,4},{4,5},{5,6},{6,7},{7,8},{8,9},{9,10},{10,1... | collective-permute-start | bytes 196616 | tf_op jit(solution)/shard_map/ppermute | solution.py:433

commit v8 on v7

--- a/solution.py
+++ b/solution.py
@@ -70,7 +70,8 @@
     prior3_ref[...] = prior
     head = jnp.concatenate(dequantize(head_ref[...], head_s_ref[...]), 1)
     head_out_ref[...] = head
-    backward_ref[...] = reduced_rows(prior, head)
+    backward_ref[: high.shape[0], :] = reduced_rows(prior, head)
+    backward_ref[high.shape[0] :, :] = jnp.zeros((ROWS - high.shape[0], BAND), F32)
     tail = jnp.concatenate(dequantize(tail_ref[...], tail_s_ref[...]), 1)
     tail_out_ref[...] = tail
     keep = high.shape[0]
@@ -132,14 +133,14 @@
 def join_kernel(width_ref, valid_ref, head_ref, tail_ref, sum_ref, forward_ref, backward_ref,
                 before_ref, after_ref, out_ref, *, tok_rows, n_tile):
     left, right = widths(width_ref, n_tile)
-    keep = backward_ref.shape[0]
+    keep = sum_ref.shape[0] // 2 - 8
     place = lax.broadcasted_iota(jnp.int32, (1, BAND), 1)
     before = pltpu.roll(before_ref[...], lax.rem(left, BAND), 1)
     after = pltpu.roll(after_ref[...], lax.rem(BAND - right, BAND), 1)
     count = jnp.where(place < left, before[keep : keep + 1], 0.0)
-    head = (backward_ref[...] + before[:keep]) * (count * 0.25)
+    head = (backward_ref[:keep, :] + before[:keep]) * (count * 0.25)
     both = jnp.where(place >= BAND - right, forward_ref[keep : keep + 1, :], 0.0)
-    tail = (forward_ref[:keep, :] + after) * (both * 0.25)
+    tail = (forward_ref[:keep, :] + after[:keep]) * (both * 0.25)
     total = sum_ref[...]
     for reduced, weight, rows in ((head, count, head_ref), (tail, both, tail_ref)):
         reduced = jnp.where(weight > 0.0, reduced, 0.0)
@@ -235,30 +236,15 @@
         fetch(i).wait()
 
 
-def project_kernel(valid_ref, early_ref, far_ref, pair_ref, shift_ref, basis_ref,
-                   out_ref, basis_out_ref, late_ref, value_ref, in_sem, out_sem, *, tok_rows):
+def project_kernel(valid_ref, token_ref, pair_ref, shift_ref, basis_ref,
+                   out_ref, basis_out_ref, value_ref, out_sem, *, tok_rows):
     keep = shift_ref.shape[0]
     steps = tok_rows // STEP
-    half = early_ref.shape[0]
-
-    size = (tok_rows - half) // 4
-
-    def fetch(i):
-        rows = pl.multiple_of(i * size, size)
-        return pltpu.make_async_copy(far_ref.at[pl.ds(half + rows, size)], late_ref.at[pl.ds(rows, size)], in_sem.at[i])
-
-    begin(4, fetch)
     leave = [pltpu.make_async_copy(basis_ref, basis_out_ref, out_sem.at[steps])]
     leave[0].start()
     for step in range(steps):
         lanes = pl.ds(step * STEP, STEP)
-        if step * STEP < half:
-            tokens = early_ref[lanes, :]
-        else:
-            for i in range(4):
-                fetch(i).wait()
-            tokens = late_ref[...]
-        wide = lax.dot_general(tokens, pair_ref[...], NN, preferred_element_type=F32).T
+        wide = lax.dot_general(token_ref[lanes, :], pair_ref[...], NN, preferred_element_type=F32).T
         place = step * STEP + lax.broadcasted_iota(jnp.int32, (1, STEP), 1)
         value = wide[:keep] + wide[keep:] - shift_ref[:, :1]
         value_ref[:, lanes] = jnp.where(place < valid_ref[0], value, 0.0)
@@ -311,6 +297,16 @@
     return lax.ppermute(value, AXES, pairs)
 
 
+def exchange(tail, head):
+    count = lax.axis_size("tile")
+    even = lax.axis_index("tile") % 2 == 0
+    far_pairs = [(i, i + 1) for i in range(1, count - 1, 2)]
+    far_pairs += [(j, i) for i, j in far_pairs]
+    inner = lax.ppermute(jnp.where(even, tail, head), "tile", [(i, i ^ 1) for i in range(count)])
+    outer = lax.ppermute(jnp.where(even, head, tail), "tile", far_pairs)
+    return jnp.where(even, outer, inner), jnp.where(even, inner, outer)
+
+
 def pick(stack, index):
     return lax.dynamic_index_in_dim(stack, index, 0, keepdims=False)
 
@@ -333,8 +329,6 @@
     n_tile = lax.axis_size("tile")
     steps = tok_rows // STEP
     last = tok_rows // BAND - 1
-    forward_pairs = [(i, i + 1) for i in range(n_tile - 1)]
-    backward_pairs = [(i + 1, i) for i in range(n_tile - 1)]
     head_rows = pl.BlockSpec((BAND, feat_dim), lambda i: (0, 0))
     tail_rows = pl.BlockSpec((BAND, feat_dim), lambda i: (last, 0))
 
@@ -358,14 +352,14 @@
         ],
         out_specs=[
             whole(ROWS, BAND),
-            whole(keep, BAND),
+            whole(ROWS, BAND),
             whole(feat_dim, 4 * keep),
             whole(BAND, feat_dim),
             whole(BAND, feat_dim),
         ],
         out_shape=[
             jax.ShapeDtypeStruct((ROWS, BAND), F32),
-            jax.ShapeDtypeStruct((keep, BAND), F32),
+            jax.ShapeDtypeStruct((ROWS, BAND), F32),
             jax.ShapeDtypeStruct((feat_dim, 4 * keep), BF16),
             jax.ShapeDtypeStruct((BAND, feat_dim), BF16),
             jax.ShapeDtypeStruct((BAND, feat_dim), BF16),
@@ -373,8 +367,7 @@
         compiler_params=params(24),
         name="band",
     )(valid_count, quant_far, quant_far, scales_far, scales_far, prior_far)
-    before = lax.ppermute(forward, "tile", forward_pairs)
-    after = lax.ppermute(backward, "tile", backward_pairs)
+    before, after = exchange(forward, backward)
     bulk = pl.pallas_call(
         functools.partial(bulk_kernel, tok_rows=tok_rows, n_tile=n_tile),
         in_specs=[smem(), smem(), far(), near(), near()],
@@ -403,9 +396,9 @@
             whole(BAND, feat_dim),
             whole(2 * keep + 16, feat_dim),
             whole(ROWS, BAND),
-            whole(keep, BAND),
-            whole(ROWS, BAND),
-            whole(keep, BAND),
+            whole(ROWS, BAND),
+            whole(ROWS, BAND),
+            whole(ROWS, BAND),
         ],
         out_specs=whole(2, feat_dim // 256 * keep + 8, 128),
         out_shape=jax.ShapeDtypeStruct((2, feat_dim // 256 * keep + 8, 128), F32),
@@ -424,28 +417,25 @@
             jax.ShapeDtypeStruct((keep, 128), F32),
             jax.ShapeDtypeStruct((keep, BAND), F32),
             jax.ShapeDtypeStruct((keep, BAND), F32),
-            jax.ShapeDtypeStruct((tok_rows - STEP, feat_dim), BF16),
-        ],
-        scratch_shapes=[pltpu.SemaphoreType.DMA((6,))],
+            jax.ShapeDtypeStruct((tok_rows, feat_dim), BF16),
+        ],
+        scratch_shapes=[pltpu.SemaphoreType.DMA((8,))],
         compiler_params=params(24),
         name="basis",
     )(own, other, prior, head_tokens, tail_tokens, tokens)
-    before = lax.ppermute(tail, "tile", forward_pairs)
-    after = lax.ppermute(head, "tile", backward_pairs)
+    before, after = exchange(tail, head)
     raw, basis = pl.pallas_call(
         functools.partial(project_kernel, tok_rows=tok_rows),
-        in_specs=[smem(), near(), far(), near(), near(), near()],
+        in_specs=[smem(), near(), near(), near(), near()],
         out_specs=[far(), far()],
         out_shape=[pltpu.HBM((keep, tok_rows), F32), pltpu.HBM((keep, feat_dim), F32)],
         scratch_shapes=[
-            pltpu.VMEM((STEP, feat_dim), BF16),
             pltpu.VMEM((keep, tok_rows), F32),
-            pltpu.SemaphoreType.DMA((4,)),
             pltpu.SemaphoreType.DMA((steps + 1,)),
         ],
         compiler_params=params(24),
         name="project",
-    )(valid_count, early, tokens, pair, shift, basis)
+    )(valid_count, early, pair, shift, basis)
     projected = pl.pallas_call(
         functools.partial(blend_kernel, tok_rows=tok_rows, n_tile=n_tile),
         in_specs=[smem(), smem()]

time: 73.2 us -> 67.8 us (0.926)
  starting transfers between devices: 28.5 us -> 25 us
  Pallas kernels: 23.7 us -> 22.4 us
  waiting for transfers between devices: 19 us -> 18.1 us
    ppermute x4, starting transfers between devices: 15.6 us -> 12 us  [the longest x2 9.24 us: exchange(): outer = lax.ppermute(jnp.where(even, head, tail), 'tile', far_pairs)]
    ppermute x4, waiting for transfers between devices: 2.58 us -> 1 us  [the longest x2 0.99 us: exchange(): outer = lax.ppermute(jnp.where(even, head, tail), 'tile', far_pairs)]
    pallas_call x1, Pallas kernels: 4.65 us -> 3.32 us  [per_device(): pl.pallas_call(functools.partial(project_kernel, tok_rows=tok_rows), in_s...]
  transfers between devices with their start and end apart: 15 -> 15, of which waited for: 11 -> 10; matrix products, arithmetic and copies ran while one was open for 0% -> 0% of each run, Pallas kernels for 21% -> 21%
where the time goes in v8:
time: 67.8 us; the launch traced here: 67.3 us
  starting transfers between devices  25 us (37%)
  Pallas kernels  22.4 us (33%)
  waiting for transfers between devices  18.1 us (27%)
  between operations  1.66 us (2%)
    ppermute x11, waiting for transfers between devices, flip(): return lax.ppermute(value, AXES, pairs)  17.1 us
    ppermute x11, starting transfers between devices, flip(): return lax.ppermute(value, AXES, pairs)  12.9 us
    pallas_call x1, Pallas kernels, per_device(): bulk(band_width, valid_count, quant_far, block_scales, prior3)  10.8 us
    ppermute x2, starting transfers between devices, exchange(): outer = lax.ppermute(jnp.where(even, head, tail), 'tile', far_pairs)  9.24 us
    pallas_call x1, Pallas kernels, per_device(): pl.pallas_call(basis_kernel, in_specs=[near()] * 5 + [far()], out_specs=[...  3.66 us
    pallas_call x1, Pallas kernels, per_device(): pl.pallas_call(functools.partial(project_kernel, tok_rows=tok_rows), in_s...  3.32 us
    ppermute x2, starting transfers between devices, exchange(): lax.ppermute(jnp.where(even, tail, head), 'tile', [(i, i ^ 1) for i in ra...  2.77 us
    pallas_call x1, Pallas kernels, per_device(): pl.pallas_call(functools.partial(band_kernel, tok_rows=tok_rows), grid=(1...  2.35 us
  transfers between devices with their start and end apart: 15, of which 10 were waited for; matrix products, arithmetic and copies ran while one was open for 0% of the time, Pallas kernels for 21%

profile of v8, /device:TPU:2, one launch (start us, length us, event | category | flops | bytes accessed | tf_op | source)
XLA Modules:
  0.0 67.3 jit_solution(6871958325909236309)
XLA Ops:
  1.3 0.0 copy-start
  1.3 0.0 copy-start.2
  1.3 2.4 %band.1 = (f32[72,256]{1,0:T(8,128)S(1)}, f32[72,256]{1,0:T(8,128)S(1)}, bf16[1024,256]{1,0:T(8,128)(2,1)S(1)}, bf16[256,1024]{1,0:T(8,128)(2,1)S(1)}, bf16[256,1024]{1,0:T(8,128)(2,1)S(1)}) custom-call(s32[1]{0:T(128)S(6)} %copy.9.valid_ref, bf16[4096,1024]{1,0:T(8,128)(2,1)} %quant_ref.1, bf16[4096,1024]{1,0:T(8,128)(2,1)} %quant_ref.1, ...), custom_call_target="tpu_custom_call" | custom-call | tf_op jit(solution)/shard_map/band/pallas_call | solution.py:342
  3.7 0.0 copy-start.1
  3.7 2.0 %collective-permute-start.1 = (f32[72,256]{1,0:T(8,128)S(1)}, f32[72,256]{1,0:T(8,128)S(1)}, u32[]{:S(2)}, u32[]{:S(2)}) collective-permute-start(f32[72,256]{1,0:T(8,128)S(1)} %get-tuple-element.34), channel_id=1, source_target_pairs={{0,1},{1,0},{2,3},{3,2},{4,5},{5,4},{6,7},{7,6},{8,9},{9,8},{10,11... | collective-permute-start | bytes 221192 | tf_op jit(solution)/shard_map/ppermute | solution.py:305
  5.7 4.4 %collective-permute-start = (f32[72,256]{1,0:T(8,128)S(1)}, f32[72,256]{1,0:T(8,128)S(1)}, u32[]{:S(2)}, u32[]{:S(2)}) collective-permute-start(f32[72,256]{1,0:T(8,128)S(1)} %get-tuple-element.35), channel_id=1, source_target_pairs={{1,2},{3,4},{5,6},{7,8},{9,10},{11,12},{13,14},{15,16},{17,18},{19... | collective-permute-start | bytes 221192 | tf_op jit(solution)/shard_map/ppermute | solution.py:306
  10.2 0.0 copy-done
  10.2 0.0 copy-done.2
  10.2 10.8 %bulk.1 = (bf16[4096,1024]{1,0:T(8,128)(2,1)}, f32[144,1024]{1,0:T(8,128)S(1)}) custom-call(s32[128]{0:T(128)S(1)} %copy-done.2, s32[1]{0:T(128)S(6)} %copy.9.valid_ref, bf16[4096,1024]{1,0:T(8,128)(2,1)} %quant_ref.1, f32[8,4096]{1,0:T(8,128)S(1)} %copy-done, bf16[1024,256]{1,0:T(8,128)(2,1)S(1)} %get-tuple-element.19.prior3_ref), custom_call_target="tpu_custom_call" | custom-call | tf_op jit(solution)/shard_map/bulk/pallas_call | solution.py:388
  20.9 0.0 collective-permute-done.1
  20.9 0.0 collective-permute-done
  21.0 0.9 %join.1 = f32[2,264,128]{2,1,0:T(8,128)S(1)} custom-call(s32[128]{0:T(128)S(1)} %copy-done.2, s32[1]{0:T(128)S(6)} %copy.9.valid_ref, bf16[256,1024]{1,0:T(8,128)(2,1)S(1)} %get-tuple-element.17.head_ref, bf16[256,1024]{1,0:T(8,128)(2,1)S(1)} %get-tuple-element.18.tail_ref, f32[144,1024]{1,0:T(8,128)S(1)} %get-tuple-element.20.sum_ref, ...), custom_call_target="tpu_custom_call" | custom-call | tf_op jit(solution)/shard_map/join/pallas_call | solution.py:389
  22.0 0.1 collective-permute-start.2
  22.1 1.3 %collective-permute-done.2 = f32[264,128]{1,0:T(8,128)S(1)} collective-permute-done((f32[264,128]{1,0:T(8,128)S(1)}, f32[264,128]{1,0:T(8,128)S(1)}, u32[]{:S(2)}, u32[]{:S(2)}) %collective-permute-start.2) | collective-permute-done | bytes 135200 | tf_op jit(solution)/shard_map/ppermute | solution.py:297
  23.4 0.8 %collective-permute-start.5 = (f32[264,128]{1,0:T(8,128)S(1)}, f32[264,128]{1,0:T(8,128)S(1)}, u32[]{:S(2)}, u32[]{:S(2)}) collective-permute-start(f32[264,128]{1,0:T(8,128)S(1)} %bitcast_add_fusion), channel_id=1, source_target_pairs={{0,6},{1,7},{2,4},{3,5},{4,2},{5,3},{6,0},{7,1},{8,14},{9,15},{10,... | collective-permute-start | bytes 405512 | tf_op jit(solution)/shard_map/ppermute | solution.py:297
  24.3 0.4 collective-permute-start.4
  24.6 3.0 %collective-permute-start.3 = (f32[264,128]{1,0:T(8,128)S(1)}, f32[264,128]{1,0:T(8,128)S(1)}, u32[]{:S(2)}, u32[]{:S(2)}) collective-permute-start(f32[264,128]{1,0:T(8,128)S(1)} %bitcast_add_fusion), channel_id=1, source_target_pairs={{0,2},{1,3},{2,0},{3,1},{4,6},{5,7},{6,4},{7,5},{8,10},{9,11},{10,... | collective-permute-start | bytes 405512 | tf_op jit(solution)/shard_map/ppermute | solution.py:297
  27.6 3.6 %collective-permute-done.5 = f32[264,128]{1,0:T(8,128)S(1)} collective-permute-done((f32[264,128]{1,0:T(8,128)S(1)}, f32[264,128]{1,0:T(8,128)S(1)}, u32[]{:S(2)}, u32[]{:S(2)}) %collective-permute-start.5) | collective-permute-done | bytes 135200 | tf_op jit(solution)/shard_map/ppermute | solution.py:297
  31.2 0.0 collective-permute-done.4
  31.2 0.9 %collective-permute-done.3 = f32[264,128]{1,0:T(8,128)S(1)} collective-permute-done((f32[264,128]{1,0:T(8,128)S(1)}, f32[264,128]{1,0:T(8,128)S(1)}, u32[]{:S(2)}, u32[]{:S(2)}) %collective-permute-start.3) | collective-permute-done | bytes 135200 | tf_op jit(solution)/shard_map/ppermute | solution.py:297
  32.0 1.6 %collective-permute-start.8 = (f32[264,128]{1,0:T(8,128)S(1)}, f32[264,128]{1,0:T(8,128)S(1)}, u32[]{:S(2)}, u32[]{:S(2)}) collective-permute-start(f32[264,128]{1,0:T(8,128)S(1)} %add_add_fusion.2), channel_id=1, source_target_pairs={{0,24},{1,25},{2,26},{3,27},{4,28},{5,29},{6,30},{7,31},{8,16},{9,... | collective-permute-start | bytes 405512 | tf_op jit(solution)/shard_map/ppermute | solution.py:297
  33.6 1.0 %collective-permute-start.7 = (f32[264,128]{1,0:T(8,128)S(1)}, f32[264,128]{1,0:T(8,128)S(1)}, u32[]{:S(2)}, u32[]{:S(2)}) collective-permute-start(f32[264,128]{1,0:T(8,128)S(1)} %add_add_fusion.2), channel_id=1, source_target_pairs={{0,16},{1,17},{2,18},{3,19},{4,20},{5,21},{6,22},{7,23},{8,24},{9,... | collective-permute-start | bytes 405512 | tf_op jit(solution)/shard_map/ppermute | solution.py:297
  34.6 1.6 %collective-permute-start.6 = (f32[264,128]{1,0:T(8,128)S(1)}, f32[264,128]{1,0:T(8,128)S(1)}, u32[]{:S(2)}, u32[]{:S(2)}) collective-permute-start(f32[264,128]{1,0:T(8,128)S(1)} %add_add_fusion.2), channel_id=1, source_target_pairs={{0,8},{1,9},{2,10},{3,11},{4,12},{5,13},{6,14},{7,15},{8,0},{9,1},... | collective-permute-start | bytes 405512 | tf_op jit(solution)/shard_map/ppermute | solution.py:297
  36.2 0.9 %collective-permute-done.8 = f32[264,128]{1,0:T(8,128)S(1)} collective-permute-done((f32[264,128]{1,0:T(8,128)S(1)}, f32[264,128]{1,0:T(8,128)S(1)}, u32[]{:S(2)}, u32[]{:S(2)}) %collective-permute-start.8) | collective-permute-done | bytes 135200 | tf_op jit(solution)/shard_map/ppermute | solution.py:297
  37.1 3.0 %collective-permute-done.7 = f32[264,128]{1,0:T(8,128)S(1)} collective-permute-done((f32[264,128]{1,0:T(8,128)S(1)}, f32[264,128]{1,0:T(8,128)S(1)}, u32[]{:S(2)}, u32[]{:S(2)}) %collective-permute-start.7) | collective-permute-done | bytes 135200 | tf_op jit(solution)/shard_map/ppermute | solution.py:297
  40.1 0.5 collective-permute-done.6
  40.7 3.3 %collective-permute-start.11 = (f32[264,128]{1,0:T(8,128)S(1)}, f32[264,128]{1,0:T(8,128)S(1)}, u32[]{:S(2)}, u32[]{:S(2)}) collective-permute-start(f32[264,128]{1,0:T(8,128)S(1)} %add_add_fusion.1), channel_id=1, source_target_pairs={{0,65},{1,64},{2,67},{3,66},{4,69},{5,68},{6,71},{7,70},{8,73},{9,... | collective-permute-start | bytes 405512 | tf_op jit(solution)/shard_map/ppermute | solution.py:297
  44.0 0.8 %collective-permute-start.10 = (f32[264,128]{1,0:T(8,128)S(1)}, f32[264,128]{1,0:T(8,128)S(1)}, u32[]{:S(2)}, u32[]{:S(2)}) collective-permute-start(f32[264,128]{1,0:T(8,128)S(1)} %add_add_fusion.1), channel_id=1, source_target_pairs={{0,64},{1,65},{2,66},{3,67},{4,68},{5,69},{6,70},{7,71},{8,72},{9,... | collective-permute-start | bytes 405512 | tf_op jit(solution)/shard_map/ppermute | solution.py:297
  44.7 0.2 collective-permute-start.9
  44.9 3.1 %collective-permute-done.11 = f32[264,128]{1,0:T(8,128)S(1)} collective-permute-done((f32[264,128]{1,0:T(8,128)S(1)}, f32[264,128]{1,0:T(8,128)S(1)}, u32[]{:S(2)}, u32[]{:S(2)}) %collective-permute-start.11) | collective-permute-done | bytes 135200 | tf_op jit(solution)/shard_map/ppermute | solution.py:297
  48.0 2.5 %collective-permute-done.10 = f32[264,128]{1,0:T(8,128)S(1)} collective-permute-done((f32[264,128]{1,0:T(8,128)S(1)}, f32[264,128]{1,0:T(8,128)S(1)}, u32[]{:S(2)}, u32[]{:S(2)}) %collective-permute-start.10) | collective-permute-done | bytes 135200 | tf_op jit(solution)/shard_map/ppermute | solution.py:297
  50.5 0.0 collective-permute-done.9
  50.5 0.3 collective-permute-start.12
  50.8 1.3 %collective-permute-done.12.other_ref = f32[264,128]{1,0:T(8,128)S(1)} collective-permute-done((f32[264,128]{1,0:T(8,128)S(1)}, f32[264,128]{1,0:T(8,128)S(1)}, u32[]{:S(2)}, u32[]{:S(2)}) %collective-permute-start.12) | collective-permute-done | bytes 135200 | tf_op jit(solution)/shard_map/ppermute | solution.py:297
  52.1 0.0 copy-done.1
  52.1 3.7 %basis.1 = (f32[64,1024]{1,0:T(8,128)S(1)}, bf16[1024,128]{1,0:T(8,128)(2,1)S(1)}, f32[64,128]{1,0:T(8,128)S(1)}, f32[64,256]{1,0:T(8,128)S(1)}, f32[64,256]{1,0:T(8,128)S(1)}, /*index=5*/bf16[4096,1024]{1,0:T(8,128)(2,1)S(1)}) custom-call(f32[264,128]{1,0:T(8,128)S(1)} %add_add_fusion.own_ref, f32[264,128]{1,0:T(8,128)S(1)} %collective-permute-done.12.other_ref, ...), custom_call_target="tpu_custom_call" | custom-call | tf_op jit(solution)/shard_map/basis/pallas_call | solution.py:410
  55.8 0.8 %collective-permute-start.14 = (f32[64,256]{1,0:T(8,128)S(1)}, f32[64,256]{1,0:T(8,128)S(1)}, u32[]{:S(2)}, u32[]{:S(2)}) collective-permute-start(f32[64,256]{1,0:T(8,128)S(1)} %get-tuple-element.38), channel_id=1, source_target_pairs={{0,1},{1,0},{2,3},{3,2},{4,5},{5,4},{6,7},{7,6},{8,9},{9,8},{10,11... | collective-permute-start | bytes 196616 | tf_op jit(solution)/shard_map/ppermute | solution.py:305
  56.6 4.8 %collective-permute-start.13 = (f32[64,256]{1,0:T(8,128)S(1)}, f32[64,256]{1,0:T(8,128)S(1)}, u32[]{:S(2)}, u32[]{:S(2)}) collective-permute-start(f32[64,256]{1,0:T(8,128)S(1)} %get-tuple-element.39), channel_id=1, source_target_pairs={{1,2},{3,4},{5,6},{7,8},{9,10},{11,12},{13,14},{15,16},{17,18},{19... | collective-permute-start | bytes 196616 | tf_op jit(solution)/shard_map/ppermute | solution.py:306
  61.4 3.3 %project.1 = (f32[64,4096]{1,0:T(8,128)}, f32[64,1024]{1,0:T(8,128)}) custom-call(s32[1]{0:T(128)S(6)} %copy.9.valid_ref, bf16[4096,1024]{1,0:T(8,128)(2,1)S(1)} %get-tuple-element.27.token_ref, bf16[1024,128]{1,0:T(8,128)(2,1)S(1)} %get-tuple-element.28.pair_ref, f32[64,128]{1,0:T(8,128)S(1)} %get-tuple-element.26.shift_ref, ...), custom_call_target="tpu_custom_call" | custom-call | tf_op jit(solution)/shard_map/project/pallas_call | solution.py:427
  64.8 0.0 collective-permute-done.14
  64.8 1.0 %collective-permute-done.13 = f32[64,256]{1,0:T(8,128)S(1)} collective-permute-done((f32[64,256]{1,0:T(8,128)S(1)}, f32[64,256]{1,0:T(8,128)S(1)}, u32[]{:S(2)}, u32[]{:S(2)}) %collective-permute-start.13) | collective-permute-done | bytes 65568 | tf_op jit(solution)/shard_map/ppermute | solution.py:306
  65.8 1.3 %blend.1 = f32[64,4096]{1,0:T(8,128)} custom-call(s32[128]{0:T(128)S(1)} %copy-done.2, s32[1]{0:T(128)S(6)} %copy.9.valid_ref, f32[64,256]{1,0:T(8,128)S(1)} %get-tuple-element.24.head_ref, f32[64,256]{1,0:T(8,128)S(1)} %get-tuple-element.25.tail_ref, f32[64,256]{1,0:T(8,128)S(1)} %get-tuple-element.37.before_ref, ...), custom_call_target="tpu_custom_call", output_to_operand_aliasing={{}: (7, {})} | custom-call | tf_op jit(solution)/shard_map/blend/pallas_call | solution.py:439
  (9 shorter events, 0.2 us)
Async XLA Ops:
  1.3 8.9 %copy-start = (f32[8,4096]{1,0:T(8,128)S(1)}, f32[8,4096]{1,0:T(8,128)}, u32[]{:S(2)}) copy-start(f32[8,4096]{1,0:T(8,128)} %scale_ref.1) | copy-start | bytes 393220
  1.3 8.9 %copy-start.2 = (s32[128]{0:T(128)S(1)}, s32[128]{0:T(128)}, u32[]{:S(2)}) copy-start(s32[128]{0:T(128)} %width_ref.5) | copy-start | bytes 1540
  3.7 48.5 %copy-start.1 = (f32[1024,64]{0,1:T(8,128)S(1)}, f32[1024,64]{0,1:T(8,128)}, u32[]{:S(2)}) copy-start(f32[1024,64]{0,1:T(8,128)} %param.9) | copy-start | bytes 786436
  3.7 17.2 %collective-permute-start.1 = (f32[72,256]{1,0:T(8,128)S(1)}, f32[72,256]{1,0:T(8,128)S(1)}, u32[]{:S(2)}, u32[]{:S(2)}) collective-permute-start(f32[72,256]{1,0:T(8,128)S(1)} %get-tuple-element.34), channel_id=1, source_target_pairs={{0,1},{1,0},{2,3},{3,2},{4,5},{5,4},{6,7},{7,6},{8,9},{9,8},{10,11... | collective-permute-start | bytes 221192 | tf_op jit(solution)/shard_map/ppermute | solution.py:305
  5.7 15.2 %collective-permute-start = (f32[72,256]{1,0:T(8,128)S(1)}, f32[72,256]{1,0:T(8,128)S(1)}, u32[]{:S(2)}, u32[]{:S(2)}) collective-permute-start(f32[72,256]{1,0:T(8,128)S(1)} %get-tuple-element.35), channel_id=1, source_target_pairs={{1,2},{3,4},{5,6},{7,8},{9,10},{11,12},{13,14},{15,16},{17,18},{19... | collective-permute-start | bytes 221192 | tf_op jit(solution)/shard_map/ppermute | solution.py:306
  22.0 1.4 %collective-permute-start.2 = (f32[264,128]{1,0:T(8,128)S(1)}, f32[264,128]{1,0:T(8,128)S(1)}, u32[]{:S(2)}, u32[]{:S(2)}) collective-permute-start(f32[264,128]{1,0:T(8,128)S(1)} %dynamic-slice_bitcast_fusion), channel_id=1, source_target_pairs={{0,32},{1,33},{2,34},{3,35},{4,36},{5,37},{6,38},{7,39},{8,40},{9,... | collective-permute-start | bytes 405512 | tf_op jit(solution)/shard_map/ppermute | solution.py:297
  23.4 7.8 %collective-permute-start.5 = (f32[264,128]{1,0:T(8,128)S(1)}, f32[264,128]{1,0:T(8,128)S(1)}, u32[]{:S(2)}, u32[]{:S(2)}) collective-permute-start(f32[264,128]{1,0:T(8,128)S(1)} %bitcast_add_fusion), channel_id=1, source_target_pairs={{0,6},{1,7},{2,4},{3,5},{4,2},{5,3},{6,0},{7,1},{8,14},{9,15},{10,... | collective-permute-start | bytes 405512 | tf_op jit(solution)/shard_map/ppermute | solution.py:297
  24.3 6.9 %collective-permute-start.4 = (f32[264,128]{1,0:T(8,128)S(1)}, f32[264,128]{1,0:T(8,128)S(1)}, u32[]{:S(2)}, u32[]{:S(2)}) collective-permute-start(f32[264,128]{1,0:T(8,128)S(1)} %bitcast_add_fusion), channel_id=1, source_target_pairs={{0,4},{1,5},{2,6},{3,7},{4,0},{5,1},{6,2},{7,3},{8,12},{9,13},{10,... | collective-permute-start | bytes 405512 | tf_op jit(solution)/shard_map/ppermute | solution.py:297
  24.6 7.4 %collective-permute-start.3 = (f32[264,128]{1,0:T(8,128)S(1)}, f32[264,128]{1,0:T(8,128)S(1)}, u32[]{:S(2)}, u32[]{:S(2)}) collective-permute-start(f32[264,128]{1,0:T(8,128)S(1)} %bitcast_add_fusion), channel_id=1, source_target_pairs={{0,2},{1,3},{2,0},{3,1},{4,6},{5,7},{6,4},{7,5},{8,10},{9,11},{10,... | collective-permute-start | bytes 405512 | tf_op jit(solution)/shard_map/ppermute | solution.py:297
  32.0 5.1 %collective-permute-start.8 = (f32[264,128]{1,0:T(8,128)S(1)}, f32[264,128]{1,0:T(8,128)S(1)}, u32[]{:S(2)}, u32[]{:S(2)}) collective-permute-start(f32[264,128]{1,0:T(8,128)S(1)} %add_add_fusion.2), channel_id=1, source_target_pairs={{0,24},{1,25},{2,26},{3,27},{4,28},{5,29},{6,30},{7,31},{8,16},{9,... | collective-permute-start | bytes 405512 | tf_op jit(solution)/shard_map/ppermute | solution.py:297
  33.6 6.5 %collective-permute-start.7 = (f32[264,128]{1,0:T(8,128)S(1)}, f32[264,128]{1,0:T(8,128)S(1)}, u32[]{:S(2)}, u32[]{:S(2)}) collective-permute-start(f32[264,128]{1,0:T(8,128)S(1)} %add_add_fusion.2), channel_id=1, source_target_pairs={{0,16},{1,17},{2,18},{3,19},{4,20},{5,21},{6,22},{7,23},{8,24},{9,... | collective-permute-start | bytes 405512 | tf_op jit(solution)/shard_map/ppermute | solution.py:297
  34.6 6.0 %collective-permute-start.6 = (f32[264,128]{1,0:T(8,128)S(1)}, f32[264,128]{1,0:T(8,128)S(1)}, u32[]{:S(2)}, u32[]{:S(2)}) collective-permute-start(f32[264,128]{1,0:T(8,128)S(1)} %add_add_fusion.2), channel_id=1, source_target_pairs={{0,8},{1,9},{2,10},{3,11},{4,12},{5,13},{6,14},{7,15},{8,0},{9,1},... | collective-permute-start | bytes 405512 | tf_op jit(solution)/shard_map/ppermute | solution.py:297
  40.7 7.3 %collective-permute-start.11 = (f32[264,128]{1,0:T(8,128)S(1)}, f32[264,128]{1,0:T(8,128)S(1)}, u32[]{:S(2)}, u32[]{:S(2)}) collective-permute-start(f32[264,128]{1,0:T(8,128)S(1)} %add_add_fusion.1), channel_id=1, source_target_pairs={{0,65},{1,64},{2,67},{3,66},{4,69},{5,68},{6,71},{7,70},{8,73},{9,... | collective-permute-start | bytes 405512 | tf_op jit(solution)/shard_map/ppermute | solution.py:297
  44.0 6.5 %collective-permute-start.10 = (f32[264,128]{1,0:T(8,128)S(1)}, f32[264,128]{1,0:T(8,128)S(1)}, u32[]{:S(2)}, u32[]{:S(2)}) collective-permute-start(f32[264,128]{1,0:T(8,128)S(1)} %add_add_fusion.1), channel_id=1, source_target_pairs={{0,64},{1,65},{2,66},{3,67},{4,68},{5,69},{6,70},{7,71},{8,72},{9,... | collective-permute-start | bytes 405512 | tf_op jit(solution)/shard_map/ppermute | solution.py:297
  44.7 5.8 %collective-permute-start.9 = (f32[264,128]{1,0:T(8,128)S(1)}, f32[264,128]{1,0:T(8,128)S(1)}, u32[]{:S(2)}, u32[]{:S(2)}) collective-permute-start(f32[264,128]{1,0:T(8,128)S(1)} %add_add_fusion.1), channel_id=1, source_target_pairs={{0,1},{1,0},{2,3},{3,2},{4,5},{5,4},{6,7},{7,6},{8,9},{9,8},{10,11... | collective-permute-start | bytes 405512 | tf_op jit(solution)/shard_map/ppermute | solution.py:297
  50.5 1.6 %collective-permute-start.12 = (f32[264,128]{1,0:T(8,128)S(1)}, f32[264,128]{1,0:T(8,128)S(1)}, u32[]{:S(2)}, u32[]{:S(2)}) collective-permute-start(f32[264,128]{1,0:T(8,128)S(1)} %add_add_fusion.own_ref), channel_id=1, source_target_pairs={{0,32},{1,33},{2,34},{3,35},{4,36},{5,37},{6,38},{7,39},{8,40},{9,... | collective-permute-start | bytes 405512 | tf_op jit(solution)/shard_map/ppermute | solution.py:297
  55.8 8.9 %collective-permute-start.14 = (f32[64,256]{1,0:T(8,128)S(1)}, f32[64,256]{1,0:T(8,128)S(1)}, u32[]{:S(2)}, u32[]{:S(2)}) collective-permute-start(f32[64,256]{1,0:T(8,128)S(1)} %get-tuple-element.38), channel_id=1, source_target_pairs={{0,1},{1,0},{2,3},{3,2},{4,5},{5,4},{6,7},{7,6},{8,9},{9,8},{10,11... | collective-permute-start | bytes 196616 | tf_op jit(solution)/shard_map/ppermute | solution.py:305
  56.6 9.2 %collective-permute-start.13 = (f32[64,256]{1,0:T(8,128)S(1)}, f32[64,256]{1,0:T(8,128)S(1)}, u32[]{:S(2)}, u32[]{:S(2)}) collective-permute-start(f32[64,256]{1,0:T(8,128)S(1)} %get-tuple-element.39), channel_id=1, source_target_pairs={{1,2},{3,4},{5,6},{7,8},{9,10},{11,12},{13,14},{15,16},{17,18},{19... | collective-permute-start | bytes 196616 | tf_op jit(solution)/shard_map/ppermute | solution.py:306
